TPU v7x, 512 devices: a 4x2x32 block of a 4x8x32 slice. The times are simulated.
512 devices in a mesh: pat: 2 (over y), slab: 32 (over z), phase: 4 (over x), enc: 2 (over core).
Axes of the slice: x: 4, y: 2, z: 32, core: 2. Of those that a mesh axis runs over, the one named last changes fastest.
The devices are a block of a 4x8x32 slice.
Arguments:
- kspace_data: bfloat16 [4, 4, 4, 96, 64, 192], P('pat', 'phase', 'enc', 'slab'), parts along dimension 0, may hold values from -6 to 6
- coil_maps: bfloat16 [4, 24, 4, 64, 192], P('pat', None, None, 'slab'), parts along dimension 0, may hold values from -1 to 1
- sampling: int32 [4, 4, 128, 192], P('phase', 'enc', 'pat'), parts along dimension 2, may hold values 0 or 1
Outputs:
- image_estimate: float32 [4, 4, 4, 4, 64, 192], P('pat', 'phase', 'enc', None, 'slab'), parts along dimension 0
- residual: float32 [4, 4, 4, 96, 64, 192], P('pat', 'phase', 'enc', 'slab'), parts along dimension 0
There are 2 independent parts, one for each index of `pat`. A program takes and returns all parts, laid end to end along the dimension named above; each array names one. Nothing has to cross between parts.
All inputs are finite; a program needn't handle non-finite values. No bound on the sum of `sampling` on one device may be relied on, other than what follows from the above.
Results may differ from a plain program's by a relative error of at most 0.0046.
Values may be sent and summed in bfloat16 or wider, within the bound.
No kernel may reach another device: no remote copies, remote signals or barrier semaphores. Data moves between devices by JAX's collectives and lax.ppermute only.
A program may use at most 64 MiB of HBM per device.

v0:
```python
import functools
import math

import jax
import jax.numpy as jnp
from jax import lax
from jax.sharding import PartitionSpec as P

ITERS = 2


tv_weight = 0.15
smoothing = 0.6


def with_halo(value, sides, width):
    for axis, dim in sides:
        size, length = (lax.axis_size(axis), value.shape[dim])
        up = [(i, (i + 1) % size) for i in range(size)]
        down = [(j, i) for i, j in up]
        last = lax.slice_in_dim(value, length - width, length, axis=dim)
        first = lax.slice_in_dim(value, 0, width, axis=dim)
        before = lax.ppermute(last, axis, up)
        after = lax.ppermute(first, axis, down)
        value = jnp.concatenate([before, value, after], axis=dim)
    return value


def over_axes(value, axes):
    return functools.reduce(lax.psum, axes, value)


def dft_table(length, direction):
    counter = jnp.arange(length, dtype=jnp.int32)
    product = counter[:, None] * counter[None, :] % length
    angle = product.astype(jnp.float32) * (2.0 * math.pi / length)
    factor = 1.0 / math.sqrt(length)
    return (
        (jnp.cos(angle) * factor).astype(jnp.bfloat16),
        (direction * jnp.sin(angle) * factor).astype(jnp.bfloat16),
    )


def along_rows(real_part, imag_part, table):
    cosine, sine = table
    real_out = jnp.matmul(real_part, cosine, preferred_element_type=jnp.float32) - jnp.matmul(
        imag_part, sine, preferred_element_type=jnp.float32
    )
    imag_out = jnp.matmul(real_part, sine, preferred_element_type=jnp.float32) + jnp.matmul(
        imag_part, cosine, preferred_element_type=jnp.float32
    )
    return (real_out, imag_out)


def along_depth(real_part, imag_part, table):
    cosine, sine = table
    real_out = jnp.einsum(
        "...zy,zw->...wy", real_part, cosine, preferred_element_type=jnp.float32
    ) - jnp.einsum("...zy,zw->...wy", imag_part, sine, preferred_element_type=jnp.float32)
    imag_out = jnp.einsum(
        "...zy,zw->...wy", real_part, sine, preferred_element_type=jnp.float32
    ) + jnp.einsum("...zy,zw->...wy", imag_part, cosine, preferred_element_type=jnp.float32)
    return (real_out, imag_out)


def coil_product(coil_real, coil_imag, real_in, imag_in, column_fwd):
    prod_real = (coil_real * real_in - coil_imag * imag_in).astype(jnp.bfloat16)
    prod_imag = (coil_real * imag_in + coil_imag * real_in).astype(jnp.bfloat16)
    mid_real, mid_imag = along_rows(prod_real, prod_imag, column_fwd)
    return jnp.stack([mid_real, mid_imag]).astype(jnp.bfloat16)


def body(kspace_data, coil_maps, sampling):
    phases = kspace_data.shape[1]
    encodings = kspace_data.shape[2]
    coils = coil_maps.shape[1]
    readout = coil_maps.shape[2]
    zdepth = coil_maps.shape[3]
    lines = coil_maps.shape[4]
    slices = kspace_data.shape[4]
    column_fwd = dft_table(lines, -1.0)
    depth_fwd = dft_table(slices, -1.0)
    column_inv = dft_table(lines, 1.0)
    depth_inv = dft_table(slices, 1.0)
    coil_real = coil_maps[0].astype(jnp.float32)
    coil_imag = coil_maps[1].astype(jnp.float32)
    sampled = sampling.astype(jnp.float32)[None, :, :, None]
    residual = -(kspace_data.astype(jnp.float32) * sampled)
    image_estimate = jnp.zeros((2, phases, encodings, readout, zdepth, lines), jnp.float32)
    for iteration in range(ITERS):
        low = residual.astype(jnp.bfloat16)
        inv_real, inv_imag = along_depth(low[0], low[1], depth_inv)
        partial_rows = jnp.stack([inv_real, inv_imag]).astype(jnp.bfloat16)
        portion = lax.all_to_all(partial_rows, "slab", split_axis=4, concat_axis=3, tiled=True)
        shaped = portion.reshape(
            2,
            portion.shape[1],
            portion.shape[2],
            coils,
            readout,
            portion.shape[4],
            portion.shape[5],
        )
        fine_real, fine_imag = along_rows(shaped[0], shaped[1], column_inv)
        grad_real = jnp.sum(coil_real * fine_real + coil_imag * fine_imag, axis=2)
        grad_imag = jnp.sum(coil_real * fine_imag - coil_imag * fine_real, axis=2)
        adjoint = jnp.stack([grad_real, grad_imag])
        padded = with_halo(image_estimate, (("phase", 1),), 1)
        difference = padded[:, 1:] - padded[:, :-1]
        modulus = difference[0] * difference[0] + difference[1] * difference[1]
        weights = difference / jnp.sqrt(modulus + smoothing * smoothing)[None]
        gradient = adjoint + tv_weight * (weights[:, :-1] - weights[:, 1:])
        grad_local = jnp.sum(gradient * gradient)
        base = lax.optimization_barrier(gradient.astype(jnp.bfloat16)).astype(jnp.float32)
        mid = coil_product(
            coil_real, coil_imag, base[0][:, :, None], base[1][:, :, None], column_fwd
        )
        mid = mid.reshape(2, phases, encodings, coils * readout, zdepth, lines)
        depth_portion = lax.all_to_all(mid, "slab", split_axis=3, concat_axis=4, tiled=True)
        out_real, out_imag = along_depth(depth_portion[0], depth_portion[1], depth_fwd)
        spectrum = jnp.stack([out_real, out_imag])
        spectrum = spectrum * sampled
        spec_local = jnp.sum(spectrum * spectrum)
        grad_sq, spec_sq = (
            over_axes(grad_local, ("slab", "phase", "enc")),
            over_axes(spec_local, ("slab", "phase", "enc")),
        )
        alpha = grad_sq / (spec_sq + 4.0 * tv_weight / smoothing * grad_sq + 1e-06)
        image_estimate = image_estimate - alpha * gradient
        residual = residual - alpha * spectrum
    return (image_estimate, residual)


def solution(mesh):
    in_specs = (
        P("pat", "phase", "enc", "slab", None, None),
        P("pat", None, None, "slab", None),
        P("phase", "enc", "pat", None),
    )
    out_specs = (
        P("pat", "phase", "enc", None, "slab", None),
        P("pat", "phase", "enc", "slab", None, None),
    )
    return jax.shard_map(body, mesh=mesh, in_specs=in_specs, out_specs=out_specs, check_vma=False)
```

profile of v0, /device:TPU:33, one launch (start us, length us, event | category | flops | bytes accessed | tf_op | source)
XLA Modules:
  0.0 447.5 jit_solution(24727096090228562)
XLA Ops:
  1.5 1.1 fusion.16
  4.0 1.2 copy.54
  5.1 46.4 %all-to-all-start = ((bf16[2,1,2,3,64,192]{5,2,3,1,0,4:T(2,128)(2,1)}), bf16[2,1,2,3,64,192]{5,2,3,1,0,4:T(2,128)(2,1)S(1)}, u32[]{:S(2)}, u32[]{:S(2)}) async-start(bf16[2,1,2,3,64,192]{5,2,3,1,0,4:T(2,128)(2,1)} %copy.54), calls=%async_computation | async-start | bytes 786432 | tf_op jit(solution)/shard_map/all_to_all | solution.py:94
  51.6 4.8 %collective-permute-start = (f32[2,1,2,4,2,192]{5,4,3,2,1,0:T(2,128)S(1)}, f32[2,1,2,4,2,192]{5,4,3,2,1,0:T(2,128)S(1)}, u32[]{:S(2)}, u32[]{:S(2)}) collective-permute-start(f32[2,1,2,4,2,192]{5,4,3,2,1,0:T(2,128)S(1)} %broadcast_in_dim.2), channel_id=1, source_target_pairs={{2,0},{4,2},{6,4},{0,6},{3,1},{5,3},{7,5},{1,7},{10,8},{12,10},{14... | collective-permute-start | bytes 73736 | tf_op jit(solution)/shard_map/ppermute | solution.py:24
  56.4 2.1 collective-permute-start.1
  58.9 3.4 collective-permute-done.1
  62.4 40.4 %all-to-all-done = bf16[2,1,2,3,64,192]{5,2,3,1,0,4:T(2,128)(2,1)S(1)} async-done(((bf16[2,1,2,3,64,192]{5,2,3,1,0,4:T(2,128)(2,1)}), bf16[2,1,2,3,64,192]{5,2,3,1,0,4:T(2,128)(2,1)S(1)}, u32[]{:S(2)}, u32[]{:S(2)}) %all-to-all-start) | async-done | bytes 294944 | tf_op jit(solution)/shard_map/all_to_all | solution.py:94
  105.3 1.0 convolution_subtract_fusion.6
  106.3 1.1 add_reduce_fusion.1
  109.4 1.0 fusion.6
  112.3 1.0 copy.63
  113.3 5.3 %all-to-all-start.1 = ((bf16[2,1,2,96,2,192]{5,4,2,1,0,3:T(2,128)(2,1)}), bf16[2,1,2,96,2,192]{5,4,2,1,0,3:T(2,128)(2,1)S(1)}, u32[]{:S(2)}, u32[]{:S(2)}) async-start(bf16[2,1,2,96,2,192]{5,4,2,1,0,3:T(2,128)(2,1)} %copy.63), calls=%async_computation.1 | async-start | bytes 786432 | tf_op jit(solution)/shard_map/all_to_all | solution.py:119
  119.3 47.3 %all-to-all-done.1 = bf16[2,1,2,96,2,192]{5,4,2,1,0,3:T(2,128)(2,1)S(1)} async-done(((bf16[2,1,2,96,2,192]{5,4,2,1,0,3:T(2,128)(2,1)}), bf16[2,1,2,96,2,192]{5,4,2,1,0,3:T(2,128)(2,1)S(1)}, u32[]{:S(2)}, u32[]{:S(2)}) %all-to-all-start.1) | async-done | bytes 294944 | tf_op jit(solution)/shard_map/all_to_all | solution.py:119
  169.9 41.9 %all-reduce.3 = (f32[]{:T(128)}, f32[]{:T(128)}) all-reduce(f32[]{:T(128)} %multiply_reduce_fusion.3, f32[]{:T(128)} %multiply_reduce_fusion.1), channel_id=1, replica_groups=mesh['pat'=2,'slab'=32,'phase'=4,'enc'=2] {'slab'}, use_global_device_ids=true, to_apply=%region_3.4 | all-reduce | flops 2 | bytes 16 | tf_op jit(solution)/shard_map/psum | solution.py:30
  211.8 9.5 %all-reduce.5 = (f32[]{:T(128)}, f32[]{:T(128)}) all-reduce(f32[]{:T(128)} %get-tuple-element.8, f32[]{:T(128)} %get-tuple-element.9), channel_id=1, replica_groups=mesh['pat'=2,'slab'=32,'phase'=4,'enc'=2] {'phase'}, use_global_device_ids=true, to_apply=%region_4.5 | all-reduce | flops 2 | bytes 16 | tf_op jit(solution)/shard_map/psum | solution.py:30
  221.3 22.3 %all-reduce.7 = (f32[]{:T(128)}, f32[]{:T(128)}) all-reduce(f32[]{:T(128)} %get-tuple-element.12, f32[]{:T(128)} %get-tuple-element.13), channel_id=1, replica_groups=mesh['pat'=2,'slab'=32,'phase'=4,'enc'=2] {'enc'}, use_global_device_ids=true, to_apply=%region_5.6 | all-reduce | flops 2 | bytes 16 | tf_op jit(solution)/shard_map/psum | solution.py:30
  247.1 1.2 copy.67
  248.3 6.4 %all-to-all-start.2 = ((bf16[2,1,2,3,64,192]{5,2,3,1,0,4:T(2,128)(2,1)}), bf16[2,1,2,3,64,192]{5,2,3,1,0,4:T(2,128)(2,1)S(1)}, u32[]{:S(2)}, u32[]{:S(2)}) async-start(bf16[2,1,2,3,64,192]{5,2,3,1,0,4:T(2,128)(2,1)} %copy.67), calls=%async_computation.2 | async-start | bytes 786432 | tf_op jit(solution)/shard_map/all_to_all | solution.py:94
  254.7 2.0 collective-permute-start.2
  256.7 3.4 collective-permute-start.3
  260.1 2.5 collective-permute-done.3
  262.7 43.5 %all-to-all-done.2 = bf16[2,1,2,3,64,192]{5,2,3,1,0,4:T(2,128)(2,1)S(1)} async-done(((bf16[2,1,2,3,64,192]{5,2,3,1,0,4:T(2,128)(2,1)}), bf16[2,1,2,3,64,192]{5,2,3,1,0,4:T(2,128)(2,1)S(1)}, u32[]{:S(2)}, u32[]{:S(2)}) %all-to-all-start.2) | async-done | bytes 294944 | tf_op jit(solution)/shard_map/all_to_all | solution.py:94
  308.8 1.0 convolution_subtract_fusion.2
  309.7 1.1 add_reduce_fusion
  312.8 1.0 fusion.10
  315.7 1.0 copy.75
  316.7 5.2 %all-to-all-start.3 = ((bf16[2,1,2,96,2,192]{5,4,2,1,0,3:T(2,128)(2,1)}), bf16[2,1,2,96,2,192]{5,4,2,1,0,3:T(2,128)(2,1)S(1)}, u32[]{:S(2)}, u32[]{:S(2)}) async-start(bf16[2,1,2,96,2,192]{5,4,2,1,0,3:T(2,128)(2,1)} %copy.75), calls=%async_computation.3 | async-start | bytes 786432 | tf_op jit(solution)/shard_map/all_to_all | solution.py:119
  322.5 47.5 %all-to-all-done.3 = bf16[2,1,2,96,2,192]{5,4,2,1,0,3:T(2,128)(2,1)S(1)} async-done(((bf16[2,1,2,96,2,192]{5,4,2,1,0,3:T(2,128)(2,1)}), bf16[2,1,2,96,2,192]{5,4,2,1,0,3:T(2,128)(2,1)S(1)}, u32[]{:S(2)}, u32[]{:S(2)}) %all-to-all-start.3) | async-done | bytes 294944 | tf_op jit(solution)/shard_map/all_to_all | solution.py:119
  373.3 41.7 %all-reduce.2 = (f32[]{:T(128)}, f32[]{:T(128)}) all-reduce(f32[]{:T(128)} %multiply_reduce_fusion.2, f32[]{:T(128)} %multiply_reduce_fusion), channel_id=1, replica_groups=mesh['pat'=2,'slab'=32,'phase'=4,'enc'=2] {'slab'}, use_global_device_ids=true, to_apply=%region_13.14 | all-reduce | flops 2 | bytes 16 | tf_op jit(solution)/shard_map/psum | solution.py:30
  415.0 6.7 %all-reduce.4 = (f32[]{:T(128)}, f32[]{:T(128)}) all-reduce(f32[]{:T(128)} %get-tuple-element.6, f32[]{:T(128)} %get-tuple-element.7), channel_id=1, replica_groups=mesh['pat'=2,'slab'=32,'phase'=4,'enc'=2] {'phase'}, use_global_device_ids=true, to_apply=%region_14.15 | all-reduce | flops 2 | bytes 16 | tf_op jit(solution)/shard_map/psum | solution.py:30
  421.7 22.0 %all-reduce.6 = (f32[]{:T(128)}, f32[]{:T(128)}) all-reduce(f32[]{:T(128)} %get-tuple-element.10, f32[]{:T(128)} %get-tuple-element.11), channel_id=1, replica_groups=mesh['pat'=2,'slab'=32,'phase'=4,'enc'=2] {'enc'}, use_global_device_ids=true, to_apply=%region_15.16 | all-reduce | flops 2 | bytes 16 | tf_op jit(solution)/shard_map/psum | solution.py:30
  445.7 1.1 multiply_subtract_fusion
  (79 shorter events, 25.2 us)
Async XLA Ops:
  5.1 53.4 %copy-start.1 = (bf16[2,24,4,2,192]{4,3,2,1,0:T(2,128)(2,1)S(1)}, bf16[2,24,4,2,192]{4,3,2,1,0:T(2,128)(2,1)}, u32[]{:S(2)}) copy-start(bf16[2,24,4,2,192]{4,3,2,1,0:T(2,128)(2,1)} %param.4) | copy-start | bytes 442372
  5.1 97.7 %all-to-all-start = ((bf16[2,1,2,3,64,192]{5,2,3,1,0,4:T(2,128)(2,1)}), bf16[2,1,2,3,64,192]{5,2,3,1,0,4:T(2,128)(2,1)S(1)}, u32[]{:S(2)}, u32[]{:S(2)}) async-start(bf16[2,1,2,3,64,192]{5,2,3,1,0,4:T(2,128)(2,1)} %copy.54), calls=%async_computation | async-start | bytes 786432 | tf_op jit(solution)/shard_map/all_to_all | solution.py:94
  51.6 7.3 %collective-permute-start = (f32[2,1,2,4,2,192]{5,4,3,2,1,0:T(2,128)S(1)}, f32[2,1,2,4,2,192]{5,4,3,2,1,0:T(2,128)S(1)}, u32[]{:S(2)}, u32[]{:S(2)}) collective-permute-start(f32[2,1,2,4,2,192]{5,4,3,2,1,0:T(2,128)S(1)} %broadcast_in_dim.2), channel_id=1, source_target_pairs={{2,0},{4,2},{6,4},{0,6},{3,1},{5,3},{7,5},{1,7},{10,8},{12,10},{14... | collective-permute-start | bytes 73736 | tf_op jit(solution)/shard_map/ppermute | solution.py:24
  56.4 5.9 %collective-permute-start.1 = (f32[2,1,2,4,2,192]{5,4,3,2,1,0:T(2,128)S(1)}, f32[2,1,2,4,2,192]{5,4,3,2,1,0:T(2,128)S(1)}, u32[]{:S(2)}, u32[]{:S(2)}) collective-permute-start(f32[2,1,2,4,2,192]{5,4,3,2,1,0:T(2,128)S(1)} %broadcast_in_dim.2), channel_id=1, source_target_pairs={{0,2},{2,4},{4,6},{6,0},{1,3},{3,5},{5,7},{7,1},{8,10},{10,12},{12... | collective-permute-start | bytes 73736 | tf_op jit(solution)/shard_map/ppermute | solution.py:23
  113.3 53.3 %all-to-all-start.1 = ((bf16[2,1,2,96,2,192]{5,4,2,1,0,3:T(2,128)(2,1)}), bf16[2,1,2,96,2,192]{5,4,2,1,0,3:T(2,128)(2,1)S(1)}, u32[]{:S(2)}, u32[]{:S(2)}) async-start(bf16[2,1,2,96,2,192]{5,4,2,1,0,3:T(2,128)(2,1)} %copy.63), calls=%async_computation.1 | async-start | bytes 786432 | tf_op jit(solution)/shard_map/all_to_all | solution.py:119
  169.1 76.5 %copy-start = (bf16[2,1,2,3,64,192]{5,4,3,2,1,0:T(8,128)(2,1)S(1)}, bf16[2,1,2,3,64,192]{5,4,3,2,1,0:T(8,128)(2,1)}, u32[]{:S(2)}) copy-start(bf16[2,1,2,3,64,192]{5,4,3,2,1,0:T(8,128)(2,1)} %param.3) | copy-start | bytes 884740
  248.3 58.0 %all-to-all-start.2 = ((bf16[2,1,2,3,64,192]{5,2,3,1,0,4:T(2,128)(2,1)}), bf16[2,1,2,3,64,192]{5,2,3,1,0,4:T(2,128)(2,1)S(1)}, u32[]{:S(2)}, u32[]{:S(2)}) async-start(bf16[2,1,2,3,64,192]{5,2,3,1,0,4:T(2,128)(2,1)} %copy.67), calls=%async_computation.2 | async-start | bytes 786432 | tf_op jit(solution)/shard_map/all_to_all | solution.py:94
  254.7 5.4 %collective-permute-start.2 = (f32[2,1,2,4,2,192]{5,4,3,2,1,0:T(2,128)S(1)}, f32[2,1,2,4,2,192]{5,4,3,2,1,0:T(2,128)S(1)}, u32[]{:S(2)}, u32[]{:S(2)}) collective-permute-start(f32[2,1,2,4,2,192]{5,4,3,2,1,0:T(2,128)S(1)} %multiply_subtract_fusion.3), channel_id=1, source_target_pairs={{2,0},{4,2},{6,4},{0,6},{3,1},{5,3},{7,5},{1,7},{10,8},{12,10},{14... | collective-permute-start | bytes 73736 | tf_op jit(solution)/shard_map/ppermute | solution.py:24
  256.7 5.9 %collective-permute-start.3 = (f32[2,1,2,4,2,192]{5,4,3,2,1,0:T(2,128)S(1)}, f32[2,1,2,4,2,192]{5,4,3,2,1,0:T(2,128)S(1)}, u32[]{:S(2)}, u32[]{:S(2)}) collective-permute-start(f32[2,1,2,4,2,192]{5,4,3,2,1,0:T(2,128)S(1)} %multiply_subtract_fusion.3), channel_id=1, source_target_pairs={{0,2},{2,4},{4,6},{6,0},{1,3},{3,5},{5,7},{7,1},{8,10},{10,12},{12... | collective-permute-start | bytes 73736 | tf_op jit(solution)/shard_map/ppermute | solution.py:23
  316.7 53.3 %all-to-all-start.3 = ((bf16[2,1,2,96,2,192]{5,4,2,1,0,3:T(2,128)(2,1)}), bf16[2,1,2,96,2,192]{5,4,2,1,0,3:T(2,128)(2,1)S(1)}, u32[]{:S(2)}, u32[]{:S(2)}) async-start(bf16[2,1,2,96,2,192]{5,4,2,1,0,3:T(2,128)(2,1)} %copy.75), calls=%async_computation.3 | async-start | bytes 786432 | tf_op jit(solution)/shard_map/all_to_all | solution.py:119
where the time goes:
time: 448 us; the launch traced here: 447 us
  waiting for transfers between devices  185 us (41%)
  blocking collectives  144 us (32%)
  starting transfers between devices  75.6 us (17%)
  matrix products  20.4 us (5%)
  other arithmetic  8.78 us (2%)
  local copies, waits for them, and re-layouts  8.66 us (2%)
  between operations  5.15 us (1%)
    psum x6, blocking collectives, over_axes(): return functools.reduce(lax.psum, axes, value)  144 us
    all_to_all x2, waiting for transfers between devices, body(): lax.all_to_all(mid, 'slab', split_axis=3, concat_axis=4, tiled=True)  94.9 us
    all_to_all x2, waiting for transfers between devices, body(): lax.all_to_all(partial_rows, 'slab', split_axis=4, concat_axis=3, tiled=T...  83.9 us
    all_to_all x2, starting transfers between devices, body(): lax.all_to_all(partial_rows, 'slab', split_axis=4, concat_axis=3, tiled=T...  52.8 us
    all_to_all x2, starting transfers between devices, body(): lax.all_to_all(mid, 'slab', split_axis=3, concat_axis=4, tiled=True)  10.5 us
  transfers between devices with their start and end apart: 8, of which 6 were waited for; matrix products, arithmetic and copies ran while one was open for 0% of the time, Pallas kernels for 0%

commit v1 on v0

v1 whole, which is shorter than its diff:
```python
import functools
import math

import jax
import jax.numpy as jnp
from jax import lax
from jax.experimental import pallas as pl
from jax.experimental.pallas import tpu as pltpu
from jax.sharding import Mesh
from jax.sharding import PartitionSpec as P

tv_weight = 0.15
smoothing = 0.6


def dft_table(length, direction):
    counter = jnp.arange(length, dtype=jnp.int32)
    product = counter[:, None] * counter[None, :] % length
    angle = product.astype(jnp.float32) * (2.0 * math.pi / length)
    factor = 1.0 / math.sqrt(length)
    return (
        (jnp.cos(angle) * factor).astype(jnp.bfloat16),
        (direction * jnp.sin(angle) * factor).astype(jnp.bfloat16),
    )


def depth_block(length, direction):
    cosine, sine = dft_table(length, direction)
    top = jnp.concatenate([cosine, -sine], axis=1)
    bottom = jnp.concatenate([sine, cosine], axis=1)
    return jnp.concatenate([top, bottom], axis=0)


def dot(a, b):
    return jnp.dot(a, b, preferred_element_type=jnp.float32)


def along_rows(real_part, imag_part, table):
    cosine, sine = table
    return (
        dot(real_part, cosine) - dot(imag_part, sine),
        dot(real_part, sine) + dot(imag_part, cosine),
    )


def adjoint_start(kspace_data, sampled, depth_inv):
    encodings, rows, slices, lines = kspace_data.shape[1:]

    def kernel(data, mask, table, out):
        for e in range(encodings):
            weight = -mask[e].astype(jnp.float32)
            for r in range(rows):
                real = (data[0, e, r].astype(jnp.float32) * weight).astype(jnp.bfloat16)
                imag = (data[1, e, r].astype(jnp.float32) * weight).astype(jnp.bfloat16)
                both = dot(table[...], jnp.concatenate([real, imag], axis=0)).astype(jnp.bfloat16)
                out[0, e, r] = both[:slices]
                out[1, e, r] = both[slices:]

    return pl.pallas_call(
        kernel, out_shape=jax.ShapeDtypeStruct(kspace_data.shape, jnp.bfloat16), name="adjoint_start"
    )(kspace_data, sampled, depth_inv)


def normal_step(where, image, extra, sampled, coils_own, coils_other, tables, second):
    column_fwd, column_inv, depth_fwd, depth_inv = tables
    _, encodings, slices, lines = image.shape
    steps, _, group = coils_own.shape[:3]
    nlo = 4
    padded = slices + 16
    f32 = jnp.float32
    bf16 = jnp.bfloat16

    def kernel(*refs):
        refs = list(refs)
        where_ref = refs.pop(0)
        if second:
            alpha_ref = refs.pop(0)
            image_ref, before_ref, after_ref, normal_ref = (refs.pop(0) for _ in range(4))
        else:
            image_ref = refs.pop(0)
        mask_ref, own_ref, other_ref = (refs.pop(0) for _ in range(3))
        fc, fs, ic, isn, zf, zi = (refs.pop(0) for _ in range(6))
        send_ref, norm_ref = refs.pop(0), refs.pop(0)
        if not second:
            out_ref = refs.pop(0)
        value, masked, ee, gg = refs
        step = pl.program_id(0)
        hi, lo, core = where_ref[0], where_ref[1], where_ref[2]

        @pl.when(step == 0)
        def _():
            total = jnp.zeros((slices, lines), f32)
            for e in range(encodings):
                if second:
                    alpha = alpha_ref[0]
                    now = [-alpha * image_ref[c, e].astype(f32) for c in range(2)]
                    back = [-alpha * before_ref[c, e].astype(f32) for c in range(2)]
                    ahead = [-alpha * after_ref[c, e].astype(f32) for c in range(2)]
                    d0 = [now[c] - back[c] for c in range(2)]
                    d1 = [ahead[c] - now[c] for c in range(2)]
                    s0 = jnp.sqrt(d0[0] * d0[0] + d0[1] * d0[1] + smoothing * smoothing)
                    s1 = jnp.sqrt(d1[0] * d1[0] + d1[1] * d1[1] + smoothing * smoothing)
                    new = [
                        image_ref[c, e].astype(f32)
                        - alpha * normal_ref[c, e]
                        + tv_weight * (d0[c] / s0 - d1[c] / s1)
                        for c in range(2)
                    ]
                else:
                    new = [image_ref[c, e].astype(f32) for c in range(2)]
                for c in range(2):
                    value[c, e] = new[c]
                    total = total + new[c] * new[c]
            gg[...] = total
            ee[...] = jnp.zeros((slices, lines), f32)
            if not second:
                out_ref[...] = jnp.zeros(out_ref.shape, f32)

        for half, coil_ref in ((0, own_ref), (1, other_ref)):
            for k in range(group):
                coil_real = coil_ref[0, 0, k].astype(f32)
                coil_imag = coil_ref[0, 1, k].astype(f32)
                for e in range(encodings):
                    real = value[0, e].astype(bf16).astype(f32)
                    imag = value[1, e].astype(bf16).astype(f32)
                    a = (coil_real * real - coil_imag * imag).astype(bf16)
                    b = (coil_real * imag + coil_imag * real).astype(bf16)
                    u_real, u_imag = along_rows(a, b, (fc[...], fs[...]))
                    both = jnp.concatenate([u_real.astype(bf16), u_imag.astype(bf16)], axis=0)
                    spectrum = dot(zf[...], both)
                    weight = mask_ref[e].astype(f32)
                    s_real = spectrum[:slices] * weight
                    s_imag = spectrum[slices:] * weight
                    ee[...] += s_real * s_real + s_imag * s_imag
                    low_real, low_imag = s_real.astype(bf16), s_imag.astype(bf16)
                    masked[half, k, 0, e] = low_real
                    masked[half, k, 1, e] = low_imag
                    if not second:
                        p = dot(zi[...], jnp.concatenate([low_real, low_imag], axis=0)).astype(bf16)
                        q_real, q_imag = along_rows(p[:slices], p[slices:], (ic[...], isn[...]))
                        out_ref[0, e] += coil_real * q_real + coil_imag * q_imag
                        out_ref[1, e] += coil_real * q_imag - coil_imag * q_real
            owner = 2 * step + (core if half == 0 else 1 - core)

            @pl.when(owner == hi)
            def _():
                for dest in range(nlo):
                    i = lax.rem(lo + dest, nlo)
                    coil = jnp.minimum((3 * dest + i) // nlo, group - 1)
                    send_ref[dest, :, :, :slices] = masked[half, coil]

        @pl.when(step == steps - 1)
        def _():
            if second:
                for c in range(2):
                    for e in range(encodings):
                        piece = value[c, e, pl.ds(pl.multiple_of(8 * hi, 8), 8), :]
                        piece = jnp.concatenate([piece, jnp.zeros((8, lines), f32)], axis=0).astype(bf16)
                        for dest in range(nlo):
                            send_ref[dest, c, e, slices : slices + 16] = piece
            norm_ref[0] = jnp.sum(gg[...])
            norm_ref[1] = jnp.sum(ee[...])

    def whole(array):
        return pl.BlockSpec(array.shape, lambda g, _n=array.ndim: (0,) * _n)

    smem = pl.BlockSpec(memory_space=pltpu.SMEM)
    arrays = [image, *extra[1:], sampled]
    consts = [*column_fwd, *column_inv, depth_fwd, depth_inv]
    coil_spec = pl.BlockSpec((1,) + coils_own.shape[1:], lambda g: (g, 0, 0, 0, 0))
    operands = [where] + ([extra[0]] if second else []) + arrays + [coils_own, coils_other] + consts
    in_specs = (
        [smem]
        + ([smem] if second else [])
        + [whole(a) for a in arrays]
        + [coil_spec, coil_spec]
        + [whole(a) for a in consts]
    )
    send = jax.ShapeDtypeStruct((nlo, 2, encodings, padded if second else slices, lines), bf16)
    outs = [send, jax.ShapeDtypeStruct((2,), f32)]
    out_specs = [whole(send), smem]
    if not second:
        outs.append(jax.ShapeDtypeStruct(image.shape, f32))
        out_specs.append(whole(outs[-1]))
    return pl.pallas_call(
        kernel,
        grid=(steps,),
        in_specs=in_specs,
        out_specs=out_specs,
        out_shape=outs,
        scratch_shapes=[
            pltpu.VMEM(image.shape, f32),
            pltpu.VMEM((2, group, 2, encodings, slices, lines), bf16),
            pltpu.VMEM((slices, lines), f32),
            pltpu.VMEM((slices, lines), f32),
        ],
        name="second_step" if second else "first_step",
    )(*operands)


def finish(where, alphas, kspace_data, sampled, rows_one, rows_two):
    encodings, rows, slices, lines = kspace_data.shape[1:]
    nlo = 4

    def kernel(where_ref, alpha, data, mask, one, two, out):
        lo = where_ref[1]
        for r in range(rows):
            source = lax.rem(r - lo + nlo, nlo)
            for e in range(encodings):
                weight = mask[e].astype(jnp.float32)
                for c in range(2):
                    start = -(data[c, e, r].astype(jnp.float32) * weight)
                    first = one[source, c, e].astype(jnp.float32)
                    last = two[source, c, e, :slices].astype(jnp.float32)
                    out[c, e, r] = start - alpha[0] * first - alpha[1] * last

    smem = pl.BlockSpec(memory_space=pltpu.SMEM)
    vmem = pl.BlockSpec(memory_space=pltpu.VMEM)
    return pl.pallas_call(
        kernel,
        in_specs=[smem, smem, vmem, vmem, vmem, vmem],
        out_specs=vmem,
        out_shape=jax.ShapeDtypeStruct(kspace_data.shape, jnp.float32),
        name="finish",
    )(where, alphas, kspace_data, sampled, rows_one, rows_two)


def body(kspace_data, coil_maps, sampling):
    encodings = kspace_data.shape[2]
    rows = kspace_data.shape[3]
    slices = kspace_data.shape[4]
    coils, readout, zdepth, lines = coil_maps.shape[1:]
    nhi, nlo = lax.axis_size("hi"), lax.axis_size("lo")
    nphase, ncore = lax.axis_size("phase"), lax.axis_size("enc")
    slabs = nhi * nlo
    group = coils // (nphase * ncore)
    hi, lo = lax.axis_index("hi"), lax.axis_index("lo")
    phase, core = lax.axis_index("phase"), lax.axis_index("enc")
    where = jnp.stack([hi, lo, core]).astype(jnp.int32)
    column_fwd = dft_table(lines, -1.0)
    column_inv = dft_table(lines, 1.0)
    depth_fwd = depth_block(slices, -1.0)
    depth_inv = depth_block(slices, 1.0)
    tables = (column_fwd, column_inv, depth_fwd, depth_inv)
    sampled = sampling[0].astype(jnp.float32)
    data = kspace_data[:, 0]

    start = adjoint_start(data, sampled, depth_inv)
    start = start.reshape(2, encodings, rows, slabs, zdepth, lines)
    start = start.transpose(3, 0, 1, 2, 4, 5).reshape(slabs, 4 * rows * zdepth, lines)
    share = lax.dynamic_slice_in_dim(coil_maps, (phase * ncore + core) * group, group, axis=1)
    share = share.transpose(2, 0, 1, 3, 4).reshape(1, readout, 2 * group * zdepth, lines)
    share = jnp.broadcast_to(share, (nhi,) + share.shape[1:]).reshape(slabs, -1, lines)
    packed = jnp.concatenate([start, share], axis=1)
    packed = lax.all_to_all(packed, ("hi", "lo"), 0, 0, tiled=True)
    part = packed[:, : start.shape[1]].reshape(slabs, 2, encodings, rows, zdepth, lines)
    part = part.transpose(1, 2, 0, 3, 4, 5).reshape(2, encodings, coils, readout, zdepth, lines)
    share = packed[:, start.shape[1] :].reshape(slabs, 2, group, zdepth, lines)
    share = share.transpose(1, 2, 0, 3, 4).reshape(2, group, slices, lines)

    coil_real = coil_maps[0].astype(jnp.float32)
    coil_imag = coil_maps[1].astype(jnp.float32)
    fine_real = dot(part[0], column_inv[0]) - dot(part[1], column_inv[1])
    fine_imag = dot(part[0], column_inv[1]) + dot(part[1], column_inv[0])
    grad_real = jnp.sum(coil_real * fine_real + coil_imag * fine_imag, axis=1)
    grad_imag = jnp.sum(coil_real * fine_imag - coil_imag * fine_real, axis=1)
    slab_one = jnp.stack([grad_real, grad_imag])

    spread = slab_one.transpose(2, 0, 1, 3, 4)[None].astype(GRAD)
    spread = jnp.broadcast_to(spread, (nhi,) + spread.shape[1:]).reshape(slabs, *spread.shape[2:])
    spread = lax.all_to_all(spread, ("hi", "lo"), 0, 0, tiled=True)
    one = spread.transpose(1, 2, 0, 3, 4).reshape(2, encodings, slices, lines)

    own = lax.all_gather(share, "phase")
    other = lax.ppermute(own, "enc", [(i, (i + 1) % ncore) for i in range(ncore)])

    up = [(i, (i + 1) % nphase) for i in range(nphase)]
    before = lax.ppermute(one, "phase", up)
    after = lax.ppermute(one, "phase", [(j, i) for i, j in up])

    def total(norms):
        norms = functools.reduce(lax.psum, ("lo", "phase", "enc"), norms)
        return norms[0] / (norms[1] + 4.0 * tv_weight / smoothing * norms[0] + 1e-06)

    send_one, norms, normal = normal_step(where, one, (), sampled, own, other, tables, False)
    rows_one = lax.all_to_all(send_one, "lo", 0, 0, tiled=True)
    alpha_one = total(norms)
    extra = (alpha_one.reshape(1), before, after, normal)
    send_two, norms = normal_step(where, one, extra, sampled, own, other, tables, True)
    rows_two = lax.all_to_all(send_two, "lo", 0, 0, tiled=True)
    alpha_two = total(norms)

    slab_two = lax.dynamic_slice_in_dim(rows_two, slices + zdepth * lo, zdepth, axis=3)
    slab_two = slab_two.transpose(1, 2, 0, 3, 4).astype(jnp.float32)
    image = -alpha_one * slab_one - alpha_two * slab_two
    alphas = jnp.stack([alpha_one, alpha_two])
    residual = finish(where, alphas, data, sampled, rows_one, rows_two)
    return (image[:, None], residual[:, None])


GRAD = jnp.bfloat16


def solution(mesh):
    names = dict(mesh.shape)
    nlo = 4
    grid = Mesh(
        mesh.devices.reshape(names["pat"], names["slab"] // nlo, nlo, names["phase"], names["enc"]),
        ("pat", "hi", "lo", "phase", "enc"),
    )
    slab = ("hi", "lo")
    in_specs = (
        P("pat", "phase", "enc", slab, None, None),
        P("pat", None, None, slab, None),
        P("phase", "enc", "pat", None),
    )
    out_specs = (
        P("pat", "phase", "enc", None, slab, None),
        P("pat", "phase", "enc", slab, None, None),
    )
    return jax.shard_map(body, mesh=grid, in_specs=in_specs, out_specs=out_specs, check_vma=False)
```

time: 448 us -> 306 us (0.68)
  waiting for transfers between devices: 185 us -> 81.6 us
  blocking collectives: 144 us -> 84.6 us
  Pallas kernels: 0 us -> 47.3 us
  matrix products: 20.4 us -> 3.95 us
  starting transfers between devices: 75.6 us -> 64.5 us
    all_to_all x4 -> x3, waiting for transfers between devices: 179 us -> 81.6 us  [the longest x1 74.7 us: body(): packed = lax.all_to_all(packed, ('hi', 'lo'), 0, 0, tiled=True)]
    psum x6, blocking collectives: 144 us -> 50.8 us  [total(): norms = functools.reduce(lax.psum, ('lo', 'phase', 'enc'), norms)]
    pallas_call x0 -> x4, Pallas kernels: none -> 47.3 us  [the longest x2 42.7 us: normal_step(): pl.pallas_call(kernel, grid=(steps,), in_specs=in_specs, out_specs=out_sp...]
    all_to_all x0 -> x1, blocking collectives: none -> 20.6 us  [body(): rows_two = lax.all_to_all(send_two, 'lo', 0, 0, tiled=True)]
    dot_general x32 -> x4, matrix products: 20.4 us -> 3.95 us  [dot(): return jnp.dot(a, b, preferred_element_type=jnp.float32)]
    all_gather x0 -> x1, blocking collectives: none -> 13.2 us  [body(): own = lax.all_gather(share, 'phase')]
    all_to_all x4 -> x3, starting transfers between devices: 63.3 us -> 54.7 us  [the longest x1 46.4 us: body(): packed = lax.all_to_all(packed, ('hi', 'lo'), 0, 0, tiled=True)]
    ppermute x4 -> x3, waiting for transfers between devices: 5.94 us -> 0.01 us  [the longest x1 0.01 us: body(): before = lax.ppermute(one, 'phase', up)]
  transfers between devices with their start and end apart: 8 -> 6, of which waited for: 6 -> 2; matrix products, arithmetic and copies ran while one was open for 0% -> 2% of each run, Pallas kernels for 0% -> 0%
where the time goes in v1:
time: 306 us; the launch traced here: 305 us
  blocking collectives  84.6 us (28%)
  waiting for transfers between devices  81.6 us (27%)
  starting transfers between devices  64.5 us (21%)
  Pallas kernels  47.3 us (15%)
  local copies, waits for them, and re-layouts  12.4 us (4%)
  other arithmetic  6.19 us (2%)
  between operations  4.81 us (2%)
  matrix products  3.95 us (1%)
    all_to_all x1, waiting for transfers between devices, body(): packed = lax.all_to_all(packed, ('hi', 'lo'), 0, 0, tiled=True)  74.7 us
    psum x6, blocking collectives, total(): norms = functools.reduce(lax.psum, ('lo', 'phase', 'enc'), norms)  50.8 us
    all_to_all x1, starting transfers between devices, body(): packed = lax.all_to_all(packed, ('hi', 'lo'), 0, 0, tiled=True)  46.4 us
    pallas_call x2, Pallas kernels, normal_step(): pl.pallas_call(kernel, grid=(steps,), in_specs=in_specs, out_specs=out_sp...  42.7 us
    all_to_all x1, blocking collectives, body(): rows_two = lax.all_to_all(send_two, 'lo', 0, 0, tiled=True)  20.6 us
    all_gather x1, blocking collectives, body(): own = lax.all_gather(share, 'phase')  13.2 us
    all_to_all x1, waiting for transfers between devices, body(): spread = lax.all_to_all(spread, ('hi', 'lo'), 0, 0, tiled=True)  6.95 us
  transfers between devices with their start and end apart: 6, of which 2 were waited for; matrix products, arithmetic and copies ran while one was open for 2% of the time, Pallas kernels for 0%

profile of v1, /device:TPU:33, one launch (start us, length us, event | category | flops | bytes accessed | tf_op | source)
XLA Modules:
  0.0 305.3 jit_solution(11309804028365931224)
XLA Ops:
  2.1 0.8 copy-done.8
  4.2 2.1 adjoint_start.1
  6.3 1.2 reshape.38
  7.7 1.2 copy.42
  8.8 46.4 %all-to-all-start = ((bf16[32,36,192]{2,1,0:T(8,128)(2,1)}), bf16[32,36,192]{2,1,0:T(8,128)(2,1)S(1)}, u32[]{:S(2)}, u32[]{:S(2)}) async-start(bf16[32,36,192]{2,1,0:T(8,128)(2,1)} %copy.42), calls=%async_computation | async-start | bytes 1310720 | tf_op jit(solution)/shard_map/all_to_all | solution.py:255
  55.6 74.7 %all-to-all-done = bf16[32,36,192]{2,1,0:T(8,128)(2,1)S(1)} async-done(((bf16[32,36,192]{2,1,0:T(8,128)(2,1)}), bf16[32,36,192]{2,1,0:T(8,128)(2,1)S(1)}, u32[]{:S(2)}, u32[]{:S(2)}) %all-to-all-start) | async-done | bytes 442400 | tf_op jit(solution)/shard_map/all_to_all | solution.py:255
  131.0 0.9 fusion.10
  132.0 0.9 fusion.8
  132.9 1.0 convolution_subtract_fusion
  133.9 1.1 add_reduce_fusion
  135.8 4.8 %all-to-all-start.1 = ((bf16[32,2,2,2,192]{4,3,2,1,0:T(2,128)(2,1)}), bf16[32,2,2,2,192]{4,3,2,1,0:T(2,128)(2,1)S(1)}, u32[]{:S(2)}, u32[]{:S(2)}) async-start(bf16[32,2,2,2,192]{4,3,2,1,0:T(2,128)(2,1)} %bitcast.23), calls=%async_computation.1 | async-start | bytes 262144 | tf_op jit(solution)/shard_map/all_to_all | solution.py:271
  140.9 13.2 %all_gather.3.refs_3_.refs_7_ = bf16[4,2,3,64,192]{4,3,2,1,0:T(8,128)(2,1)S(1)} all-gather(bf16[1,2,3,64,192]{4,3,2,1,0:T(8,128)(2,1)S(1)} %copy.54), channel_id=1, replica_groups=mesh['pat'=2,'hi'=8,'lo'=4,'phase'=4,'enc'=2] {'phase'}, dimensions={0}, use_global_device_ids=true | all-gather | bytes 737280 | tf_op jit(solution)/shard_map/all_gather | solution.py:274
  154.1 4.3 %collective-permute-start = (bf16[4,2,3,64,192]{4,3,2,1,0:T(8,128)(2,1)S(1)}, bf16[4,2,3,64,192]{4,3,2,1,0:T(8,128)(2,1)S(1)}, u32[]{:S(2)}, u32[]{:S(2)}) collective-permute-start(bf16[4,2,3,64,192]{4,3,2,1,0:T(8,128)(2,1)S(1)} %all_gather.3.refs_3_.refs_7_), channel_id=1, source_target_pairs={{0,1},{1,0},{2,3},{3,2},{4,5},{5,4},{6,7},{7,6},{8,9},{9,8},{10,11... | collective-permute-start | bytes 1769480 | tf_op jit(solution)/shard_map/ppermute | solution.py:275
  159.0 1.4 multiply_convert_fusion.2.refs_5_.refs_7_.refs_9_.refs_11_
  160.4 1.5 multiply_convert_fusion
  161.8 6.9 %all-to-all-done.1 = bf16[32,2,2,2,192]{4,3,2,1,0:T(2,128)(2,1)S(1)} async-done(((bf16[32,2,2,2,192]{4,3,2,1,0:T(2,128)(2,1)}), bf16[32,2,2,2,192]{4,3,2,1,0:T(2,128)(2,1)S(1)}, u32[]{:S(2)}, u32[]{:S(2)}) %all-to-all-start.1) | async-done | bytes 98336 | tf_op jit(solution)/shard_map/all_to_all | solution.py:271
  168.9 0.8 reshape.43.refs_1_.refs_2_
  169.7 0.9 copy-done.1
  170.6 28.1 %first_step.1 = (bf16[4,2,2,64,192]{4,3,2,1,0:T(8,128)(2,1)}, f32[2]{0:T(128)}, f32[2,2,64,192]{3,2,1,0:T(8,128)}) custom-call(s32[3]{0:T(128)} %pad_add_fusion.refs_0_.where_ref, bf16[2,2,64,192]{3,2,1,0:T(8,128)(2,1)} %reshape.43.refs_1_.refs_2_, f32[2,64,192]{2,1,0:T(8,128)} %convert_bitcast_fusion.mask.refs_2_.refs_6_, ...), custom_call_target="tpu_custom_call" | custom-call | tf_op jit(solution)/shard_map/first_step/pallas_call | solution.py:185
  199.2 7.0 %psum.42 = f32[2]{0:T(128)S(1)} all-reduce(f32[2]{0:T(128)S(1)} %copy-done.10), channel_id=1, replica_groups=mesh['pat'=2,'hi'=8,'lo'=4,'phase'=4,'enc'=2] {'lo'}, use_global_device_ids=true, to_apply=%region_2.3 | all-reduce | flops 2 | bytes 16 | tf_op jit(solution)/shard_map/psum | solution.py:282
  206.2 3.3 %collective-permute-start.1 = (bf16[2,2,64,192]{3,2,1,0:T(8,128)(2,1)S(1)}, bf16[2,2,64,192]{3,2,1,0:T(8,128)(2,1)S(1)}, u32[]{:S(2)}, u32[]{:S(2)}) collective-permute-start(bf16[2,2,64,192]{3,2,1,0:T(8,128)(2,1)S(1)} %copy-done.4), channel_id=1, source_target_pairs={{0,2},{2,4},{4,6},{6,0},{1,3},{3,5},{5,7},{7,1},{8,10},{10,12},{12... | collective-permute-start | bytes 294920 | tf_op jit(solution)/shard_map/ppermute | solution.py:278
  209.5 7.6 %psum.43 = f32[2]{0:T(128)S(1)} all-reduce(f32[2]{0:T(128)S(1)} %psum.42), channel_id=1, replica_groups=mesh['pat'=2,'hi'=8,'lo'=4,'phase'=4,'enc'=2] {'phase'}, use_global_device_ids=true, to_apply=%region_3.4 | all-reduce | flops 2 | bytes 16 | tf_op jit(solution)/shard_map/psum | solution.py:282
  217.0 2.2 collective-permute-start.2
  219.2 10.0 %psum.44 = f32[2]{0:T(128)S(1)} all-reduce(f32[2]{0:T(128)S(1)} %psum.43), channel_id=1, replica_groups=mesh['pat'=2,'hi'=8,'lo'=4,'phase'=4,'enc'=2] {'enc'}, use_global_device_ids=true, to_apply=%region_4.5 | all-reduce | flops 2 | bytes 16 | tf_op jit(solution)/shard_map/psum | solution.py:282
  232.5 14.7 %second_step.1 = (bf16[4,2,2,80,192]{4,3,2,1,0:T(8,128)(2,1)}, f32[2]{0:T(128)}) custom-call(s32[3]{0:T(128)} %pad_add_fusion.refs_0_.where_ref, f32[1]{0:T(128)} %bitcast.30.refs_1_, bf16[2,2,64,192]{3,2,1,0:T(8,128)(2,1)} %reshape.43.refs_1_.refs_2_, bf16[2,2,64,192]{3,2,1,0:T(8,128)(2,1)} %copy-done.6, bf16[2,2,64,192]{3,2,1,0:T(8,128)(2,1)} %copy-done.7, ...), custom_call_target="tpu_custom_call" | custom-call | tf_op jit(solution)/shard_map/second_step/pallas_call | solution.py:185
  247.1 20.6 %all_to_all.20.two = bf16[4,2,2,80,192]{4,3,2,1,0:T(8,128)(2,1)S(1)} all-to-all(bf16[4,2,2,80,192]{4,3,2,1,0:T(8,128)(2,1)} %get-tuple-element.10), channel_id=1, replica_groups=mesh['pat'=2,'hi'=8,'lo'=4,'phase'=4,'enc'=2] {'lo'}, dimensions={0} | all-to-all | bytes 983040 | tf_op jit(solution)/shard_map/all_to_all | solution.py:290
  267.7 3.6 %all-to-all-start.3 = ((bf16[4,2,2,64,192]{4,3,2,1,0:T(8,128)(2,1)}), bf16[4,2,2,64,192]{4,3,2,1,0:T(8,128)(2,1)S(1)}, u32[]{:S(2)}, u32[]{:S(2)}) async-start(bf16[4,2,2,64,192]{4,3,2,1,0:T(8,128)(2,1)} %get-tuple-element.11), calls=%async_computation.3 | async-start | bytes 1048576 | tf_op jit(solution)/shard_map/all_to_all | solution.py:286
  271.9 12.1 %psum.45 = f32[2]{0:T(128)S(1)} all-reduce(f32[2]{0:T(128)S(1)} %copy-done.9), channel_id=1, replica_groups=mesh['pat'=2,'hi'=8,'lo'=4,'phase'=4,'enc'=2] {'lo'}, use_global_device_ids=true, to_apply=%region_5.6 | all-reduce | flops 2 | bytes 16 | tf_op jit(solution)/shard_map/psum | solution.py:282
  284.0 7.0 %psum.46 = f32[2]{0:T(128)S(1)} all-reduce(f32[2]{0:T(128)S(1)} %psum.45), channel_id=1, replica_groups=mesh['pat'=2,'hi'=8,'lo'=4,'phase'=4,'enc'=2] {'phase'}, use_global_device_ids=true, to_apply=%region_6.7 | all-reduce | flops 2 | bytes 16 | tf_op jit(solution)/shard_map/psum | solution.py:282
  291.1 7.1 %psum.47 = f32[2]{0:T(128)S(1)} all-reduce(f32[2]{0:T(128)S(1)} %psum.46), channel_id=1, replica_groups=mesh['pat'=2,'hi'=8,'lo'=4,'phase'=4,'enc'=2] {'enc'}, use_global_device_ids=true, to_apply=%region_7.8 | all-reduce | flops 2 | bytes 16 | tf_op jit(solution)/shard_map/psum | solution.py:282
  302.0 0.8 copy-done.3
  302.8 2.6 finish.1
  (56 shorter events, 10.1 us)
Async XLA Ops:
  1.9 0.9 copy-start.8
  8.8 46.4 %copy-start.5 = (bf16[2,24,4,2,192]{4,3,2,1,0:T(2,128)(2,1)S(1)}, bf16[2,24,4,2,192]{4,3,2,1,0:T(2,128)(2,1)}, u32[]{:S(2)}) copy-start(bf16[2,24,4,2,192]{4,3,2,1,0:T(2,128)(2,1)} %param.4) | copy-start | bytes 442372
  8.8 121.4 %all-to-all-start = ((bf16[32,36,192]{2,1,0:T(8,128)(2,1)}), bf16[32,36,192]{2,1,0:T(8,128)(2,1)S(1)}, u32[]{:S(2)}, u32[]{:S(2)}) async-start(bf16[32,36,192]{2,1,0:T(8,128)(2,1)} %copy.42), calls=%async_computation | async-start | bytes 1310720 | tf_op jit(solution)/shard_map/all_to_all | solution.py:255
  135.8 33.0 %all-to-all-start.1 = ((bf16[32,2,2,2,192]{4,3,2,1,0:T(2,128)(2,1)}), bf16[32,2,2,2,192]{4,3,2,1,0:T(2,128)(2,1)S(1)}, u32[]{:S(2)}, u32[]{:S(2)}) async-start(bf16[32,2,2,2,192]{4,3,2,1,0:T(2,128)(2,1)} %bitcast.23), calls=%async_computation.1 | async-start | bytes 262144 | tf_op jit(solution)/shard_map/all_to_all | solution.py:271
  154.1 15.6 %copy-start = (bf16[4,2,3,64,192]{4,3,2,1,0:T(8,128)(2,1)}, bf16[4,2,3,64,192]{4,3,2,1,0:T(8,128)(2,1)S(1)}, u32[]{:S(2)}) copy-start(bf16[4,2,3,64,192]{4,3,2,1,0:T(8,128)(2,1)S(1)} %all_gather.3.refs_3_.refs_7_) | copy-start | bytes 1769476
  154.1 15.6 %collective-permute-start = (bf16[4,2,3,64,192]{4,3,2,1,0:T(8,128)(2,1)S(1)}, bf16[4,2,3,64,192]{4,3,2,1,0:T(8,128)(2,1)S(1)}, u32[]{:S(2)}, u32[]{:S(2)}) collective-permute-start(bf16[4,2,3,64,192]{4,3,2,1,0:T(8,128)(2,1)S(1)} %all_gather.3.refs_3_.refs_7_), channel_id=1, source_target_pairs={{0,1},{1,0},{2,3},{3,2},{4,5},{5,4},{6,7},{7,6},{8,9},{9,8},{10,11... | collective-permute-start | bytes 1769480 | tf_op jit(solution)/shard_map/ppermute | solution.py:275
  169.7 0.9 copy-start.1
  170.5 35.6 %copy-start.4 = (bf16[2,2,64,192]{3,2,1,0:T(8,128)(2,1)S(1)}, bf16[2,2,64,192]{3,2,1,0:T(8,128)(2,1)}, u32[]{:S(2)}) copy-start(bf16[2,2,64,192]{3,2,1,0:T(8,128)(2,1)} %reshape.43.refs_1_.refs_2_) | copy-start | bytes 294916
  198.6 0.6 copy-start.10
  206.2 25.6 %collective-permute-start.1 = (bf16[2,2,64,192]{3,2,1,0:T(8,128)(2,1)S(1)}, bf16[2,2,64,192]{3,2,1,0:T(8,128)(2,1)S(1)}, u32[]{:S(2)}, u32[]{:S(2)}) collective-permute-start(bf16[2,2,64,192]{3,2,1,0:T(8,128)(2,1)S(1)} %copy-done.4), channel_id=1, source_target_pairs={{0,2},{2,4},{4,6},{6,0},{1,3},{3,5},{5,7},{7,1},{8,10},{10,12},{12... | collective-permute-start | bytes 294920 | tf_op jit(solution)/shard_map/ppermute | solution.py:278
  217.0 14.8 %collective-permute-start.2 = (bf16[2,2,64,192]{3,2,1,0:T(8,128)(2,1)S(1)}, bf16[2,2,64,192]{3,2,1,0:T(8,128)(2,1)S(1)}, u32[]{:S(2)}, u32[]{:S(2)}) collective-permute-start(bf16[2,2,64,192]{3,2,1,0:T(8,128)(2,1)S(1)} %copy-done.4), channel_id=1, source_target_pairs={{2,0},{4,2},{6,4},{0,6},{3,1},{5,3},{7,5},{1,7},{10,8},{12,10},{14... | collective-permute-start | bytes 294920 | tf_op jit(solution)/shard_map/ppermute | solution.py:279
  231.8 0.6 copy-start.6
  231.8 0.7 copy-start.7
  267.7 34.3 %copy-start.2 = (bf16[4,2,2,80,192]{4,3,2,1,0:T(8,128)(2,1)}, bf16[4,2,2,80,192]{4,3,2,1,0:T(8,128)(2,1)S(1)}, u32[]{:S(2)}) copy-start(bf16[4,2,2,80,192]{4,3,2,1,0:T(8,128)(2,1)S(1)} %all_to_all.20.two) | copy-start | bytes 1474564
  267.7 34.3 %all-to-all-start.3 = ((bf16[4,2,2,64,192]{4,3,2,1,0:T(8,128)(2,1)}), bf16[4,2,2,64,192]{4,3,2,1,0:T(8,128)(2,1)S(1)}, u32[]{:S(2)}, u32[]{:S(2)}) async-start(bf16[4,2,2,64,192]{4,3,2,1,0:T(8,128)(2,1)} %get-tuple-element.11), calls=%async_computation.3 | async-start | bytes 1048576 | tf_op jit(solution)/shard_map/all_to_all | solution.py:286
  271.3 0.6 copy-start.9
  302.0 0.8 copy-start.3

commit v2 on v0

v2 whole, which is shorter than its diff:
```python
import math

import jax
import jax.numpy as jnp
import numpy as np
from jax import lax
from jax.experimental import pallas as pl
from jax.experimental.pallas import tpu as pltpu
from jax.sharding import Mesh
from jax.sharding import PartitionSpec as P

tv_weight = 0.15
smoothing = 0.6
f32 = jnp.float32
bf16 = jnp.bfloat16

LANE = 128
HALF = 64
WIDE = 384


def dft(length, direction):
    counter = np.arange(length)
    angle = (counter[:, None] * counter[None, :] % length).astype(np.float32) * np.float32(2.0 * math.pi / length)
    factor = np.float32(1.0 / math.sqrt(length))
    return np.cos(angle) * factor, np.float32(direction) * np.sin(angle) * factor


def column_table(length, direction):
    real, imag = dft(length, direction)
    whole = np.concatenate(
        [np.concatenate([real, imag], axis=1), np.concatenate([-imag, real], axis=1)], axis=0
    )
    order = np.concatenate(
        [
            np.arange(LANE),
            length + np.arange(LANE),
            np.arange(LANE, length),
            length + np.arange(LANE, length),
        ]
    )
    packed = whole[order][:, order]
    tail = np.concatenate([-packed[:, WIDE - HALF :], packed[:, WIDE - LANE : WIDE - HALF]], axis=1)
    return jnp.asarray(np.concatenate([packed, tail], axis=1), dtype=bf16)


def depth_table(length, direction):
    real, imag = dft(length, direction)
    return jnp.asarray(
        np.concatenate(
            [np.concatenate([real, -imag], axis=1), np.concatenate([imag, real], axis=1)], axis=0
        ),
        dtype=bf16,
    )


def dot(a, b):
    return jnp.dot(a, b, preferred_element_type=f32)


def lanes(*pieces):
    return jnp.concatenate(pieces, axis=1)


def stack(*pieces):
    return jnp.concatenate(pieces, axis=0)


def left_half(shape):
    return lax.broadcasted_iota(jnp.int32, shape, 1) < HALF


def swapped(d):
    return pltpu.roll(d, HALF, 1)


def times_i(d):
    other = swapped(d)
    return jnp.where(left_half(d.shape), -other, other)


def doubled(d):
    other = swapped(d)
    left = left_half(d.shape)
    return jnp.where(left, d, other), jnp.where(left, other, d)


def mask_lanes(mask):
    mask = mask.astype(f32)
    return mask[:, :LANE], lanes(mask[:, LANE:], mask[:, LANE:])


def call(kernel, name, flops, **kwargs):
    return pl.pallas_call(
        kernel,
        name=name,
        cost_estimate=pl.CostEstimate(flops=flops, transcendentals=0, bytes_accessed=2**20),
        **kwargs,
    )


SMEM = pl.BlockSpec(memory_space=pltpu.SMEM)
VMEM = pl.BlockSpec(memory_space=pltpu.VMEM)


def depart(where, data, sampling, coils, depth_inv, nhi, group):
    encodings, rows, slices, _ = data.shape[1:]
    images = encodings * rows

    def kernel(where_ref, data_ref, mask_ref, coil_ref, table, out):
        for e in range(encodings):
            weight = -mask_ref[e].astype(f32)
            for r in range(rows):
                both = stack(*((data_ref[c, e, r].astype(f32) * weight).astype(bf16) for c in range(2)))
                both = dot(table[...], both)
                real, imag = both[:slices], both[slices:]
                at = (e * rows + r) * WIDE
                out[:, at : at + LANE] = real[:, :LANE].astype(bf16)
                out[:, at + LANE : at + 2 * LANE] = imag[:, :LANE].astype(bf16)
                out[:, at + 2 * LANE : at + WIDE] = lanes(real[:, LANE:], imag[:, LANE:]).astype(bf16)
        first = where_ref[3] * group
        for k in range(group):
            real, imag = coil_ref[0, first + k].astype(f32), coil_ref[1, first + k].astype(f32)
            block = lanes(real[:, :LANE], imag[:, :LANE], lanes(real[:, LANE:], imag[:, LANE:]))
            block = stack(block, block).astype(bf16)
            at = (images + k) * WIDE
            for h in range(nhi // 2):
                out[16 * h : 16 * h + 16, at : at + WIDE] = block

    return call(
        kernel,
        "depart",
        10**8,
        in_specs=[SMEM, VMEM, VMEM, VMEM, VMEM],
        out_specs=VMEM,
        out_shape=jax.ShapeDtypeStruct((slices, (images + group) * WIDE), bf16),
    )(where, data, sampling, coils, depth_inv)


def slab_gradient(packed, coil_rows, column_inv, encodings, nhi):
    rows, _, slices, lines = coil_rows.shape

    def kernel(in_ref, coil_ref, table, out, send):
        images = [in_ref[:, i * WIDE : (i + 1) * WIDE] for i in range(encodings * rows)]
        fine = dot(stack(*images), table[...])
        coil = []
        for r in range(rows):
            real, imag = coil_ref[r, 0].astype(f32), coil_ref[r, 1].astype(f32)
            coil.append(
                (
                    real[:, :LANE],
                    imag[:, :LANE],
                    lanes(real[:, LANE:], real[:, LANE:]),
                    lanes(imag[:, LANE:], imag[:, LANE:]),
                )
            )
        even = lax.rem(lax.broadcasted_iota(jnp.int32, (8, WIDE), 0) // 2, 2) == 0
        for e in range(encodings):
            total = jnp.zeros((8, WIDE), f32)
            for r in range(rows):
                at = (e * rows + r) * slices
                a, b, d, t = (fine[at : at + slices, j * LANE : (j + 1) * LANE] for j in range(4))
                ca, cb, dr, di = coil[r]
                value = lanes(ca * a + cb * b, ca * b - cb * a, dr * d - di * t)
                value = jnp.sum(value.reshape(slices // 8, 8, WIDE), axis=0)
                turned = (-2 * r) % 8
                one = value if turned == 0 else pltpu.roll(value, turned, 0)
                two = pltpu.roll(value, (turned + 4) % 8, 0) if (turned + 4) % 8 else value
                total = total + jnp.where(even, one, two)
            for x in range(4):
                out[x, :, e * WIDE : (e + 1) * WIDE] = pltpu.roll(total, 8 - 2 * x, 0) if x else total
            block = stack(total, total).astype(bf16)
            for h in range(nhi // 2):
                send[16 * h : 16 * h + 16, e * WIDE : (e + 1) * WIDE] = block

    return call(
        kernel,
        "slab_gradient",
        10**8,
        in_specs=[VMEM, VMEM, VMEM],
        out_specs=[VMEM, VMEM],
        out_shape=[
            jax.ShapeDtypeStruct((4, 8, encodings * WIDE), f32),
            jax.ShapeDtypeStruct((slices, encodings * WIDE), bf16),
        ],
    )(packed, coil_rows, column_inv)


def step_length(norm_ref):
    gg, ee = (jnp.sum(norm_ref[:, i : i + 1, :], axis=0) for i in range(2))
    return gg / (ee + 4.0 * tv_weight / smoothing * gg + 1e-06)


def image_step(where, image, extra, sampling, own, other, tables, nlo, members, second):
    column_fwd, column_inv, depth_fwd, depth_inv = tables
    slices, width = image.shape
    encodings = width // WIDE
    steps = own.shape[0]
    group = own.shape[2] // WIDE
    block = group * encodings * slices

    def kernel(*refs):
        refs = list(refs)
        where_ref = refs.pop(0)
        if second:
            norms_ref, image_ref, before_ref, after_ref, normal_ref, *firsts = (refs.pop(0) for _ in range(8))
        else:
            image_ref = refs.pop(0)
        mask_ref, own_ref, other_ref, wf, wi, zf, zi = (refs.pop(0) for _ in range(7))
        sends = [refs.pop(0) for _ in range(3)]
        norm_ref, out_ref = refs.pop(0), refs.pop(0)
        value, ahead_ref, mask_a, mask_d, masked, product, squares = refs
        step = pl.program_id(0)
        hi, lo, core = where_ref[0], where_ref[1], where_ref[2]

        def column(ref, e, j):
            at = e * WIDE + j * LANE
            return ref[:, at : at + LANE].astype(f32)

        @pl.when(step == 0)
        def _():
            total = jnp.zeros((slices, LANE), f32)
            for e in range(encodings):
                now = [column(image_ref, e, j) for j in range(3)]
                if second:
                    alpha = step_length(norms_ref)
                    new = [-alpha * v for v in now]
                    slopes = []
                    for d in (
                        [new[j] + alpha * column(before_ref, e, j) for j in range(3)],
                        [-alpha * column(after_ref, e, j) - new[j] for j in range(3)],
                    ):
                        near = jnp.sqrt(d[0] * d[0] + d[1] * d[1] + smoothing * smoothing)
                        square = d[2] * d[2]
                        far = jnp.sqrt(square + swapped(square) + smoothing * smoothing)
                        slopes.append([d[0] / near, d[1] / near, d[2] / far])
                    now = [
                        now[j] - alpha * column(normal_ref, e, j) + tv_weight * (slopes[0][j] - slopes[1][j])
                        for j in range(3)
                    ]
                    for j in range(3):
                        at = e * WIDE + j * LANE
                        ahead_ref[:, at : at + LANE] = now[j]
                for j in range(3):
                    at = e * WIDE + j * LANE
                    total = total + now[j] * now[j]
                    now[j] = now[j].astype(bf16).astype(f32)
                    value[:, e * 512 + j * LANE : e * 512 + (j + 1) * LANE] = now[j]
                value[:, e * 512 + 3 * LANE : (e + 1) * 512] = times_i(now[2])
                a, d = mask_lanes(mask_ref[e])
                mask_a[:, e * LANE : (e + 1) * LANE] = a
                mask_d[:, e * LANE : (e + 1) * LANE] = d
            norm_ref[:, 0:1, :] = jnp.full((members, 1, LANE), jnp.sum(total), f32)
            squares[...] = jnp.zeros(squares.shape, f32)
            if not second:
                out_ref[...] = jnp.zeros(out_ref.shape, f32)

        for half, coil_ref in ((0, own_ref), (1, other_ref)):

            def coil_lanes(k):
                a, b, d = (coil_ref[0, :, k * WIDE + j * LANE : k * WIDE + (j + 1) * LANE].astype(f32) for j in range(3))
                return (a, b, *doubled(d))

            for k in range(group):
                ca, cb, dr, di = coil_lanes(k)
                for e in range(encodings):
                    va, vb, vd, vt = (value[:, e * 512 + j * LANE : e * 512 + (j + 1) * LANE] for j in range(4))
                    at = (k * encodings + e) * slices
                    product[at : at + slices, :LANE] = (ca * va - cb * vb).astype(bf16)
                    product[at : at + slices, LANE : 2 * LANE] = (ca * vb + cb * va).astype(bf16)
                    product[at : at + slices, 2 * LANE :] = (dr * vd + di * vt).astype(bf16)
            u = dot(product[...], wf[...]).astype(bf16)
            weight_a, weight_d = mask_a[...], mask_d[...]
            total = jnp.zeros(weight_a.shape, f32)
            for k in range(group):

                def pair(j):
                    return lanes(
                        *(
                            u[(k * encodings + e) * slices : (k * encodings + e + 1) * slices, j * LANE : (j + 1) * LANE]
                            for e in range(encodings)
                        )
                    )

                near = dot(zf[...], stack(pair(0), pair(1)))
                far = dot(zi[...], stack(pair(2), pair(3)))
                sa, sb = near[:slices] * weight_a, near[slices:] * weight_a
                sd, st = far[:slices] * weight_d, far[slices:] * weight_d
                total = total + (sa * sa + sb * sb + sd * sd)
                sa, sb, sd, st = (x.astype(bf16) for x in (sa, sb, sd, st))
                for e in range(encodings):
                    for j, x in enumerate((sa, sb, sd)):
                        at = e * WIDE + j * LANE
                        masked[half * group + k, :, at : at + LANE] = x[:, e * LANE : (e + 1) * LANE]
                if not second:
                    near = dot(zi[...], stack(sa, sb)).astype(bf16)
                    far = dot(zf[:slices, :], stack(sd, st)).astype(bf16)
                    for e in range(encodings):
                        at = (k * encodings + e) * slices
                        for j, x in enumerate((near[:slices], near[slices:], far)):
                            product[at : at + slices, j * LANE : (j + 1) * LANE] = x[:, e * LANE : (e + 1) * LANE]
            squares[...] += total
            if not second:
                q = dot(product[...], wi[...])
                sums = [[0.0, 0.0, 0.0] for _ in range(encodings)]
                for k in range(group):
                    ca, cb, dr, di = coil_lanes(k)
                    for e in range(encodings):
                        at = (k * encodings + e) * slices
                        qa, qb, qd, qt = (q[at : at + slices, j * LANE : (j + 1) * LANE] for j in range(4))
                        sums[e][0] += ca * qa + cb * qb
                        sums[e][1] += ca * qb - cb * qa
                        sums[e][2] += dr * qd - di * qt
                for e in range(encodings):
                    for j in range(3):
                        at = e * WIDE + j * LANE
                        out_ref[:, at : at + LANE] += sums[e][j]
            owner = 2 * step + (core if half == 0 else 1 - core)

            @pl.when(owner == hi)
            def _():
                for j, send_ref in enumerate(sends):
                    dest = lax.bitwise_xor(lo, j)
                    coil = (3 * dest + lax.rem(lo + dest, nlo)) // nlo
                    send_ref[:slices] = masked[half * group + coil]

        @pl.when(step == steps - 1)
        def _():
            if second:
                piece = ahead_ref[pl.ds(pl.multiple_of(8 * hi, 8), 8), :]
                turned = [pltpu.roll(piece, 8 - 2 * dest, 0) if dest else piece for dest in range(nlo)]
                for j in range(nlo):
                    dest = lax.bitwise_xor(lo, j)
                    part = turned[0]
                    for k in range(1, nlo):
                        part = jnp.where(dest == k, turned[k], part)
                    part = stack(part, part).astype(bf16)
                    if j < 3:
                        sends[j][slices : slices + 16] = part
                        sends[j][slices + 16 :] = firsts[j][...]
                    else:
                        out_ref[...] = part
            norm_ref[:, 1:2, :] = jnp.full((members, 1, LANE), jnp.sum(squares[...]), f32)

    def whole(array):
        return pl.BlockSpec(array.shape, lambda g, _n=array.ndim: (0,) * _n)

    coil_spec = pl.BlockSpec((1,) + own.shape[1:], lambda g: (g, 0, 0))
    consts = [column_fwd, column_inv, depth_fwd, depth_inv]
    arrays = [*extra[:1], image, *extra[1:], sampling]
    height = 2 * slices + 16 if second else slices
    outs = [jax.ShapeDtypeStruct((height, width), bf16)] * 3
    outs.append(jax.ShapeDtypeStruct((members, 2, LANE), f32))
    outs.append(jax.ShapeDtypeStruct((16, width), bf16) if second else jax.ShapeDtypeStruct(image.shape, f32))
    return call(
        kernel,
        "second_step" if second else "first_step",
        (2 if second else 4) * 10**9,
        grid=(steps,),
        in_specs=[SMEM] + [whole(a) for a in arrays] + [coil_spec, coil_spec] + [whole(a) for a in consts],
        out_specs=[whole(o) for o in outs],
        out_shape=outs,
        scratch_shapes=[
            pltpu.VMEM((slices, encodings * 512), f32),
            pltpu.VMEM((slices, width), f32),
            pltpu.VMEM((slices, encodings * LANE), f32),
            pltpu.VMEM((slices, encodings * LANE), f32),
            pltpu.VMEM((2 * group, slices, width), bf16),
            pltpu.VMEM((block, WIDE), bf16),
            pltpu.VMEM((slices, encodings * LANE), f32),
        ],
    )(where, *arrays, own, other, *consts)


def finish(where, norms_one, norms_two, data, sampling, slab_one, rows, last, readout):
    encodings, nrows, slices, lines = data.shape[1:]

    def kernel(where_ref, norm_one, norm_two, data_ref, mask_ref, slab, keep, near, far, last_ref, out, image):
        lo = where_ref[1]
        alphas = step_length(norm_one), step_length(norm_two)
        for j, rows_ref in enumerate((keep, near, far)):
            r = jnp.where(lax.rem(lo, 2) == 0, j, nrows - 1 - j)
            for e in range(encodings):
                weight = mask_ref[e].astype(f32)
                real, imag = (-(data_ref[c, e, r].astype(f32) * weight) for c in range(2))
                a, b, d = (
                    alphas[0] * rows_ref[slices + 16 :, e * WIDE + k * LANE : e * WIDE + (k + 1) * LANE].astype(f32)
                    + alphas[1] * rows_ref[:slices, e * WIDE + k * LANE : e * WIDE + (k + 1) * LANE].astype(f32)
                    for k in range(3)
                )
                out[0, e, r, :, :LANE] = real[:, :LANE] - a
                out[1, e, r, :, :LANE] = imag[:, :LANE] - b
                out[0, e, r, :, LANE:] = real[:, LANE:] - d[:, :HALF]
                out[1, e, r, :, LANE:] = imag[:, LANE:] - swapped(d)[:, :HALF]
        for j in range(readout):
            x = lax.bitwise_xor(lo, j)
            for e in range(encodings):
                for k in range(3):
                    at = e * WIDE + k * LANE
                    if j < 3:
                        step = (keep, near, far)[j][slices : slices + 16, at : at + LANE]
                    else:
                        step = last_ref[:, at : at + LANE]
                    value = -alphas[0] * slab[x, :, at : at + LANE] - alphas[1] * step.astype(f32)[:8]
                    if k < 2:
                        image[k, e, x, :, :LANE] = value[:2]
                    else:
                        image[0, e, x, :, LANE:] = value[:2, :HALF]
                        image[1, e, x, :, LANE:] = swapped(value)[:2, :HALF]

    return call(
        kernel,
        "finish",
        10**7,
        in_specs=[SMEM] + [VMEM] * 9,
        out_specs=[VMEM, VMEM],
        out_shape=[
            jax.ShapeDtypeStruct(data.shape, f32),
            jax.ShapeDtypeStruct((2, encodings, readout, 2, lines), f32),
        ],
    )(where, norms_one, norms_two, data, sampling, slab_one, *rows, last)


def body(kspace_data, coil_maps, sampling):
    encodings = kspace_data.shape[2]
    rows = kspace_data.shape[3]
    slices = kspace_data.shape[4]
    coils, readout, zdepth, lines = coil_maps.shape[1:]
    nhi, nlo = lax.axis_size("hi"), lax.axis_size("lo")
    nphase, ncore = lax.axis_size("phase"), lax.axis_size("enc")
    slabs = nhi * nlo
    group = coils // (nphase * ncore)
    assert (nlo, readout, rows, zdepth, lines, slices) == (4, 4, 3, 2, LANE + HALF, 2 * slabs)
    assert group * nhi == coils and nphase * ncore == nhi and ncore == 2
    phase, core = lax.axis_index("phase"), lax.axis_index("enc")
    share_index = phase * ncore + core
    where = jnp.stack([lax.axis_index("hi"), lax.axis_index("lo"), core, share_index]).astype(jnp.int32)
    column_fwd, column_inv = column_table(lines, -1.0), column_table(lines, 1.0)
    depth_fwd, depth_inv = depth_table(slices, -1.0), depth_table(slices, 1.0)
    tables = (column_fwd, column_inv, depth_fwd, depth_inv)
    sampling = sampling[0]
    data = kspace_data[:, 0]

    def round_ring(value):
        value = value.reshape(slabs, zdepth, -1)
        return lax.all_to_all(value, ("hi", "lo"), 0, 0, tiled=True).reshape(slices, -1)

    packed = depart(where, data, sampling, coil_maps.reshape(2, coils, -1, lines), depth_inv, nhi, group)
    packed = round_ring(packed)
    coil_rows = coil_maps.reshape(2, slabs, rows, zdepth, lines).transpose(2, 0, 1, 3, 4)
    coil_rows = coil_rows.reshape(rows, 2, slices, lines)
    slab_one, spread = slab_gradient(packed, coil_rows, column_inv, encodings, nhi)
    one = round_ring(spread)
    own = lax.all_gather(packed[:, encodings * rows * WIDE :], "phase")
    other = lax.ppermute(own, "enc", [(i, (i + 1) % ncore) for i in range(ncore)])

    up = [(i, (i + 1) % nphase) for i in range(nphase)]
    before = lax.ppermute(one, "phase", up)
    after = lax.ppermute(one, "phase", [(j, i) for i, j in up])

    def total(norms):
        return lax.all_to_all(norms, ("lo", "phase", "enc"), 0, 0, tiled=True)

    members = nlo * nphase * ncore

    def swap(value, j):
        return lax.ppermute(value, "lo", [(i, i ^ j) for i in range(nlo)])

    *rows_one, norms, normal = image_step(where, one, (), sampling, own, other, tables, nlo, members, False)
    norms_one = total(norms)
    extra = (norms_one, before, after, normal, *rows_one)
    *rows_two, norms, last = image_step(where, one, extra, sampling, own, other, tables, nlo, members, True)
    norms_two = total(norms)
    got = [rows_two[0], swap(rows_two[1], 1), swap(rows_two[2], 2)]
    last = swap(last, 3)
    residual, image = finish(where, norms_one, norms_two, data, sampling, slab_one, got, last, readout)
    return (image[:, None], residual[:, None])


def solution(mesh):
    names = dict(mesh.shape)
    nlo = 4
    grid = Mesh(
        mesh.devices.reshape(names["pat"], names["slab"] // nlo, nlo, names["phase"], names["enc"]),
        ("pat", "hi", "lo", "phase", "enc"),
    )
    slab = ("hi", "lo")
    in_specs = (
        P("pat", "phase", "enc", slab, None, None),
        P("pat", None, None, slab, None),
        P("phase", "enc", "pat", None),
    )
    out_specs = (
        P("pat", "phase", "enc", None, slab, None),
        P("pat", "phase", "enc", slab, None, None),
    )
    return jax.shard_map(body, mesh=grid, in_specs=in_specs, out_specs=out_specs, check_vma=False)
```

time: 448 us -> 217 us (0.48)
  blocking collectives: 144 us -> 11.9 us
  waiting for transfers between devices: 185 us -> 76.2 us
  Pallas kernels: 0 us -> 28 us
  matrix products: 20.4 us -> 0 us
  starting transfers between devices: 75.6 us -> 88.6 us
  other arithmetic: 8.78 us -> 0.59 us
    psum x6 -> x0, blocking collectives: 144 us -> none  [over_axes(): return functools.reduce(lax.psum, axes, value)]
    all_to_all x4, waiting for transfers between devices: 179 us -> 63 us  [the longest x2 63 us: round_ring(): lax.all_to_all(value, ('hi', 'lo'), 0, 0, tiled=True).reshape(slices, -1)]
    pallas_call x0 -> x5, Pallas kernels: none -> 28 us  [the longest x2 20.9 us: image_step(): call(kernel, 'second_step' if second else 'first_step', (2 if second else...]
    dot_general x32 -> x0, matrix products: 20.4 us -> none  [the longest x4 4.1 us: along_rows(): jnp.matmul(imag_part, cosine, preferred_element_type=jnp.float32)]
    all_gather x0 -> x1, blocking collectives: none -> 11.9 us  [body(): own = lax.all_gather(packed[:, encodings * rows * WIDE:], 'phase')]
    ppermute x4 -> x6, starting transfers between devices: 12.3 us -> 21.4 us  [the longest x3 9.4 us: swap(): return lax.ppermute(value, 'lo', [(i, i ^ j) for i in range(nlo)])]
    ppermute x4 -> x6, waiting for transfers between devices: 5.94 us -> 13.2 us  [the longest x3 8.56 us: swap(): return lax.ppermute(value, 'lo', [(i, i ^ j) for i in range(nlo)])]
    reshape x0 -> x7, local copies, waits for them, and re-layouts: none -> 7.15 us  [the longest x2 3.51 us: round_ring(): value = value.reshape(slabs, zdepth, -1)]
  transfers between devices with their start and end apart: 8 -> 10, of which waited for: 6 -> 5; matrix products, arithmetic and copies ran while one was open for 0% -> 1% of each run, Pallas kernels for 0% -> 0%
where the time goes in v2:
time: 217 us; the launch traced here: 216 us
  starting transfers between devices  88.6 us (41%)
  waiting for transfers between devices  76.2 us (35%)
  Pallas kernels  28 us (13%)
  blocking collectives  11.9 us (5%)
  local copies, waits for them, and re-layouts  10.1 us (5%)
    all_to_all x2, waiting for transfers between devices, round_ring(): lax.all_to_all(value, ('hi', 'lo'), 0, 0, tiled=True).reshape(slices, -1)  63 us
    all_to_all x2, starting transfers between devices, round_ring(): lax.all_to_all(value, ('hi', 'lo'), 0, 0, tiled=True).reshape(slices, -1)  51.3 us
    pallas_call x2, Pallas kernels, image_step(): call(kernel, 'second_step' if second else 'first_step', (2 if second else...  20.9 us
    all_to_all x2, starting transfers between devices, total(): return lax.all_to_all(norms, ('lo', 'phase', 'enc'), 0, 0, tiled=True)  15.9 us
    all_gather x1, blocking collectives, body(): own = lax.all_gather(packed[:, encodings * rows * WIDE:], 'phase')  11.9 us
    ppermute x3, starting transfers between devices, swap(): return lax.ppermute(value, 'lo', [(i, i ^ j) for i in range(nlo)])  9.4 us
    ppermute x3, waiting for transfers between devices, swap(): return lax.ppermute(value, 'lo', [(i, i ^ j) for i in range(nlo)])  8.56 us
    ppermute x1, starting transfers between devices, body(): lax.ppermute(own, 'enc', [(i, (i + 1) % ncore) for i in range(ncore)])  5.55 us
  transfers between devices with their start and end apart: 10, of which 5 were waited for; matrix products, arithmetic and copies ran while one was open for 1% of the time, Pallas kernels for 0%

profile of v2, /device:TPU:33, one launch (start us, length us, event | category | flops | bytes accessed | tf_op | source)
XLA Modules:
  0.0 216.3 jit_solution(12555882870837471431)
XLA Ops:
  0.6 1.8 reshape.25.coil_ref
  2.4 0.6 pad_add_fusion.where_ref.refs_0_
  3.0 2.2 %depart.1 = bf16[64,3456]{1,0:T(8,128)(2,1)} custom-call(s32[4]{0:T(128)} %pad_add_fusion.where_ref.refs_0_, bf16[2,2,3,64,192]{4,3,2,1,0:T(8,128)(2,1)} %bitcast.17, s32[2,64,192]{2,1,0:T(8,128)} %bitcast.24, bf16[2,24,8,192]{3,2,1,0:T(8,128)(2,1)} %reshape.25.coil_ref, bf16[128,128]{1,0:T(8,128)(2,1)} %constant.29.clone.table.refs_8_.refs_15_), custom_call_target="tpu_custom_call" | custom-call | flops 100000000 | bytes 1048576 | tf_op jit(solution)/shard_map/depart/pallas_call | solution.py:130
  5.2 2.0 reshape.26
  7.2 46.4 %all-to-all-start = ((bf16[32,2,3456]{2,1,0:T(2,128)(2,1)}), bf16[32,2,3456]{2,1,0:T(2,128)(2,1)S(1)}, u32[]{:S(2)}, u32[]{:S(2)}) async-start(bf16[32,2,3456]{2,1,0:T(2,128)(2,1)} %reshape.26), calls=%async_computation | async-start | bytes 884736 | tf_op jit(solution)/shard_map/all_to_all | solution.py:446
  53.8 0.9 reshape.29.coil_ref
  54.7 55.5 %all-to-all-done = bf16[32,2,3456]{2,1,0:T(2,128)(2,1)S(1)} async-done(((bf16[32,2,3456]{2,1,0:T(2,128)(2,1)}), bf16[32,2,3456]{2,1,0:T(2,128)(2,1)S(1)}, u32[]{:S(2)}, u32[]{:S(2)}) %all-to-all-start) | async-done | bytes 442400 | tf_op jit(solution)/shard_map/all_to_all | solution.py:446
  110.2 0.2 reshape.27.in_ref
  110.4 0.8 copy-done
  111.1 2.3 %slab_gradient.1 = (f32[4,8,768]{2,1,0:T(8,128)}, bf16[64,768]{1,0:T(8,128)(2,1)}) custom-call(bf16[64,3456]{1,0:T(8,128)(2,1)} %copy-done, bf16[3,2,64,192]{3,2,1,0:T(8,128)(2,1)} %reshape.29.coil_ref, bf16[384,512]{1,0:T(8,128)(2,1)} %constant.27.clone.table.refs_6_.refs_13_), custom_call_target="tpu_custom_call" | custom-call | flops 100000000 | bytes 1048576 | tf_op jit(solution)/shard_map/slab_gradient/pallas_call | solution.py:176
  113.4 1.6 reshape.30
  115.0 4.9 %all-to-all-start.1 = ((bf16[32,2,768]{2,1,0:T(2,128)(2,1)}), bf16[32,2,768]{2,1,0:T(2,128)(2,1)S(1)}, u32[]{:S(2)}, u32[]{:S(2)}) async-start(bf16[32,2,768]{2,1,0:T(2,128)(2,1)} %reshape.30), calls=%async_computation.1 | async-start | bytes 196608 | tf_op jit(solution)/shard_map/all_to_all | solution.py:446
  119.9 11.9 %all-gather = bf16[256,1152]{1,0:T(8,128)(2,1)S(1)} all-gather(bf16[64,1152]{1,0:T(8,128)(2,1)S(1)} %slice-done), channel_id=2, replica_groups=mesh['pat'=2,'hi'=8,'lo'=4,'phase'=4,'enc'=2] {'phase'}, dimensions={0}, use_global_device_ids=true | all-gather | bytes 737280 | tf_op jit(solution)/shard_map/all_gather | solution.py:454
  131.8 5.6 %collective-permute-start = (bf16[4,64,1152]{2,1,0:T(8,128)(2,1)S(1)}, bf16[4,64,1152]{2,1,0:T(8,128)(2,1)S(1)}, u32[]{:S(2)}, u32[]{:S(2)}) collective-permute-start(bf16[4,64,1152]{2,1,0:T(8,128)(2,1)S(1)} %bitcast.21), channel_id=1, source_target_pairs={{0,1},{1,0},{2,3},{3,2},{4,5},{5,4},{6,7},{7,6},{8,9},{9,8},{10,11... | collective-permute-start | bytes 1769480 | tf_op jit(solution)/shard_map/ppermute | solution.py:455
  137.4 7.5 %all-to-all-done.1 = bf16[32,2,768]{2,1,0:T(2,128)(2,1)S(1)} async-done(((bf16[32,2,768]{2,1,0:T(2,128)(2,1)}), bf16[32,2,768]{2,1,0:T(2,128)(2,1)S(1)}, u32[]{:S(2)}, u32[]{:S(2)}) %all-to-all-start.1) | async-done | bytes 98336 | tf_op jit(solution)/shard_map/all_to_all | solution.py:446
  144.9 0.7 reshape.31.refs_1_.refs_2_
  145.6 0.8 copy-done.9
  146.4 13.0 %first_step.1 = (bf16[64,768]{1,0:T(8,128)(2,1)}, bf16[64,768]{1,0:T(8,128)(2,1)}, bf16[64,768]{1,0:T(8,128)(2,1)}, f32[32,2,128]{2,1,0:T(2,128)}, f32[64,768]{1,0:T(8,128)}) custom-call(s32[4]{0:T(128)} %pad_add_fusion.where_ref.refs_0_, bf16[64,768]{1,0:T(8,128)(2,1)} %reshape.31.refs_1_.refs_2_, s32[2,64,192]{2,1,0:T(8,128)} %bitcast.25, ...), custom_call_target="tpu_custom_call" | custom-call | flops 4000000000 | bytes 1048576 | tf_op jit(solution)/shard_map/first_step/pallas_call | solution.py:355
  159.4 8.9 %all-to-all-start.2 = ((f32[32,2,128]{2,1,0:T(2,128)}), f32[32,2,128]{2,1,0:T(2,128)S(1)}, u32[]{:S(2)}, u32[]{:S(2)}) async-start(f32[32,2,128]{2,1,0:T(2,128)} %get-tuple-element.17), calls=%async_computation.2 | async-start | bytes 65536 | tf_op jit(solution)/shard_map/all_to_all | solution.py:462
  168.2 4.5 %collective-permute-start.2 = (bf16[64,768]{1,0:T(8,128)(2,1)S(1)}, bf16[64,768]{1,0:T(8,128)(2,1)S(1)}, u32[]{:S(2)}, u32[]{:S(2)}) collective-permute-start(bf16[64,768]{1,0:T(8,128)(2,1)S(1)} %copy-done.7), channel_id=1, source_target_pairs={{2,0},{4,2},{6,4},{0,6},{3,1},{5,3},{7,5},{1,7},{10,8},{12,10},{14... | collective-permute-start | bytes 294920 | tf_op jit(solution)/shard_map/ppermute | solution.py:459
  172.8 2.0 collective-permute-start.1
  174.7 4.6 %collective-permute-done.1.refs_3_ = bf16[64,768]{1,0:T(8,128)(2,1)S(1)} collective-permute-done((bf16[64,768]{1,0:T(8,128)(2,1)S(1)}, bf16[64,768]{1,0:T(8,128)(2,1)S(1)}, u32[]{:S(2)}, u32[]{:S(2)}) %collective-permute-start.1) | collective-permute-done | bytes 98336 | tf_op jit(solution)/shard_map/ppermute | solution.py:458
  179.4 0.6 copy-done.11
  180.0 7.9 %second_step.1 = (bf16[144,768]{1,0:T(8,128)(2,1)}, bf16[144,768]{1,0:T(8,128)(2,1)}, bf16[144,768]{1,0:T(8,128)(2,1)}, f32[32,2,128]{2,1,0:T(2,128)}, bf16[16,768]{1,0:T(8,128)(2,1)}) custom-call(s32[4]{0:T(128)} %pad_add_fusion.where_ref.refs_0_, f32[32,2,128]{2,1,0:T(2,128)} %copy-done.5, bf16[64,768]{1,0:T(8,128)(2,1)} %reshape.31.refs_1_.refs_2_, ...), custom_call_target="tpu_custom_call" | custom-call | flops 2000000000 | bytes 1048576 | tf_op jit(solution)/shard_map/second_step/pallas_call | solution.py:355
  188.0 7.0 %all-to-all-start.3 = ((f32[32,2,128]{2,1,0:T(2,128)}), f32[32,2,128]{2,1,0:T(2,128)S(1)}, u32[]{:S(2)}, u32[]{:S(2)}) async-start(f32[32,2,128]{2,1,0:T(2,128)} %get-tuple-element.22), calls=%async_computation.3 | async-start | bytes 65536 | tf_op jit(solution)/shard_map/all_to_all | solution.py:462
  195.0 3.3 %collective-permute-start.3 = (bf16[144,768]{1,0:T(8,128)(2,1)}, bf16[144,768]{1,0:T(8,128)(2,1)S(1)}, u32[]{:S(2)}, u32[]{:S(2)}) collective-permute-start(bf16[144,768]{1,0:T(8,128)(2,1)} %get-tuple-element.25), channel_id=1, source_target_pairs={{0,8},{8,0},{16,24},{24,16},{1,9},{9,1},{17,25},{25,17},{2,10},{10... | collective-permute-start | bytes 663560 | tf_op jit(solution)/shard_map/ppermute | solution.py:467
  198.3 4.2 %collective-permute-start.4 = (bf16[144,768]{1,0:T(8,128)(2,1)}, bf16[144,768]{1,0:T(8,128)(2,1)S(1)}, u32[]{:S(2)}, u32[]{:S(2)}) collective-permute-start(bf16[144,768]{1,0:T(8,128)(2,1)} %get-tuple-element.26), channel_id=1, source_target_pairs={{0,16},{8,24},{16,0},{24,8},{1,17},{9,25},{17,1},{25,9},{2,18},{10... | collective-permute-start | bytes 663560 | tf_op jit(solution)/shard_map/ppermute | solution.py:467
  202.5 2.0 collective-permute-start.5
  204.4 6.3 %collective-permute-done.5.last_ref = bf16[16,768]{1,0:T(8,128)(2,1)S(1)} collective-permute-done((bf16[16,768]{1,0:T(8,128)(2,1)S(1)}, bf16[16,768]{1,0:T(8,128)(2,1)S(1)}, u32[]{:S(2)}, u32[]{:S(2)}) %collective-permute-start.5) | collective-permute-done | bytes 24608 | tf_op jit(solution)/shard_map/ppermute | solution.py:467
  210.8 2.2 %collective-permute-done.4.far = bf16[144,768]{1,0:T(8,128)(2,1)S(1)} collective-permute-done((bf16[144,768]{1,0:T(8,128)(2,1)}, bf16[144,768]{1,0:T(8,128)(2,1)S(1)}, u32[]{:S(2)}, u32[]{:S(2)}) %collective-permute-start.4) | collective-permute-done | bytes 221216 | tf_op jit(solution)/shard_map/ppermute | solution.py:467
  213.0 0.7 copy-done.4
  213.7 2.6 %finish.1 = (f32[2,2,3,64,192]{4,3,2,1,0:T(8,128)}, f32[2,2,4,2,192]{4,3,2,1,0:T(2,128)}) custom-call(s32[4]{0:T(128)} %pad_add_fusion.where_ref.refs_0_, f32[32,2,128]{2,1,0:T(2,128)} %copy-done.5, f32[32,2,128]{2,1,0:T(2,128)} %copy-done.6, bf16[2,2,3,64,192]{4,3,2,1,0:T(8,128)(2,1)} %bitcast.18, s32[2,64,192]{2,1,0:T(8,128)} %bitcast.27, ...), custom_call_target="tpu_custom_call" | custom-call | flops 10000000 | bytes 1048576 | tf_op jit(solution)/shard_map/finish/pallas_call | solution.py:411
  (30 shorter events, 0.3 us)
Async XLA Ops:
  7.2 46.4 %copy-start.1 = (bf16[2,24,4,2,192]{4,3,2,1,0:T(2,128)(2,1)S(1)}, bf16[2,24,4,2,192]{4,3,2,1,0:T(2,128)(2,1)}, u32[]{:S(2)}) copy-start(bf16[2,24,4,2,192]{4,3,2,1,0:T(2,128)(2,1)} %param.8) | copy-start | bytes 442372
  7.2 103.0 %all-to-all-start = ((bf16[32,2,3456]{2,1,0:T(2,128)(2,1)}), bf16[32,2,3456]{2,1,0:T(2,128)(2,1)S(1)}, u32[]{:S(2)}, u32[]{:S(2)}) async-start(bf16[32,2,3456]{2,1,0:T(2,128)(2,1)} %reshape.26), calls=%async_computation | async-start | bytes 884736 | tf_op jit(solution)/shard_map/all_to_all | solution.py:446
  110.3 0.8 copy-start
  115.0 4.9 %slice-start = ((bf16[64,3456]{1,0:T(8,128)(2,1)}), bf16[64,1152]{1,0:T(8,128)(2,1)S(1)}, s32[]{:S(2)}) async-start(bf16[64,3456]{1,0:T(8,128)(2,1)} %copy-done), calls=%async_computation.4 | async-start | bytes 294912 | tf_op jit(solution)/shard_map/slice | solution.py:454
  115.0 29.9 %all-to-all-start.1 = ((bf16[32,2,768]{2,1,0:T(2,128)(2,1)}), bf16[32,2,768]{2,1,0:T(2,128)(2,1)S(1)}, u32[]{:S(2)}, u32[]{:S(2)}) async-start(bf16[32,2,768]{2,1,0:T(2,128)(2,1)} %reshape.30), calls=%async_computation.1 | async-start | bytes 196608 | tf_op jit(solution)/shard_map/all_to_all | solution.py:446
  131.8 13.7 %copy-start.2 = (bf16[256,1152]{1,0:T(8,128)(2,1)}, bf16[256,1152]{1,0:T(8,128)(2,1)S(1)}, u32[]{:S(2)}) copy-start(bf16[256,1152]{1,0:T(8,128)(2,1)S(1)} %all-gather) | copy-start | bytes 1769476
  131.8 13.7 %collective-permute-start = (bf16[4,64,1152]{2,1,0:T(8,128)(2,1)S(1)}, bf16[4,64,1152]{2,1,0:T(8,128)(2,1)S(1)}, u32[]{:S(2)}, u32[]{:S(2)}) collective-permute-start(bf16[4,64,1152]{2,1,0:T(8,128)(2,1)S(1)} %bitcast.21), channel_id=1, source_target_pairs={{0,1},{1,0},{2,3},{3,2},{4,5},{5,4},{6,7},{7,6},{8,9},{9,8},{10,11... | collective-permute-start | bytes 1769480 | tf_op jit(solution)/shard_map/ppermute | solution.py:455
  145.6 22.7 %copy-start.7 = (bf16[64,768]{1,0:T(8,128)(2,1)S(1)}, bf16[64,768]{1,0:T(8,128)(2,1)}, u32[]{:S(2)}) copy-start(bf16[64,768]{1,0:T(8,128)(2,1)} %reshape.31.refs_1_.refs_2_) | copy-start | bytes 294916
  145.6 0.8 copy-start.9
  159.4 20.0 %all-to-all-start.2 = ((f32[32,2,128]{2,1,0:T(2,128)}), f32[32,2,128]{2,1,0:T(2,128)S(1)}, u32[]{:S(2)}, u32[]{:S(2)}) async-start(f32[32,2,128]{2,1,0:T(2,128)} %get-tuple-element.17), calls=%async_computation.2 | async-start | bytes 65536 | tf_op jit(solution)/shard_map/all_to_all | solution.py:462
  168.2 6.5 %collective-permute-start.2 = (bf16[64,768]{1,0:T(8,128)(2,1)S(1)}, bf16[64,768]{1,0:T(8,128)(2,1)S(1)}, u32[]{:S(2)}, u32[]{:S(2)}) collective-permute-start(bf16[64,768]{1,0:T(8,128)(2,1)S(1)} %copy-done.7), channel_id=1, source_target_pairs={{2,0},{4,2},{6,4},{0,6},{3,1},{5,3},{7,5},{1,7},{10,8},{12,10},{14... | collective-permute-start | bytes 294920 | tf_op jit(solution)/shard_map/ppermute | solution.py:459
  172.8 6.6 %collective-permute-start.1 = (bf16[64,768]{1,0:T(8,128)(2,1)S(1)}, bf16[64,768]{1,0:T(8,128)(2,1)S(1)}, u32[]{:S(2)}, u32[]{:S(2)}) collective-permute-start(bf16[64,768]{1,0:T(8,128)(2,1)S(1)} %copy-done.7), channel_id=1, source_target_pairs={{0,2},{2,4},{4,6},{6,0},{1,3},{3,5},{5,7},{7,1},{8,10},{10,12},{12... | collective-permute-start | bytes 294920 | tf_op jit(solution)/shard_map/ppermute | solution.py:458
  174.7 4.6 %copy-start.10 = (bf16[64,768]{1,0:T(8,128)(2,1)}, bf16[64,768]{1,0:T(8,128)(2,1)S(1)}, u32[]{:S(2)}) copy-start(bf16[64,768]{1,0:T(8,128)(2,1)S(1)} %collective-permute-done.2.refs_4_) | copy-start | bytes 294916
  179.4 0.6 copy-start.11
  179.4 0.7 copy-start.5
  188.0 14.5 %copy-start.12 = (bf16[16,768]{1,0:T(8,128)(2,1)S(1)}, bf16[16,768]{1,0:T(8,128)(2,1)}, u32[]{:S(2)}) copy-start(bf16[16,768]{1,0:T(8,128)(2,1)} %get-tuple-element.27) | copy-start | bytes 73732
  188.0 25.0 %all-to-all-start.3 = ((f32[32,2,128]{2,1,0:T(2,128)}), f32[32,2,128]{2,1,0:T(2,128)S(1)}, u32[]{:S(2)}, u32[]{:S(2)}) async-start(f32[32,2,128]{2,1,0:T(2,128)} %get-tuple-element.22), calls=%async_computation.3 | async-start | bytes 65536 | tf_op jit(solution)/shard_map/all_to_all | solution.py:462
  195.0 15.8 %collective-permute-start.3 = (bf16[144,768]{1,0:T(8,128)(2,1)}, bf16[144,768]{1,0:T(8,128)(2,1)S(1)}, u32[]{:S(2)}, u32[]{:S(2)}) collective-permute-start(bf16[144,768]{1,0:T(8,128)(2,1)} %get-tuple-element.25), channel_id=1, source_target_pairs={{0,8},{8,0},{16,24},{24,16},{1,9},{9,1},{17,25},{25,17},{2,10},{10... | collective-permute-start | bytes 663560 | tf_op jit(solution)/shard_map/ppermute | solution.py:467
  198.3 14.7 %collective-permute-start.4 = (bf16[144,768]{1,0:T(8,128)(2,1)}, bf16[144,768]{1,0:T(8,128)(2,1)S(1)}, u32[]{:S(2)}, u32[]{:S(2)}) collective-permute-start(bf16[144,768]{1,0:T(8,128)(2,1)} %get-tuple-element.26), channel_id=1, source_target_pairs={{0,16},{8,24},{16,0},{24,8},{1,17},{9,25},{17,1},{25,9},{2,18},{10... | collective-permute-start | bytes 663560 | tf_op jit(solution)/shard_map/ppermute | solution.py:467
  202.5 8.3 %collective-permute-start.5 = (bf16[16,768]{1,0:T(8,128)(2,1)S(1)}, bf16[16,768]{1,0:T(8,128)(2,1)S(1)}, u32[]{:S(2)}, u32[]{:S(2)}) collective-permute-start(bf16[16,768]{1,0:T(8,128)(2,1)S(1)} %copy-done.12), channel_id=1, source_target_pairs={{0,24},{8,16},{16,8},{24,0},{1,25},{9,17},{17,9},{25,1},{2,26},{10... | collective-permute-start | bytes 73736 | tf_op jit(solution)/shard_map/ppermute | solution.py:467
  210.8 2.2 %copy-start.8 = (bf16[16,768]{1,0:T(8,128)(2,1)}, bf16[16,768]{1,0:T(8,128)(2,1)S(1)}, u32[]{:S(2)}) copy-start(bf16[16,768]{1,0:T(8,128)(2,1)S(1)} %collective-permute-done.5.last_ref) | copy-start | bytes 73732
  210.8 2.2 %copy-start.3 = (bf16[144,768]{1,0:T(8,128)(2,1)}, bf16[144,768]{1,0:T(8,128)(2,1)S(1)}, u32[]{:S(2)}) copy-start(bf16[144,768]{1,0:T(8,128)(2,1)S(1)} %collective-permute-done.3.near) | copy-start | bytes 663556
  213.0 0.7 copy-start.4
  213.0 0.7 copy-start.6

commit v3 on v2

v3 whole, which is shorter than its diff:
```python
import math

import jax
import jax.numpy as jnp
import numpy as np
from jax import lax
from jax.experimental import pallas as pl
from jax.experimental.pallas import tpu as pltpu
from jax.sharding import Mesh
from jax.sharding import PartitionSpec as P

tv_weight = 0.15
smoothing = 0.6
f32 = jnp.float32
bf16 = jnp.bfloat16

LANE = 128
HALF = 64
WIDE = 384


def dft(length, direction):
    counter = np.arange(length)
    angle = (counter[:, None] * counter[None, :] % length).astype(np.float32) * np.float32(2.0 * math.pi / length)
    factor = np.float32(1.0 / math.sqrt(length))
    return np.cos(angle) * factor, np.float32(direction) * np.sin(angle) * factor


def column_table(length, direction):
    real, imag = dft(length, direction)
    whole = np.concatenate(
        [np.concatenate([real, imag], axis=1), np.concatenate([-imag, real], axis=1)], axis=0
    )
    order = np.concatenate(
        [
            np.arange(LANE),
            length + np.arange(LANE),
            np.arange(LANE, length),
            length + np.arange(LANE, length),
        ]
    )
    packed = whole[order][:, order]
    tail = np.concatenate([-packed[:, WIDE - HALF :], packed[:, WIDE - LANE : WIDE - HALF]], axis=1)
    return jnp.asarray(np.concatenate([packed, tail], axis=1), dtype=bf16)


def depth_table(length, direction):
    real, imag = dft(length, direction)
    return jnp.asarray(
        np.concatenate(
            [np.concatenate([real, -imag], axis=1), np.concatenate([imag, real], axis=1)], axis=0
        ),
        dtype=bf16,
    )


def dot(a, b):
    return jnp.dot(a, b, preferred_element_type=f32)


def lanes(*pieces):
    return jnp.concatenate(pieces, axis=1)


def stack(*pieces):
    return jnp.concatenate(pieces, axis=0)


def left_half(shape):
    return lax.broadcasted_iota(jnp.int32, shape, 1) < HALF


def swapped(d):
    return pltpu.roll(d, HALF, 1)


def times_i(d):
    other = swapped(d)
    return jnp.where(left_half(d.shape), -other, other)


def doubled(d):
    other = swapped(d)
    left = left_half(d.shape)
    return jnp.where(left, d, other), jnp.where(left, other, d)


def mask_lanes(mask):
    mask = mask.astype(f32)
    return mask[:, :LANE], lanes(mask[:, LANE:], mask[:, LANE:])


def call(kernel, flops, **kwargs):
    return pl.pallas_call(
        kernel,
        cost_estimate=pl.CostEstimate(flops=flops, transcendentals=0, bytes_accessed=2**20),
        compiler_params=pltpu.CompilerParams(vmem_limit_bytes=32 * 2**20),
        **kwargs,
    )


VMEM = pl.BlockSpec(memory_space=pltpu.VMEM)


def distant(value):
    return pltpu.with_memory_space_constraint(value, pltpu.HBM)


def depart(data, sampling, coils, depth_inv, nhi, group):
    encodings, rows, slices, _ = data.shape[1:]
    images = encodings * rows

    slabs = slices // 2

    def kernel(data_ref, mask_ref, coil_ref, table, out):
        share_index = lax.axis_index("phase") * lax.axis_size("enc") + lax.axis_index("enc")
        for e in range(encodings):
            weight = -mask_ref[e].astype(f32)
            for r in range(rows):
                both = stack(*((data_ref[c, e, r].astype(f32) * weight).astype(bf16) for c in range(2)))
                both = dot(table[...], both)
                real, imag = both[:slices], both[slices:]
                at = (e * rows + r) * WIDE
                for j, x in enumerate((real[:, :LANE], imag[:, :LANE], lanes(real[:, LANE:], imag[:, LANE:]))):
                    x = x.astype(bf16).reshape(slabs, 2, LANE)
                    out[:, :, at + j * LANE : at + (j + 1) * LANE] = x
        first = share_index * group
        for k in range(group):
            real, imag = (coil_ref[c, first + k].astype(f32) for c in range(2))
            tail = jnp.concatenate([real[:, :, LANE:], imag[:, :, LANE:]], axis=2)
            at = (images + k) * WIDE
            for j, x in enumerate((real[:, :, :LANE], imag[:, :, :LANE], tail)):
                x = x.astype(bf16)
                for h in range(nhi):
                    out[4 * h : 4 * h + 4, :, at + j * LANE : at + (j + 1) * LANE] = x

    return call(
        kernel,
        10**8,
        in_specs=[VMEM, VMEM, VMEM, VMEM],
        out_specs=VMEM,
        out_shape=jax.ShapeDtypeStruct((slabs, 2, (images + group) * WIDE), bf16),
    )(*(distant(a) for a in (data, sampling, coils, depth_inv)))


def slab_gradient(packed, coil_rows, column_inv, encodings, nhi):
    rows, _, slices, _ = coil_rows.shape

    def kernel(in_ref, coil_ref, table, out, send):
        images = [in_ref[:, i * WIDE : (i + 1) * WIDE] for i in range(encodings * rows)]
        fine = dot(stack(*images), table[...])
        coil = []
        for r in range(rows):
            real, imag = coil_ref[r, 0].astype(f32), coil_ref[r, 1].astype(f32)
            coil.append(
                (
                    real[:, :LANE],
                    imag[:, :LANE],
                    lanes(real[:, LANE:], real[:, LANE:]),
                    lanes(imag[:, LANE:], imag[:, LANE:]),
                )
            )
        even = lax.rem(lax.broadcasted_iota(jnp.int32, (8, WIDE), 0) // 2, 2) == 0
        for e in range(encodings):
            total = jnp.zeros((8, WIDE), f32)
            for r in range(rows):
                at = (e * rows + r) * slices
                a, b, d, t = (fine[at : at + slices, j * LANE : (j + 1) * LANE] for j in range(4))
                ca, cb, dr, di = coil[r]
                value = lanes(ca * a + cb * b, ca * b - cb * a, dr * d - di * t)
                value = jnp.sum(value.reshape(slices // 8, 8, WIDE), axis=0)
                turned = (-2 * r) % 8
                one = value if turned == 0 else pltpu.roll(value, turned, 0)
                two = pltpu.roll(value, (turned + 4) % 8, 0) if (turned + 4) % 8 else value
                total = total + jnp.where(even, one, two)
            for x in range(4):
                mine = pltpu.roll(total, 8 - 2 * x, 0) if x else total
                out[x, :, e * WIDE : (e + 1) * WIDE] = mine
                for h in range(nhi):
                    send[4 * h + x, :, e * WIDE : (e + 1) * WIDE] = mine[:2].astype(bf16)

    return call(
        kernel,
        10**8,
        in_specs=[VMEM, VMEM, VMEM],
        out_specs=[VMEM, VMEM],
        out_shape=[
            jax.ShapeDtypeStruct((4, 8, encodings * WIDE), f32),
            jax.ShapeDtypeStruct((slices // 2, 2, encodings * WIDE), bf16),
        ],
    )(packed, coil_rows, column_inv)


def step_length(norm_ref):
    gg, ee = (jnp.sum(norm_ref[:, i : i + 1, :], axis=0) for i in range(2))
    return gg / (ee + 4.0 * tv_weight / smoothing * gg + 1e-06)


def whole(array):
    return pl.BlockSpec(array.shape, lambda g, _n=len(array.shape): (0,) * _n)


def coil_lanes(ref, step, k):
    a, b, d = (ref[step, :, k * WIDE + j * LANE : k * WIDE + (j + 1) * LANE].astype(f32) for j in range(3))
    return (a, b, *doubled(d))


def forward_step(image, extra, sampling, own, other, tables, members, second):
    column_fwd, _, depth_fwd, depth_inv = tables
    slices, width = image.shape
    encodings = width // WIDE
    steps = own.shape[0]
    group = own.shape[2] // WIDE
    nlo = 4

    def kernel(*refs):
        refs = list(refs)
        if second:
            norms_ref, image_ref, before_ref, after_ref, normal_ref, *firsts = (refs.pop(0) for _ in range(8))
        else:
            image_ref = refs.pop(0)
        mask_ref, own_ref, other_ref, wf, zf, zi = (refs.pop(0) for _ in range(6))
        sends = [refs.pop(0) for _ in range(3)]
        norm_ref, out_ref = refs.pop(0), refs.pop(0)
        value, ahead_ref, mask_a, mask_d, product, squares, *spectra = refs
        spectrum = spectra[0] if second else out_ref
        only = lambda condition: (lambda f: f()) if second else pl.when(condition)
        hi, lo, core = (lax.axis_index(name) for name in ("hi", "lo", "enc"))

        def column(ref, e, j):
            at = e * WIDE + j * LANE
            return ref[:, at : at + LANE].astype(f32)

        @only(pl.program_id(0) == 0 if not second else True)
        def _():
            total = jnp.zeros((slices, LANE), f32)
            for e in range(encodings):
                now = [column(image_ref, e, j) for j in range(3)]
                if second:
                    alpha = step_length(norms_ref)
                    new = [-alpha * v for v in now]
                    slopes = []
                    for d in (
                        [new[j] + alpha * column(before_ref, e, j) for j in range(3)],
                        [-alpha * column(after_ref, e, j) - new[j] for j in range(3)],
                    ):
                        close = jnp.sqrt(d[0] * d[0] + d[1] * d[1] + smoothing * smoothing)
                        square = d[2] * d[2]
                        far = jnp.sqrt(square + swapped(square) + smoothing * smoothing)
                        slopes.append([d[0] / close, d[1] / close, d[2] / far])
                    now = [
                        now[j] - alpha * column(normal_ref, e, j) + tv_weight * (slopes[0][j] - slopes[1][j])
                        for j in range(3)
                    ]
                    for j in range(3):
                        at = e * WIDE + j * LANE
                        ahead_ref[:, at : at + LANE] = now[j]
                for j in range(3):
                    total = total + now[j] * now[j]
                    now[j] = now[j].astype(bf16).astype(f32)
                    value[:, e * 512 + j * LANE : e * 512 + (j + 1) * LANE] = now[j]
                value[:, e * 512 + 3 * LANE : (e + 1) * 512] = times_i(now[2])
                a, d = mask_lanes(mask_ref[e])
                mask_a[:, e * LANE : (e + 1) * LANE] = a
                mask_d[:, e * LANE : (e + 1) * LANE] = d
            norm_ref[:, 0:1, :] = jnp.full((members, 1, LANE), jnp.sum(total), f32)
            squares[...] = jnp.zeros(squares.shape, f32)

        def one_step(step, carry):
            at_step = step if second else 0
            for half, coil_ref in ((0, own_ref), (1, other_ref)):
                for k in range(group):
                    ca, cb, dr, di = coil_lanes(coil_ref, at_step, k)
                    for e in range(encodings):
                        va, vb, vd, vt = (value[:, e * 512 + j * LANE : e * 512 + (j + 1) * LANE] for j in range(4))
                        at = ((half * group + k) * encodings + e) * slices
                        product[at : at + slices, :LANE] = (ca * va - cb * vb).astype(bf16)
                        product[at : at + slices, LANE : 2 * LANE] = (ca * vb + cb * va).astype(bf16)
                        product[at : at + slices, 2 * LANE :] = (dr * vd + di * vt).astype(bf16)
            weight_a, weight_d = mask_a[...], mask_d[...]
            total = jnp.zeros(weight_a.shape, f32)
            rows = group * encodings * slices
            for half in range(2):
                u = dot(product[half * rows : (half + 1) * rows, :], wf[...]).astype(bf16)
                for k in range(group):

                    def pair(j):
                        return lanes(
                            *(
                                u[(k * encodings + e) * slices : (k * encodings + e + 1) * slices, j * LANE : (j + 1) * LANE]
                                for e in range(encodings)
                            )
                        )

                    close = dot(zf[...], stack(pair(0), pair(1)))
                    far = dot(zi[...], stack(pair(2), pair(3)))
                    sa, sb = close[:slices] * weight_a, close[slices:] * weight_a
                    sd, st = far[:slices] * weight_d, far[slices:] * weight_d
                    total = total + (sa * sa + sb * sb + sd * sd)
                    for j, x in enumerate((sa, sb, sd, st)):
                        spectrum[half * group + k, :, j * 2 * LANE : (j + 1) * 2 * LANE] = x.astype(bf16)
            squares[...] += total
            for half in range(2):
                owner = 2 * step + (core if half == 0 else 1 - core)

                @pl.when(owner == hi)
                def _():
                    for j, send_ref in enumerate(sends):
                        dest = lax.bitwise_xor(lo, j)
                        coil = (3 * dest + lax.rem(lo + dest, nlo)) // nlo
                        send_ref[:slices] = spectrum[half * group + coil, :, :width]

            return carry

        if second:
            lax.fori_loop(0, steps, one_step, 0)
        else:
            one_step(pl.program_id(0), 0)
        if second:
            piece = ahead_ref[pl.ds(pl.multiple_of(8 * hi, 8), 8), :]
            turned = [pltpu.roll(piece, 8 - 2 * dest, 0) if dest else piece for dest in range(nlo)]
            for j in range(nlo):
                dest = lax.bitwise_xor(lo, j)
                part = turned[0]
                for k in range(1, nlo):
                    part = jnp.where(dest == k, turned[k], part)
                part = stack(part, part).astype(bf16)
                if j < 3:
                    sends[j][slices : slices + 16] = part
                    sends[j][slices + 16 :] = firsts[j][...]
                else:
                    out_ref[...] = part

        @only(pl.program_id(0) == steps - 1 if not second else True)
        def _():
            norm_ref[:, 1:2, :] = jnp.full((members, 1, LANE), jnp.sum(squares[...]), f32)

    arrays = [*extra[:1], image, *extra[1:], sampling, own, other, column_fwd, depth_fwd, depth_inv]
    wide = encodings * 512
    norms = jax.ShapeDtypeStruct((members, 2, LANE), f32)
    scratch = [
        pltpu.VMEM((slices, wide), f32),
        pltpu.VMEM((slices, width), f32),
        pltpu.VMEM((slices, encodings * LANE), f32),
        pltpu.VMEM((slices, encodings * LANE), f32),
        pltpu.VMEM((2 * group * encodings * slices, WIDE), bf16),
        pltpu.VMEM((slices, encodings * LANE), f32),
    ]
    if second:
        outs = [jax.ShapeDtypeStruct((2 * slices + 16, width), bf16)] * 3
        return call(
            kernel,
            2 * 10**9,
            in_specs=[VMEM] * len(arrays),
            out_specs=[VMEM] * 5,
            out_shape=[*outs, norms, jax.ShapeDtypeStruct((16, width), bf16)],
            scratch_shapes=[*scratch, pltpu.VMEM((2 * group, slices, wide), bf16)],
        )(*(distant(a) if i > 3 and i < 8 else a for i, a in enumerate(arrays)))
    outs = [pltpu.HBM((slices, width), bf16)] * 3 + [norms]
    coil_spec = pl.BlockSpec((1,) + own.shape[1:], lambda g: (g, 0, 0))
    spectrum_spec = pl.BlockSpec((2 * group, slices, wide), lambda g: (g, 0, 0))
    return call(
        kernel,
        2 * 10**9,
        grid=(steps,),
        in_specs=[whole(image), whole(sampling), coil_spec, coil_spec, *(whole(a) for a in arrays[4:])],
        out_specs=[*(whole(o) for o in outs), spectrum_spec],
        out_shape=[*outs, pltpu.HBM((steps * 2 * group, slices, wide), bf16)],
        scratch_shapes=scratch,
    )(*arrays)


def adjoint_step(spectrum, own, other, tables, width):
    _, column_inv, depth_fwd, depth_inv = tables
    _, slices, wide = spectrum.shape
    encodings = wide // 512
    steps = own.shape[0]
    group = own.shape[2] // WIDE

    def kernel(spectrum_ref, own_ref, other_ref, wi, zf, zi, out_ref, product):
        @pl.when(pl.program_id(0) == 0)
        def _():
            out_ref[...] = jnp.zeros(out_ref.shape, f32)

        def one_step():
            for half in range(2):
                for k in range(group):
                    sa, sb, sd, st = (
                        spectrum_ref[half * group + k, :, j * 2 * LANE : (j + 1) * 2 * LANE]
                        for j in range(4)
                    )
                    close = dot(zi[...], stack(sa, sb)).astype(bf16)
                    far = dot(zf[:slices, :], stack(sd, st)).astype(bf16)
                    for e in range(encodings):
                        at = ((half * group + k) * encodings + e) * slices
                        for j, x in enumerate((close[:slices], close[slices:], far)):
                            product[at : at + slices, j * LANE : (j + 1) * LANE] = x[:, e * LANE : (e + 1) * LANE]
            rows = group * encodings * slices
            sums = [[0.0, 0.0, 0.0] for _ in range(encodings)]
            for half, coil_ref in ((0, own_ref), (1, other_ref)):
                q = dot(product[half * rows : (half + 1) * rows, :], wi[...])
                for k in range(group):
                    ca, cb, dr, di = coil_lanes(coil_ref, 0, k)
                    for e in range(encodings):
                        at = (k * encodings + e) * slices
                        qa, qb, qd, qt = (q[at : at + slices, j * LANE : (j + 1) * LANE] for j in range(4))
                        sums[e][0] += ca * qa + cb * qb
                        sums[e][1] += ca * qb - cb * qa
                        sums[e][2] += dr * qd - di * qt
            for e in range(encodings):
                for j in range(3):
                    at = e * WIDE + j * LANE
                    out_ref[:, at : at + LANE] += sums[e][j]

        one_step()

    arrays = [spectrum, own, other, column_inv, depth_fwd, depth_inv]
    coil_spec = pl.BlockSpec((1,) + own.shape[1:], lambda g: (g, 0, 0))
    spectrum_spec = pl.BlockSpec((2 * group, slices, wide), lambda g: (g, 0, 0))
    out = pltpu.HBM((slices, width), f32)
    return call(
        kernel,
        2 * 10**9,
        grid=(steps,),
        in_specs=[spectrum_spec, coil_spec, coil_spec, *(whole(a) for a in arrays[3:])],
        out_specs=whole(out),
        out_shape=out,
        scratch_shapes=[pltpu.VMEM((2 * group * encodings * slices, WIDE), bf16)],
    )(distant(spectrum), *arrays[1:])


def finish(norms_one, norms_two, data, sampling, slab_one, rows, last, readout):
    encodings, nrows, slices, lines = data.shape[1:]

    def kernel(norm_one, norm_two, data_ref, mask_ref, slab, keep, one, two, last_ref, out, image):
        lo = lax.axis_index("lo")
        alphas = step_length(norm_one), step_length(norm_two)
        for j, rows_ref in enumerate((keep, one, two)):
            r = jnp.where(lax.rem(lo, 2) == 0, j, nrows - 1 - j)
            for e in range(encodings):
                weight = mask_ref[e].astype(f32)
                real, imag = (-(data_ref[c, e, r].astype(f32) * weight) for c in range(2))
                a, b, d = (
                    alphas[0] * rows_ref[slices + 16 :, (2 * k + e) * LANE : (2 * k + e + 1) * LANE].astype(f32)
                    + alphas[1] * rows_ref[:slices, (2 * k + e) * LANE : (2 * k + e + 1) * LANE].astype(f32)
                    for k in range(3)
                )
                out[0, e, r, :, :LANE] = real[:, :LANE] - a
                out[1, e, r, :, :LANE] = imag[:, :LANE] - b
                out[0, e, r, :, LANE:] = real[:, LANE:] - d[:, :HALF]
                out[1, e, r, :, LANE:] = imag[:, LANE:] - swapped(d)[:, :HALF]
        for j in range(readout):
            x = lax.bitwise_xor(lo, j)
            for e in range(encodings):
                for k in range(3):
                    at = e * WIDE + k * LANE
                    if j < 3:
                        step = (keep, one, two)[j][slices : slices + 16, at : at + LANE]
                    else:
                        step = last_ref[:, at : at + LANE]
                    value = -alphas[0] * slab[x, :, at : at + LANE] - alphas[1] * step.astype(f32)[:8]
                    if k < 2:
                        image[k, e, x, :, :LANE] = value[:2]
                    else:
                        image[0, e, x, :, LANE:] = value[:2, :HALF]
                        image[1, e, x, :, LANE:] = swapped(value)[:2, :HALF]

    return call(
        kernel,
        10**7,
        in_specs=[VMEM] * 9,
        out_specs=[VMEM, VMEM],
        out_shape=[
            jax.ShapeDtypeStruct(data.shape, f32),
            jax.ShapeDtypeStruct((2, encodings, readout, 2, lines), f32),
        ],
    )(norms_one, norms_two, data, sampling, slab_one, *rows, last)


def reconstruct(kspace_data, coil_maps, sampling):
    encodings = kspace_data.shape[2]
    rows = kspace_data.shape[3]
    slices = kspace_data.shape[4]
    coils, readout, zdepth, lines = coil_maps.shape[1:]
    nhi, nlo = lax.axis_size("hi"), lax.axis_size("lo")
    nphase, ncore = lax.axis_size("phase"), lax.axis_size("enc")
    slabs = nhi * nlo
    group = coils // (nphase * ncore)
    assert (nlo, readout, rows, zdepth, lines, slices) == (4, 4, 3, 2, LANE + HALF, 2 * slabs)
    assert group * nhi == coils and nphase * ncore == nhi and ncore == 2
    column_fwd, column_inv = column_table(lines, -1.0), column_table(lines, 1.0)
    depth_fwd, depth_inv = depth_table(slices, -1.0), depth_table(slices, 1.0)
    tables = (column_fwd, column_inv, depth_fwd, depth_inv)
    sampling = sampling[0]
    data = kspace_data[:, 0]

    def round_ring(value):
        value = value.reshape(slabs, zdepth, -1)
        return lax.all_to_all(value, ("hi", "lo"), 0, 0, tiled=True).reshape(slices, -1)

    packed = depart(data, sampling, coil_maps, depth_inv, nhi, group)
    packed = round_ring(packed)
    coil_rows = coil_maps.reshape(2, slabs, rows, zdepth, lines).transpose(2, 0, 1, 3, 4)
    coil_rows = coil_rows.reshape(rows, 2, slices, lines)
    slab_one, spread = slab_gradient(packed, coil_rows, column_inv, encodings, nhi)
    one = round_ring(spread)
    own = lax.all_gather(packed[:, encodings * rows * WIDE :], "phase")
    other = lax.ppermute(own, "enc", [(i, (i + 1) % ncore) for i in range(ncore)])

    up = [(i, (i + 1) % nphase) for i in range(nphase)]
    before = lax.ppermute(one, "phase", up)
    after = lax.ppermute(one, "phase", [(j, i) for i, j in up])

    def total(norms):
        return lax.all_to_all(norms, ("lo", "phase", "enc"), 0, 0, tiled=True)

    members = nlo * nphase * ncore

    def swap(value, j):
        return lax.ppermute(value, "lo", [(i, i ^ j) for i in range(nlo)])

    *rows_one, norms, spectrum = forward_step(one, (), sampling, own, other, tables, members, False)
    norms_one = total(norms)
    normal = adjoint_step(spectrum, own, other, tables, one.shape[1])
    extra = (norms_one, before, after, normal, *rows_one)
    *rows_two, norms, last = forward_step(one, extra, sampling, own, other, tables, members, True)
    near = swap(rows_two[1], 1)
    far = swap(rows_two[2], 2)
    norms_two = total(norms)
    last = swap(last, 3)
    got = [rows_two[0], near, far]
    residual, image = finish(norms_one, norms_two, data, sampling, slab_one, got, last, readout)
    return (image[:, None], residual[:, None])


def solution(mesh):
    names = dict(mesh.shape)
    nlo = 4
    grid = Mesh(
        mesh.devices.reshape(names["pat"], names["slab"] // nlo, nlo, names["phase"], names["enc"]),
        ("pat", "hi", "lo", "phase", "enc"),
    )
    slab = ("hi", "lo")
    in_specs = (
        P("pat", "phase", "enc", slab, None, None),
        P("pat", None, None, slab, None),
        P("phase", "enc", "pat", None),
    )
    out_specs = (
        P("pat", "phase", "enc", None, slab, None),
        P("pat", "phase", "enc", slab, None, None),
    )
    return jax.shard_map(reconstruct, mesh=grid, in_specs=in_specs, out_specs=out_specs, check_vma=False)
```

time: 217 us -> 197 us (0.908)
  local copies, waits for them, and re-layouts: 10.1 us -> 1.51 us
  Pallas kernels: 28 us -> 21.7 us
  waiting for transfers between devices: 76.2 us -> 71.1 us
    pallas_call x5 -> x6, Pallas kernels: 28 us -> 21.7 us  [the longest x1 6.34 us: forward_step(): call(kernel, 2 * 10 ** 9, in_specs=[VMEM] * len(arrays), out_specs=[VMEM]...]
    reshape x5 -> x2, local copies, waits for them, and re-layouts: 6.3 us -> 1.25 us  [the longest x1 1.07 us: reconstruct(): coil_maps.reshape(2, slabs, rows, zdepth, lines).transpose(2, 0, 1, 3, 4)]
    ppermute x3, waiting for transfers between devices: 4.63 us -> 0.01 us  [the longest x1 0.01 us: reconstruct(): lax.ppermute(own, 'enc', [(i, (i + 1) % ncore) for i in range(ncore)])]
    unnamed x26 -> x12, local copies, waits for them, and re-layouts: 2.97 us -> 0.04 us
  transfers between devices with their start and end apart: 10 -> 10, of which waited for: 5 -> 4; matrix products, arithmetic and copies ran while one was open for 1% -> 1% of each run, Pallas kernels for 0% -> 3%
where the time goes in v3:
time: 197 us; the launch traced here: 196 us
  starting transfers between devices  88.9 us (45%)
  waiting for transfers between devices  71.1 us (36%)
  Pallas kernels  21.7 us (11%)
  blocking collectives  11.9 us (6%)
    all_to_all x2, waiting for transfers between devices, round_ring(): lax.all_to_all(value, ('hi', 'lo'), 0, 0, tiled=True).reshape(slices, -1)  62.8 us
    all_to_all x2, starting transfers between devices, round_ring(): lax.all_to_all(value, ('hi', 'lo'), 0, 0, tiled=True).reshape(slices, -1)  51.1 us
    all_to_all x2, starting transfers between devices, total(): return lax.all_to_all(norms, ('lo', 'phase', 'enc'), 0, 0, tiled=True)  16.3 us
    all_gather x1, blocking collectives, reconstruct(): own = lax.all_gather(packed[:, encodings * rows * WIDE:], 'phase')  11.9 us
    ppermute x3, starting transfers between devices, swap(): return lax.ppermute(value, 'lo', [(i, i ^ j) for i in range(nlo)])  9.4 us
    ppermute x3, waiting for transfers between devices, swap(): return lax.ppermute(value, 'lo', [(i, i ^ j) for i in range(nlo)])  8.37 us
    pallas_call x1, Pallas kernels, forward_step(): call(kernel, 2 * 10 ** 9, in_specs=[VMEM] * len(arrays), out_specs=[VMEM]...  6.34 us
    ppermute x1, starting transfers between devices, reconstruct(): lax.ppermute(own, 'enc', [(i, (i + 1) % ncore) for i in range(ncore)])  5.54 us
  transfers between devices with their start and end apart: 10, of which 4 were waited for; matrix products, arithmetic and copies ran while one was open for 1% of the time, Pallas kernels for 3%

profile of v3, /device:TPU:33, one launch (start us, length us, event | category | flops | bytes accessed | tf_op | source)
XLA Modules:
  0.0 196.0 jit_solution(5267253511414646170)
XLA Ops:
  0.6 0.0 copy-start.3
  0.6 0.0 copy-start.2
  0.7 0.0 copy-start.5
  0.7 0.0 copy-start.4
  0.7 2.4 %shard_map.86 = bf16[32,2,3456]{2,1,0:T(2,128)(2,1)} custom-call(bf16[2,2,3,64,192]{4,3,2,1,0:T(8,128)(2,1)} %bitcast.13, s32[2,64,192]{2,1,0:T(8,128)} %bitcast.19, bf16[2,24,4,2,192]{4,3,2,1,0:T(2,128)(2,1)} %coil_ref.1, bf16[128,128]{1,0:T(8,128)(2,1)} %constant.11.clone.table.refs_6_.zi.refs_13_), custom_call_target="tpu_custom_call" | custom-call | flops 100000000 | bytes 1048576 | tf_op jit(solution)/shard_map/pallas_call | solution.py:137
  3.0 46.3 %all-to-all-start = ((bf16[32,2,3456]{2,1,0:T(2,128)(2,1)}), bf16[32,2,3456]{2,1,0:T(2,128)(2,1)S(1)}, u32[]{:S(2)}, u32[]{:S(2)}) async-start(bf16[32,2,3456]{2,1,0:T(2,128)(2,1)} %shard_map.86), calls=%async_computation | async-start | bytes 884736 | tf_op jit(solution)/shard_map/all_to_all | solution.py:499
  49.4 1.1 copy.13
  50.4 0.2 reshape.18.coil_ref
  50.6 55.3 %all-to-all-done = bf16[32,2,3456]{2,1,0:T(2,128)(2,1)S(1)} async-done(((bf16[32,2,3456]{2,1,0:T(2,128)(2,1)}), bf16[32,2,3456]{2,1,0:T(2,128)(2,1)S(1)}, u32[]{:S(2)}, u32[]{:S(2)}) %all-to-all-start) | async-done | bytes 442400 | tf_op jit(solution)/shard_map/all_to_all | solution.py:499
  105.9 0.2 reshape.16.in_ref
  106.1 1.1 shard_map.87
  107.1 4.8 %all-to-all-start.1 = ((bf16[32,2,768]{2,1,0:T(2,128)(2,1)}), bf16[32,2,768]{2,1,0:T(2,128)(2,1)S(1)}, u32[]{:S(2)}, u32[]{:S(2)}) async-start(bf16[32,2,768]{2,1,0:T(2,128)(2,1)} %get-tuple-element.16), calls=%async_computation.1 | async-start | bytes 196608 | tf_op jit(solution)/shard_map/all_to_all | solution.py:499
  111.9 11.9 %all-gather = bf16[256,1152]{1,0:T(8,128)(2,1)S(1)} all-gather(bf16[64,1152]{1,0:T(8,128)(2,1)S(1)} %slice.4), channel_id=2, replica_groups=mesh['pat'=2,'hi'=8,'lo'=4,'phase'=4,'enc'=2] {'phase'}, dimensions={0}, use_global_device_ids=true | all-gather | bytes 737280 | tf_op jit(solution)/shard_map/all_gather | solution.py:507
  123.9 5.5 %collective-permute-start = (bf16[4,64,1152]{2,1,0:T(8,128)(2,1)S(1)}, bf16[4,64,1152]{2,1,0:T(8,128)(2,1)S(1)}, u32[]{:S(2)}, u32[]{:S(2)}) collective-permute-start(bf16[4,64,1152]{2,1,0:T(8,128)(2,1)S(1)} %bitcast.15), channel_id=1, source_target_pairs={{0,1},{1,0},{2,3},{3,2},{4,5},{5,4},{6,7},{7,6},{8,9},{9,8},{10,11... | collective-permute-start | bytes 1769480 | tf_op jit(solution)/shard_map/ppermute | solution.py:508
  129.4 7.5 %all-to-all-done.1 = bf16[32,2,768]{2,1,0:T(2,128)(2,1)S(1)} async-done(((bf16[32,2,768]{2,1,0:T(2,128)(2,1)}), bf16[32,2,768]{2,1,0:T(2,128)(2,1)S(1)}, u32[]{:S(2)}, u32[]{:S(2)}) %all-to-all-start.1) | async-done | bytes 98336 | tf_op jit(solution)/shard_map/all_to_all | solution.py:499
  137.0 0.0 collective-permute-done.refs_3_.other_ref.refs_10_
  137.0 5.5 %shard_map.88 = (bf16[64,768]{1,0:T(8,128)(2,1)}, bf16[64,768]{1,0:T(8,128)(2,1)}, bf16[64,768]{1,0:T(8,128)(2,1)}, f32[32,2,128]{2,1,0:T(2,128)}, bf16[24,64,1024]{2,1,0:T(8,128)(2,1)}) custom-call(bf16[64,768]{1,0:T(8,128)(2,1)S(1)} %reshape.19.refs_0_.refs_1_, s32[2,64,192]{2,1,0:T(8,128)S(1)} %bitcast.20, bf16[4,64,1152]{2,1,0:T(8,128)(2,1)S(1)} %bitcast.16, ...), custom_call_target="tpu_custom_call" | custom-call | flops 2000000000 | bytes 1048576 | tf_op jit(solution)/shard_map/pallas_call | solution.py:362
  142.5 8.9 %all-to-all-start.2 = ((f32[32,2,128]{2,1,0:T(2,128)}), f32[32,2,128]{2,1,0:T(2,128)S(1)}, u32[]{:S(2)}, u32[]{:S(2)}) async-start(f32[32,2,128]{2,1,0:T(2,128)} %get-tuple-element.17), calls=%async_computation.2 | async-start | bytes 65536 | tf_op jit(solution)/shard_map/all_to_all | solution.py:515
  151.4 3.3 %collective-permute-start.1 = (bf16[64,768]{1,0:T(8,128)(2,1)S(1)}, bf16[64,768]{1,0:T(8,128)(2,1)S(1)}, u32[]{:S(2)}, u32[]{:S(2)}) collective-permute-start(bf16[64,768]{1,0:T(8,128)(2,1)S(1)} %reshape.19.refs_0_.refs_1_), channel_id=1, source_target_pairs={{0,2},{2,4},{4,6},{6,0},{1,3},{3,5},{5,7},{7,1},{8,10},{10,12},{12... | collective-permute-start | bytes 294920 | tf_op jit(solution)/shard_map/ppermute | solution.py:511
  154.7 3.3 %collective-permute-start.2 = (bf16[64,768]{1,0:T(8,128)(2,1)S(1)}, bf16[64,768]{1,0:T(8,128)(2,1)S(1)}, u32[]{:S(2)}, u32[]{:S(2)}) collective-permute-start(bf16[64,768]{1,0:T(8,128)(2,1)S(1)} %reshape.19.refs_0_.refs_1_), channel_id=1, source_target_pairs={{2,0},{4,2},{6,4},{0,6},{3,1},{5,3},{7,5},{1,7},{10,8},{12,10},{14... | collective-permute-start | bytes 294920 | tf_op jit(solution)/shard_map/ppermute | solution.py:512
  157.9 5.3 %shard_map.89.refs_4_ = f32[64,768]{1,0:T(8,128)} custom-call(bf16[24,64,1024]{2,1,0:T(8,128)(2,1)} %get-tuple-element.18.spectrum_ref, bf16[4,64,1152]{2,1,0:T(8,128)(2,1)S(1)} %bitcast.17, bf16[4,64,1152]{2,1,0:T(8,128)(2,1)S(1)} %collective-permute-done.refs_3_.other_ref.refs_10_, bf16[384,512]{1,0:T(8,128)(2,1)S(1)} %copy-done.2, ...), custom_call_target="tpu_custom_call" | custom-call | flops 2000000000 | bytes 1048576 | tf_op jit(solution)/shard_map/pallas_call | solution.py:421
  163.2 0.0 collective-permute-done.1.refs_2_
  163.2 0.0 collective-permute-done.2.refs_3_
  163.2 0.0 copy-start
  163.2 6.3 %shard_map.90 = (bf16[144,768]{1,0:T(8,128)(2,1)S(1)}, bf16[144,768]{1,0:T(8,128)(2,1)S(1)}, bf16[144,768]{1,0:T(8,128)(2,1)S(1)}, f32[32,2,128]{2,1,0:T(2,128)}, bf16[16,768]{1,0:T(8,128)(2,1)S(1)}) custom-call(f32[32,2,128]{2,1,0:T(2,128)S(1)} %all-to-all-done.2.refs_0_.norm_one, bf16[64,768]{1,0:T(8,128)(2,1)S(1)} %reshape.19.refs_0_.refs_1_, ...), custom_call_target="tpu_custom_call" | custom-call | flops 2000000000 | bytes 1048576 | tf_op jit(solution)/shard_map/pallas_call | solution.py:351
  169.6 7.4 %all-to-all-start.3 = ((f32[32,2,128]{2,1,0:T(2,128)}), f32[32,2,128]{2,1,0:T(2,128)S(1)}, u32[]{:S(2)}, u32[]{:S(2)}) async-start(f32[32,2,128]{2,1,0:T(2,128)} %get-tuple-element.22), calls=%async_computation.3 | async-start | bytes 65536 | tf_op jit(solution)/shard_map/all_to_all | solution.py:515
  177.0 3.3 %collective-permute-start.3 = (bf16[144,768]{1,0:T(8,128)(2,1)S(1)}, bf16[144,768]{1,0:T(8,128)(2,1)S(1)}, u32[]{:S(2)}, u32[]{:S(2)}) collective-permute-start(bf16[144,768]{1,0:T(8,128)(2,1)S(1)} %get-tuple-element.25), channel_id=1, source_target_pairs={{0,8},{8,0},{16,24},{24,16},{1,9},{9,1},{17,25},{25,17},{2,10},{10... | collective-permute-start | bytes 663560 | tf_op jit(solution)/shard_map/ppermute | solution.py:520
  180.3 4.2 %collective-permute-start.4 = (bf16[144,768]{1,0:T(8,128)(2,1)S(1)}, bf16[144,768]{1,0:T(8,128)(2,1)S(1)}, u32[]{:S(2)}, u32[]{:S(2)}) collective-permute-start(bf16[144,768]{1,0:T(8,128)(2,1)S(1)} %get-tuple-element.26), channel_id=1, source_target_pairs={{0,16},{8,24},{16,0},{24,8},{1,17},{9,25},{17,1},{25,9},{2,18},{10... | collective-permute-start | bytes 663560 | tf_op jit(solution)/shard_map/ppermute | solution.py:520
  184.5 2.0 collective-permute-start.5
  186.4 6.1 %collective-permute-done.5.last_ref = bf16[16,768]{1,0:T(8,128)(2,1)S(1)} collective-permute-done((bf16[16,768]{1,0:T(8,128)(2,1)S(1)}, bf16[16,768]{1,0:T(8,128)(2,1)S(1)}, u32[]{:S(2)}, u32[]{:S(2)}) %collective-permute-start.5) | collective-permute-done | bytes 24608 | tf_op jit(solution)/shard_map/ppermute | solution.py:520
  192.6 2.2 %collective-permute-done.4.two = bf16[144,768]{1,0:T(8,128)(2,1)S(1)} collective-permute-done((bf16[144,768]{1,0:T(8,128)(2,1)S(1)}, bf16[144,768]{1,0:T(8,128)(2,1)S(1)}, u32[]{:S(2)}, u32[]{:S(2)}) %collective-permute-start.4) | collective-permute-done | bytes 221216 | tf_op jit(solution)/shard_map/ppermute | solution.py:520
  194.8 1.2 shard_map.91
  (12 shorter events, 0.1 us)
Async XLA Ops:
  0.6 136.3 %copy-start.3 = (bf16[128,128]{1,0:T(8,128)(2,1)S(1)}, bf16[128,128]{1,0:T(8,128)(2,1)}, u32[]{:S(2)}) copy-start(bf16[128,128]{1,0:T(8,128)(2,1)} %constant.11.clone.table.refs_6_.zi.refs_13_) | copy-start | bytes 98308
  0.6 105.4 %copy-start.2 = (bf16[384,512]{1,0:T(8,128)(2,1)S(1)}, bf16[384,512]{1,0:T(8,128)(2,1)}, u32[]{:S(2)}) copy-start(bf16[384,512]{1,0:T(8,128)(2,1)} %constant.9.clone.table.wi) | copy-start | bytes 1179652
  0.7 136.3 %copy-start.5 = (bf16[128,128]{1,0:T(8,128)(2,1)S(1)}, bf16[128,128]{1,0:T(8,128)(2,1)}, u32[]{:S(2)}) copy-start(bf16[128,128]{1,0:T(8,128)(2,1)} %constant.10.clone.refs_5_.zf.refs_12_) | copy-start | bytes 98308
  0.7 136.3 %copy-start.4 = (bf16[384,512]{1,0:T(8,128)(2,1)S(1)}, bf16[384,512]{1,0:T(8,128)(2,1)}, u32[]{:S(2)}) copy-start(bf16[384,512]{1,0:T(8,128)(2,1)} %constant.8.clone.refs_4_.refs_11_) | copy-start | bytes 1179652
  0.7 136.3 %copy-start.1 = (s32[1,2,64,192]{3,2,1,0:T(8,128)S(1)}, s32[1,2,64,192]{3,2,1,0:T(8,128)}, u32[]{:S(2)}) copy-start(s32[1,2,64,192]{3,2,1,0:T(8,128)} %param.9) | copy-start | bytes 294916
  3.0 102.8 %all-to-all-start = ((bf16[32,2,3456]{2,1,0:T(2,128)(2,1)}), bf16[32,2,3456]{2,1,0:T(2,128)(2,1)S(1)}, u32[]{:S(2)}, u32[]{:S(2)}) async-start(bf16[32,2,3456]{2,1,0:T(2,128)(2,1)} %shard_map.86), calls=%async_computation | async-start | bytes 884736 | tf_op jit(solution)/shard_map/all_to_all | solution.py:499
  107.1 29.8 %all-to-all-start.1 = ((bf16[32,2,768]{2,1,0:T(2,128)(2,1)}), bf16[32,2,768]{2,1,0:T(2,128)(2,1)S(1)}, u32[]{:S(2)}, u32[]{:S(2)}) async-start(bf16[32,2,768]{2,1,0:T(2,128)(2,1)} %get-tuple-element.16), calls=%async_computation.1 | async-start | bytes 196608 | tf_op jit(solution)/shard_map/all_to_all | solution.py:499
  123.9 13.1 %collective-permute-start = (bf16[4,64,1152]{2,1,0:T(8,128)(2,1)S(1)}, bf16[4,64,1152]{2,1,0:T(8,128)(2,1)S(1)}, u32[]{:S(2)}, u32[]{:S(2)}) collective-permute-start(bf16[4,64,1152]{2,1,0:T(8,128)(2,1)S(1)} %bitcast.15), channel_id=1, source_target_pairs={{0,1},{1,0},{2,3},{3,2},{4,5},{5,4},{6,7},{7,6},{8,9},{9,8},{10,11... | collective-permute-start | bytes 1769480 | tf_op jit(solution)/shard_map/ppermute | solution.py:508
  142.5 20.7 %all-to-all-start.2 = ((f32[32,2,128]{2,1,0:T(2,128)}), f32[32,2,128]{2,1,0:T(2,128)S(1)}, u32[]{:S(2)}, u32[]{:S(2)}) async-start(f32[32,2,128]{2,1,0:T(2,128)} %get-tuple-element.17), calls=%async_computation.2 | async-start | bytes 65536 | tf_op jit(solution)/shard_map/all_to_all | solution.py:515
  151.4 11.8 %collective-permute-start.1 = (bf16[64,768]{1,0:T(8,128)(2,1)S(1)}, bf16[64,768]{1,0:T(8,128)(2,1)S(1)}, u32[]{:S(2)}, u32[]{:S(2)}) collective-permute-start(bf16[64,768]{1,0:T(8,128)(2,1)S(1)} %reshape.19.refs_0_.refs_1_), channel_id=1, source_target_pairs={{0,2},{2,4},{4,6},{6,0},{1,3},{3,5},{5,7},{7,1},{8,10},{10,12},{12... | collective-permute-start | bytes 294920 | tf_op jit(solution)/shard_map/ppermute | solution.py:511
  154.7 8.5 %collective-permute-start.2 = (bf16[64,768]{1,0:T(8,128)(2,1)S(1)}, bf16[64,768]{1,0:T(8,128)(2,1)S(1)}, u32[]{:S(2)}, u32[]{:S(2)}) collective-permute-start(bf16[64,768]{1,0:T(8,128)(2,1)S(1)} %reshape.19.refs_0_.refs_1_), channel_id=1, source_target_pairs={{2,0},{4,2},{6,4},{0,6},{3,1},{5,3},{7,5},{1,7},{10,8},{12,10},{14... | collective-permute-start | bytes 294920 | tf_op jit(solution)/shard_map/ppermute | solution.py:512
  163.2 31.6 %copy-start = (bf16[2,1,2,3,64,192]{5,4,3,2,1,0:T(8,128)(2,1)S(1)}, bf16[2,1,2,3,64,192]{5,4,3,2,1,0:T(8,128)(2,1)}, u32[]{:S(2)}) copy-start(bf16[2,1,2,3,64,192]{5,4,3,2,1,0:T(8,128)(2,1)} %param.7) | copy-start | bytes 884740
  169.6 25.2 %all-to-all-start.3 = ((f32[32,2,128]{2,1,0:T(2,128)}), f32[32,2,128]{2,1,0:T(2,128)S(1)}, u32[]{:S(2)}, u32[]{:S(2)}) async-start(f32[32,2,128]{2,1,0:T(2,128)} %get-tuple-element.22), calls=%async_computation.3 | async-start | bytes 65536 | tf_op jit(solution)/shard_map/all_to_all | solution.py:515
  177.0 15.6 %collective-permute-start.3 = (bf16[144,768]{1,0:T(8,128)(2,1)S(1)}, bf16[144,768]{1,0:T(8,128)(2,1)S(1)}, u32[]{:S(2)}, u32[]{:S(2)}) collective-permute-start(bf16[144,768]{1,0:T(8,128)(2,1)S(1)} %get-tuple-element.25), channel_id=1, source_target_pairs={{0,8},{8,0},{16,24},{24,16},{1,9},{9,1},{17,25},{25,17},{2,10},{10... | collective-permute-start | bytes 663560 | tf_op jit(solution)/shard_map/ppermute | solution.py:520
  180.3 14.5 %collective-permute-start.4 = (bf16[144,768]{1,0:T(8,128)(2,1)S(1)}, bf16[144,768]{1,0:T(8,128)(2,1)S(1)}, u32[]{:S(2)}, u32[]{:S(2)}) collective-permute-start(bf16[144,768]{1,0:T(8,128)(2,1)S(1)} %get-tuple-element.26), channel_id=1, source_target_pairs={{0,16},{8,24},{16,0},{24,8},{1,17},{9,25},{17,1},{25,9},{2,18},{10... | collective-permute-start | bytes 663560 | tf_op jit(solution)/shard_map/ppermute | solution.py:520
  184.5 8.1 %collective-permute-start.5 = (bf16[16,768]{1,0:T(8,128)(2,1)S(1)}, bf16[16,768]{1,0:T(8,128)(2,1)S(1)}, u32[]{:S(2)}, u32[]{:S(2)}) collective-permute-start(bf16[16,768]{1,0:T(8,128)(2,1)S(1)} %get-tuple-element.27), channel_id=1, source_target_pairs={{0,24},{8,16},{16,8},{24,0},{1,25},{9,17},{17,9},{25,1},{2,26},{10... | collective-permute-start | bytes 73736 | tf_op jit(solution)/shard_map/ppermute | solution.py:520

commit v4 on v3

--- a/solution.py
+++ b/solution.py
@@ -224,6 +224,15 @@
         norm_ref, out_ref = refs.pop(0), refs.pop(0)
         value, ahead_ref, mask_a, mask_d, product, squares, *spectra = refs
         spectrum = spectra[0] if second else out_ref
+        copies = []
+        if second:
+            for j in range(3):
+                copies.append(
+                    pltpu.make_async_copy(firsts[j], sends[j].at[pl.ds(slices + 16, slices)], spectra[1].at[j])
+                )
+            copies.append(pltpu.make_async_copy(normal_ref, spectra[2], spectra[1].at[3]))
+            for copy in reversed(copies):
+                copy.start()
         only = lambda condition: (lambda f: f()) if second else pl.when(condition)
         hi, lo, core = (lax.axis_index(name) for name in ("hi", "lo", "enc"))
 
@@ -248,10 +257,16 @@
                         square = d[2] * d[2]
                         far = jnp.sqrt(square + swapped(square) + smoothing * smoothing)
                         slopes.append([d[0] / close, d[1] / close, d[2] / far])
-                    now = [
-                        now[j] - alpha * column(normal_ref, e, j) + tv_weight * (slopes[0][j] - slopes[1][j])
-                        for j in range(3)
-                    ]
+                    now = [now[j] + tv_weight * (slopes[0][j] - slopes[1][j]) for j in range(3)]
+                    for j in range(3):
+                        at = e * WIDE + j * LANE
+                        ahead_ref[:, at : at + LANE] = now[j]
+            if second:
+                copies[3].wait()
+            for e in range(encodings):
+                now = [column(image_ref, e, j) for j in range(3)]
+                if second:
+                    now = [column(ahead_ref, e, j) - alpha * column(spectra[2], e, j) for j in range(3)]
                     for j in range(3):
                         at = e * WIDE + j * LANE
                         ahead_ref[:, at : at + LANE] = now[j]
@@ -279,26 +294,26 @@
                         product[at : at + slices, 2 * LANE :] = (dr * vd + di * vt).astype(bf16)
             weight_a, weight_d = mask_a[...], mask_d[...]
             total = jnp.zeros(weight_a.shape, f32)
-            rows = group * encodings * slices
-            for half in range(2):
-                u = dot(product[half * rows : (half + 1) * rows, :], wf[...]).astype(bf16)
-                for k in range(group):
-
-                    def pair(j):
-                        return lanes(
-                            *(
-                                u[(k * encodings + e) * slices : (k * encodings + e + 1) * slices, j * LANE : (j + 1) * LANE]
-                                for e in range(encodings)
-                            )
+            u = dot(product[...], wf[...]).astype(bf16)
+            for k in range(2 * group):
+
+                def pair(j):
+                    return lanes(
+                        *(
+                            u[(k * encodings + e) * slices : (k * encodings + e + 1) * slices, j * LANE : (j + 1) * LANE]
+                            for e in range(encodings)
                         )
-
-                    close = dot(zf[...], stack(pair(0), pair(1)))
-                    far = dot(zi[...], stack(pair(2), pair(3)))
-                    sa, sb = close[:slices] * weight_a, close[slices:] * weight_a
-                    sd, st = far[:slices] * weight_d, far[slices:] * weight_d
-                    total = total + (sa * sa + sb * sb + sd * sd)
-                    for j, x in enumerate((sa, sb, sd, st)):
-                        spectrum[half * group + k, :, j * 2 * LANE : (j + 1) * 2 * LANE] = x.astype(bf16)
+                    )
+
+                close = dot(zf[...], stack(pair(0), pair(1)))
+                sd = dot(zi[:slices, :], stack(pair(2), pair(3))) * weight_d
+                sa, sb = close[:slices] * weight_a, close[slices:] * weight_a
+                total = total + (sa * sa + sb * sb + sd * sd)
+                parts = [sa, sb, sd]
+                if not second:
+                    parts.append(lanes(*(times_i(sd[:, e * LANE : (e + 1) * LANE]) for e in range(encodings))))
+                for j, x in enumerate(parts):
+                    spectrum[k, :, j * 2 * LANE : (j + 1) * 2 * LANE] = x.astype(bf16)
             squares[...] += total
             for half in range(2):
                 owner = 2 * step + (core if half == 0 else 1 - core)
@@ -327,7 +342,7 @@
                 part = stack(part, part).astype(bf16)
                 if j < 3:
                     sends[j][slices : slices + 16] = part
-                    sends[j][slices + 16 :] = firsts[j][...]
+                    copies[j].wait()
                 else:
                     out_ref[...] = part
 
@@ -351,10 +366,10 @@
         return call(
             kernel,
             2 * 10**9,
-            in_specs=[VMEM] * len(arrays),
+            in_specs=[VMEM] * 4 + [pl.BlockSpec(memory_space=pl.ANY)] * 4 + [VMEM] * (len(arrays) - 8),
             out_specs=[VMEM] * 5,
             out_shape=[*outs, norms, jax.ShapeDtypeStruct((16, width), bf16)],
-            scratch_shapes=[*scratch, pltpu.VMEM((2 * group, slices, wide), bf16)],
+            scratch_shapes=[*scratch, pltpu.VMEM((2 * group, slices, width), bf16), pltpu.SemaphoreType.DMA((4,)), pltpu.VMEM((slices, width), f32)],
         )(*(distant(a) if i > 3 and i < 8 else a for i, a in enumerate(arrays)))
     outs = [pltpu.HBM((slices, width), bf16)] * 3 + [norms]
     coil_spec = pl.BlockSpec((1,) + own.shape[1:], lambda g: (g, 0, 0))
@@ -395,14 +410,13 @@
                         at = ((half * group + k) * encodings + e) * slices
                         for j, x in enumerate((close[:slices], close[slices:], far)):
                             product[at : at + slices, j * LANE : (j + 1) * LANE] = x[:, e * LANE : (e + 1) * LANE]
-            rows = group * encodings * slices
+            q = dot(product[...], wi[...])
             sums = [[0.0, 0.0, 0.0] for _ in range(encodings)]
             for half, coil_ref in ((0, own_ref), (1, other_ref)):
-                q = dot(product[half * rows : (half + 1) * rows, :], wi[...])
                 for k in range(group):
                     ca, cb, dr, di = coil_lanes(coil_ref, 0, k)
                     for e in range(encodings):
-                        at = (k * encodings + e) * slices
+                        at = ((half * group + k) * encodings + e) * slices
                         qa, qb, qd, qt = (q[at : at + slices, j * LANE : (j + 1) * LANE] for j in range(4))
                         sums[e][0] += ca * qa + cb * qb
                         sums[e][1] += ca * qb - cb * qa

time: 197 us -> 195 us (0.990)
  no operation moved by 1% of the time
where the time goes in v4:
time: 195 us; the launch traced here: 194 us
  starting transfers between devices  88.9 us (46%)
  waiting for transfers between devices  71.1 us (36%)
  Pallas kernels  19.8 us (10%)
  blocking collectives  11.9 us (6%)
    all_to_all x2, waiting for transfers between devices, round_ring(): lax.all_to_all(value, ('hi', 'lo'), 0, 0, tiled=True).reshape(slices, -1)  62.8 us
    all_to_all x2, starting transfers between devices, round_ring(): lax.all_to_all(value, ('hi', 'lo'), 0, 0, tiled=True).reshape(slices, -1)  51.1 us
    all_to_all x2, starting transfers between devices, total(): return lax.all_to_all(norms, ('lo', 'phase', 'enc'), 0, 0, tiled=True)  16.3 us
    all_gather x1, blocking collectives, reconstruct(): own = lax.all_gather(packed[:, encodings * rows * WIDE:], 'phase')  11.9 us
    ppermute x3, starting transfers between devices, swap(): return lax.ppermute(value, 'lo', [(i, i ^ j) for i in range(nlo)])  9.4 us
    ppermute x3, waiting for transfers between devices, swap(): return lax.ppermute(value, 'lo', [(i, i ^ j) for i in range(nlo)])  8.37 us
    ppermute x1, starting transfers between devices, reconstruct(): lax.ppermute(own, 'enc', [(i, (i + 1) % ncore) for i in range(ncore)])  5.54 us
    pallas_call x1, Pallas kernels, adjoint_step(): call(kernel, 2 * 10 ** 9, grid=(steps,), in_specs=[spectrum_spec, coil_sp...  5.26 us
  transfers between devices with their start and end apart: 10, of which 4 were waited for; matrix products, arithmetic and copies ran while one was open for 1% of the time, Pallas kernels for 3%

profile of v4, /device:TPU:33, one launch (start us, length us, event | category | flops | bytes accessed | tf_op | source)
XLA Modules:
  0.0 194.1 jit_solution(15702099239281380007)
XLA Ops:
  0.6 0.0 copy-start.3
  0.6 0.0 copy-start.2
  0.7 0.0 copy-start.5
  0.7 0.0 copy-start.4
  0.7 2.4 %shard_map.86 = bf16[32,2,3456]{2,1,0:T(2,128)(2,1)} custom-call(bf16[2,2,3,64,192]{4,3,2,1,0:T(8,128)(2,1)} %bitcast.13, s32[2,64,192]{2,1,0:T(8,128)} %bitcast.19, bf16[2,24,4,2,192]{4,3,2,1,0:T(2,128)(2,1)} %coil_ref.1, bf16[128,128]{1,0:T(8,128)(2,1)} %constant.11.clone.table.refs_6_.zi.refs_13_), custom_call_target="tpu_custom_call" | custom-call | flops 100000000 | bytes 1048576 | tf_op jit(solution)/shard_map/pallas_call | solution.py:137
  3.0 46.3 %all-to-all-start = ((bf16[32,2,3456]{2,1,0:T(2,128)(2,1)}), bf16[32,2,3456]{2,1,0:T(2,128)(2,1)S(1)}, u32[]{:S(2)}, u32[]{:S(2)}) async-start(bf16[32,2,3456]{2,1,0:T(2,128)(2,1)} %shard_map.86), calls=%async_computation | async-start | bytes 884736 | tf_op jit(solution)/shard_map/all_to_all | solution.py:513
  49.4 1.1 copy.13
  50.4 0.2 reshape.18.coil_ref
  50.6 55.3 %all-to-all-done = bf16[32,2,3456]{2,1,0:T(2,128)(2,1)S(1)} async-done(((bf16[32,2,3456]{2,1,0:T(2,128)(2,1)}), bf16[32,2,3456]{2,1,0:T(2,128)(2,1)S(1)}, u32[]{:S(2)}, u32[]{:S(2)}) %all-to-all-start) | async-done | bytes 442400 | tf_op jit(solution)/shard_map/all_to_all | solution.py:513
  105.9 0.2 reshape.16.in_ref
  106.1 1.1 shard_map.87
  107.1 4.8 %all-to-all-start.1 = ((bf16[32,2,768]{2,1,0:T(2,128)(2,1)}), bf16[32,2,768]{2,1,0:T(2,128)(2,1)S(1)}, u32[]{:S(2)}, u32[]{:S(2)}) async-start(bf16[32,2,768]{2,1,0:T(2,128)(2,1)} %get-tuple-element.16), calls=%async_computation.1 | async-start | bytes 196608 | tf_op jit(solution)/shard_map/all_to_all | solution.py:513
  111.9 11.9 %all-gather = bf16[256,1152]{1,0:T(8,128)(2,1)S(1)} all-gather(bf16[64,1152]{1,0:T(8,128)(2,1)S(1)} %slice.4), channel_id=2, replica_groups=mesh['pat'=2,'hi'=8,'lo'=4,'phase'=4,'enc'=2] {'phase'}, dimensions={0}, use_global_device_ids=true | all-gather | bytes 737280 | tf_op jit(solution)/shard_map/all_gather | solution.py:521
  123.9 5.5 %collective-permute-start = (bf16[4,64,1152]{2,1,0:T(8,128)(2,1)S(1)}, bf16[4,64,1152]{2,1,0:T(8,128)(2,1)S(1)}, u32[]{:S(2)}, u32[]{:S(2)}) collective-permute-start(bf16[4,64,1152]{2,1,0:T(8,128)(2,1)S(1)} %bitcast.15), channel_id=1, source_target_pairs={{0,1},{1,0},{2,3},{3,2},{4,5},{5,4},{6,7},{7,6},{8,9},{9,8},{10,11... | collective-permute-start | bytes 1769480 | tf_op jit(solution)/shard_map/ppermute | solution.py:522
  129.4 7.5 %all-to-all-done.1 = bf16[32,2,768]{2,1,0:T(2,128)(2,1)S(1)} async-done(((bf16[32,2,768]{2,1,0:T(2,128)(2,1)}), bf16[32,2,768]{2,1,0:T(2,128)(2,1)S(1)}, u32[]{:S(2)}, u32[]{:S(2)}) %all-to-all-start.1) | async-done | bytes 98336 | tf_op jit(solution)/shard_map/all_to_all | solution.py:513
  137.0 0.0 collective-permute-done.refs_3_.other_ref.refs_10_
  137.0 4.9 %shard_map.88 = (bf16[64,768]{1,0:T(8,128)(2,1)}, bf16[64,768]{1,0:T(8,128)(2,1)}, bf16[64,768]{1,0:T(8,128)(2,1)}, f32[32,2,128]{2,1,0:T(2,128)}, bf16[24,64,1024]{2,1,0:T(8,128)(2,1)}) custom-call(bf16[64,768]{1,0:T(8,128)(2,1)S(1)} %reshape.19.refs_0_.refs_1_, s32[2,64,192]{2,1,0:T(8,128)S(1)} %bitcast.20, bf16[4,64,1152]{2,1,0:T(8,128)(2,1)S(1)} %bitcast.16, ...), custom_call_target="tpu_custom_call" | custom-call | flops 2000000000 | bytes 1048576 | tf_op jit(solution)/shard_map/pallas_call | solution.py:377
  141.9 8.9 %all-to-all-start.2 = ((f32[32,2,128]{2,1,0:T(2,128)}), f32[32,2,128]{2,1,0:T(2,128)S(1)}, u32[]{:S(2)}, u32[]{:S(2)}) async-start(f32[32,2,128]{2,1,0:T(2,128)} %get-tuple-element.17), calls=%async_computation.2 | async-start | bytes 65536 | tf_op jit(solution)/shard_map/all_to_all | solution.py:529
  150.7 3.3 %collective-permute-start.1 = (bf16[64,768]{1,0:T(8,128)(2,1)S(1)}, bf16[64,768]{1,0:T(8,128)(2,1)S(1)}, u32[]{:S(2)}, u32[]{:S(2)}) collective-permute-start(bf16[64,768]{1,0:T(8,128)(2,1)S(1)} %reshape.19.refs_0_.refs_1_), channel_id=1, source_target_pairs={{0,2},{2,4},{4,6},{6,0},{1,3},{3,5},{5,7},{7,1},{8,10},{10,12},{12... | collective-permute-start | bytes 294920 | tf_op jit(solution)/shard_map/ppermute | solution.py:525
  154.0 3.3 %collective-permute-start.2 = (bf16[64,768]{1,0:T(8,128)(2,1)S(1)}, bf16[64,768]{1,0:T(8,128)(2,1)S(1)}, u32[]{:S(2)}, u32[]{:S(2)}) collective-permute-start(bf16[64,768]{1,0:T(8,128)(2,1)S(1)} %reshape.19.refs_0_.refs_1_), channel_id=1, source_target_pairs={{2,0},{4,2},{6,4},{0,6},{3,1},{5,3},{7,5},{1,7},{10,8},{12,10},{14... | collective-permute-start | bytes 294920 | tf_op jit(solution)/shard_map/ppermute | solution.py:526
  157.3 5.3 %shard_map.89.refs_4_ = f32[64,768]{1,0:T(8,128)} custom-call(bf16[24,64,1024]{2,1,0:T(8,128)(2,1)} %get-tuple-element.18.spectrum_ref, bf16[4,64,1152]{2,1,0:T(8,128)(2,1)S(1)} %bitcast.17, bf16[4,64,1152]{2,1,0:T(8,128)(2,1)S(1)} %collective-permute-done.refs_3_.other_ref.refs_10_, bf16[384,512]{1,0:T(8,128)(2,1)S(1)} %copy-done.2, ...), custom_call_target="tpu_custom_call" | custom-call | flops 2000000000 | bytes 1048576 | tf_op jit(solution)/shard_map/pallas_call | solution.py:435
  162.6 0.0 all-to-all-done.2.refs_0_.norm_one
  162.6 0.0 copy-start
  162.6 5.1 %shard_map.90 = (bf16[144,768]{1,0:T(8,128)(2,1)S(1)}, bf16[144,768]{1,0:T(8,128)(2,1)S(1)}, bf16[144,768]{1,0:T(8,128)(2,1)S(1)}, f32[32,2,128]{2,1,0:T(2,128)}, bf16[16,768]{1,0:T(8,128)(2,1)S(1)}) custom-call(f32[32,2,128]{2,1,0:T(2,128)S(1)} %all-to-all-done.2.refs_0_.norm_one, bf16[64,768]{1,0:T(8,128)(2,1)S(1)} %reshape.19.refs_0_.refs_1_, ...), custom_call_target="tpu_custom_call" | custom-call | flops 2000000000 | bytes 1048576 | tf_op jit(solution)/shard_map/pallas_call | solution.py:366
  167.7 7.5 %all-to-all-start.3 = ((f32[32,2,128]{2,1,0:T(2,128)}), f32[32,2,128]{2,1,0:T(2,128)S(1)}, u32[]{:S(2)}, u32[]{:S(2)}) async-start(f32[32,2,128]{2,1,0:T(2,128)} %get-tuple-element.22), calls=%async_computation.3 | async-start | bytes 65536 | tf_op jit(solution)/shard_map/all_to_all | solution.py:529
  175.2 3.3 %collective-permute-start.3 = (bf16[144,768]{1,0:T(8,128)(2,1)S(1)}, bf16[144,768]{1,0:T(8,128)(2,1)S(1)}, u32[]{:S(2)}, u32[]{:S(2)}) collective-permute-start(bf16[144,768]{1,0:T(8,128)(2,1)S(1)} %get-tuple-element.25), channel_id=1, source_target_pairs={{0,8},{8,0},{16,24},{24,16},{1,9},{9,1},{17,25},{25,17},{2,10},{10... | collective-permute-start | bytes 663560 | tf_op jit(solution)/shard_map/ppermute | solution.py:534
  178.5 4.2 %collective-permute-start.4 = (bf16[144,768]{1,0:T(8,128)(2,1)S(1)}, bf16[144,768]{1,0:T(8,128)(2,1)S(1)}, u32[]{:S(2)}, u32[]{:S(2)}) collective-permute-start(bf16[144,768]{1,0:T(8,128)(2,1)S(1)} %get-tuple-element.26), channel_id=1, source_target_pairs={{0,16},{8,24},{16,0},{24,8},{1,17},{9,25},{17,1},{25,9},{2,18},{10... | collective-permute-start | bytes 663560 | tf_op jit(solution)/shard_map/ppermute | solution.py:534
  182.6 2.0 %collective-permute-start.5 = (bf16[16,768]{1,0:T(8,128)(2,1)S(1)}, bf16[16,768]{1,0:T(8,128)(2,1)S(1)}, u32[]{:S(2)}, u32[]{:S(2)}) collective-permute-start(bf16[16,768]{1,0:T(8,128)(2,1)S(1)} %get-tuple-element.27), channel_id=1, source_target_pairs={{0,24},{8,16},{16,8},{24,0},{1,25},{9,17},{17,9},{25,1},{2,26},{10... | collective-permute-start | bytes 73736 | tf_op jit(solution)/shard_map/ppermute | solution.py:534
  184.6 6.1 %collective-permute-done.5.last_ref = bf16[16,768]{1,0:T(8,128)(2,1)S(1)} collective-permute-done((bf16[16,768]{1,0:T(8,128)(2,1)S(1)}, bf16[16,768]{1,0:T(8,128)(2,1)S(1)}, u32[]{:S(2)}, u32[]{:S(2)}) %collective-permute-start.5) | collective-permute-done | bytes 24608 | tf_op jit(solution)/shard_map/ppermute | solution.py:534
  190.7 2.2 %collective-permute-done.4.two = bf16[144,768]{1,0:T(8,128)(2,1)S(1)} collective-permute-done((bf16[144,768]{1,0:T(8,128)(2,1)S(1)}, bf16[144,768]{1,0:T(8,128)(2,1)S(1)}, u32[]{:S(2)}, u32[]{:S(2)}) %collective-permute-start.4) | collective-permute-done | bytes 221216 | tf_op jit(solution)/shard_map/ppermute | solution.py:534
  193.0 0.0 all-to-all-done.3.norm_two
  193.0 1.2 shard_map.91
  (12 shorter events, 0.1 us)
Async XLA Ops:
  0.6 136.3 %copy-start.3 = (bf16[128,128]{1,0:T(8,128)(2,1)S(1)}, bf16[128,128]{1,0:T(8,128)(2,1)}, u32[]{:S(2)}) copy-start(bf16[128,128]{1,0:T(8,128)(2,1)} %constant.11.clone.table.refs_6_.zi.refs_13_) | copy-start | bytes 98308
  0.6 105.4 %copy-start.2 = (bf16[384,512]{1,0:T(8,128)(2,1)S(1)}, bf16[384,512]{1,0:T(8,128)(2,1)}, u32[]{:S(2)}) copy-start(bf16[384,512]{1,0:T(8,128)(2,1)} %constant.9.clone.table.wi) | copy-start | bytes 1179652
  0.7 136.3 %copy-start.5 = (bf16[128,128]{1,0:T(8,128)(2,1)S(1)}, bf16[128,128]{1,0:T(8,128)(2,1)}, u32[]{:S(2)}) copy-start(bf16[128,128]{1,0:T(8,128)(2,1)} %constant.10.clone.refs_5_.zf.refs_12_) | copy-start | bytes 98308
  0.7 136.3 %copy-start.4 = (bf16[384,512]{1,0:T(8,128)(2,1)S(1)}, bf16[384,512]{1,0:T(8,128)(2,1)}, u32[]{:S(2)}) copy-start(bf16[384,512]{1,0:T(8,128)(2,1)} %constant.8.clone.refs_4_.refs_11_) | copy-start | bytes 1179652
  0.7 136.3 %copy-start.1 = (s32[1,2,64,192]{3,2,1,0:T(8,128)S(1)}, s32[1,2,64,192]{3,2,1,0:T(8,128)}, u32[]{:S(2)}) copy-start(s32[1,2,64,192]{3,2,1,0:T(8,128)} %param.9) | copy-start | bytes 294916
  3.0 102.8 %all-to-all-start = ((bf16[32,2,3456]{2,1,0:T(2,128)(2,1)}), bf16[32,2,3456]{2,1,0:T(2,128)(2,1)S(1)}, u32[]{:S(2)}, u32[]{:S(2)}) async-start(bf16[32,2,3456]{2,1,0:T(2,128)(2,1)} %shard_map.86), calls=%async_computation | async-start | bytes 884736 | tf_op jit(solution)/shard_map/all_to_all | solution.py:513
  107.1 29.8 %all-to-all-start.1 = ((bf16[32,2,768]{2,1,0:T(2,128)(2,1)}), bf16[32,2,768]{2,1,0:T(2,128)(2,1)S(1)}, u32[]{:S(2)}, u32[]{:S(2)}) async-start(bf16[32,2,768]{2,1,0:T(2,128)(2,1)} %get-tuple-element.16), calls=%async_computation.1 | async-start | bytes 196608 | tf_op jit(solution)/shard_map/all_to_all | solution.py:513
  123.9 13.1 %collective-permute-start = (bf16[4,64,1152]{2,1,0:T(8,128)(2,1)S(1)}, bf16[4,64,1152]{2,1,0:T(8,128)(2,1)S(1)}, u32[]{:S(2)}, u32[]{:S(2)}) collective-permute-start(bf16[4,64,1152]{2,1,0:T(8,128)(2,1)S(1)} %bitcast.15), channel_id=1, source_target_pairs={{0,1},{1,0},{2,3},{3,2},{4,5},{5,4},{6,7},{7,6},{8,9},{9,8},{10,11... | collective-permute-start | bytes 1769480 | tf_op jit(solution)/shard_map/ppermute | solution.py:522
  141.9 20.7 %all-to-all-start.2 = ((f32[32,2,128]{2,1,0:T(2,128)}), f32[32,2,128]{2,1,0:T(2,128)S(1)}, u32[]{:S(2)}, u32[]{:S(2)}) async-start(f32[32,2,128]{2,1,0:T(2,128)} %get-tuple-element.17), calls=%async_computation.2 | async-start | bytes 65536 | tf_op jit(solution)/shard_map/all_to_all | solution.py:529
  150.7 11.8 %collective-permute-start.1 = (bf16[64,768]{1,0:T(8,128)(2,1)S(1)}, bf16[64,768]{1,0:T(8,128)(2,1)S(1)}, u32[]{:S(2)}, u32[]{:S(2)}) collective-permute-start(bf16[64,768]{1,0:T(8,128)(2,1)S(1)} %reshape.19.refs_0_.refs_1_), channel_id=1, source_target_pairs={{0,2},{2,4},{4,6},{6,0},{1,3},{3,5},{5,7},{7,1},{8,10},{10,12},{12... | collective-permute-start | bytes 294920 | tf_op jit(solution)/shard_map/ppermute | solution.py:525
  154.0 8.5 %collective-permute-start.2 = (bf16[64,768]{1,0:T(8,128)(2,1)S(1)}, bf16[64,768]{1,0:T(8,128)(2,1)S(1)}, u32[]{:S(2)}, u32[]{:S(2)}) collective-permute-start(bf16[64,768]{1,0:T(8,128)(2,1)S(1)} %reshape.19.refs_0_.refs_1_), channel_id=1, source_target_pairs={{2,0},{4,2},{6,4},{0,6},{3,1},{5,3},{7,5},{1,7},{10,8},{12,10},{14... | collective-permute-start | bytes 294920 | tf_op jit(solution)/shard_map/ppermute | solution.py:526
  162.6 30.4 %copy-start = (bf16[2,1,2,3,64,192]{5,4,3,2,1,0:T(8,128)(2,1)S(1)}, bf16[2,1,2,3,64,192]{5,4,3,2,1,0:T(8,128)(2,1)}, u32[]{:S(2)}) copy-start(bf16[2,1,2,3,64,192]{5,4,3,2,1,0:T(8,128)(2,1)} %param.7) | copy-start | bytes 884740
  167.7 25.3 %all-to-all-start.3 = ((f32[32,2,128]{2,1,0:T(2,128)}), f32[32,2,128]{2,1,0:T(2,128)S(1)}, u32[]{:S(2)}, u32[]{:S(2)}) async-start(f32[32,2,128]{2,1,0:T(2,128)} %get-tuple-element.22), calls=%async_computation.3 | async-start | bytes 65536 | tf_op jit(solution)/shard_map/all_to_all | solution.py:529
  175.2 15.6 %collective-permute-start.3 = (bf16[144,768]{1,0:T(8,128)(2,1)S(1)}, bf16[144,768]{1,0:T(8,128)(2,1)S(1)}, u32[]{:S(2)}, u32[]{:S(2)}) collective-permute-start(bf16[144,768]{1,0:T(8,128)(2,1)S(1)} %get-tuple-element.25), channel_id=1, source_target_pairs={{0,8},{8,0},{16,24},{24,16},{1,9},{9,1},{17,25},{25,17},{2,10},{10... | collective-permute-start | bytes 663560 | tf_op jit(solution)/shard_map/ppermute | solution.py:534
  178.5 14.5 %collective-permute-start.4 = (bf16[144,768]{1,0:T(8,128)(2,1)S(1)}, bf16[144,768]{1,0:T(8,128)(2,1)S(1)}, u32[]{:S(2)}, u32[]{:S(2)}) collective-permute-start(bf16[144,768]{1,0:T(8,128)(2,1)S(1)} %get-tuple-element.26), channel_id=1, source_target_pairs={{0,16},{8,24},{16,0},{24,8},{1,17},{9,25},{17,1},{25,9},{2,18},{10... | collective-permute-start | bytes 663560 | tf_op jit(solution)/shard_map/ppermute | solution.py:534
  182.6 8.1 %collective-permute-start.5 = (bf16[16,768]{1,0:T(8,128)(2,1)S(1)}, bf16[16,768]{1,0:T(8,128)(2,1)S(1)}, u32[]{:S(2)}, u32[]{:S(2)}) collective-permute-start(bf16[16,768]{1,0:T(8,128)(2,1)S(1)} %get-tuple-element.27), channel_id=1, source_target_pairs={{0,24},{8,16},{16,8},{24,0},{1,25},{9,17},{17,9},{25,1},{2,26},{10... | collective-permute-start | bytes 73736 | tf_op jit(solution)/shard_map/ppermute | solution.py:534

commit v5 on v4

--- a/solution.py
+++ b/solution.py
@@ -143,7 +143,7 @@
     )(*(distant(a) for a in (data, sampling, coils, depth_inv)))
 
 
-def slab_gradient(packed, coil_rows, column_inv, encodings, nhi):
+def slab_gradient(packed, coil_rows, column_inv, encodings, nhi, first):
     rows, _, slices, _ = coil_rows.shape
 
     def kernel(in_ref, coil_ref, table, out, send):
@@ -177,7 +177,7 @@
                 mine = pltpu.roll(total, 8 - 2 * x, 0) if x else total
                 out[x, :, e * WIDE : (e + 1) * WIDE] = mine
                 for h in range(nhi):
-                    send[4 * h + x, :, e * WIDE : (e + 1) * WIDE] = mine[:2].astype(bf16)
+                    send[(4 * h + x - first) % (4 * nhi), :, e * WIDE : (e + 1) * WIDE] = mine[:2].astype(bf16)
 
     return call(
         kernel,
@@ -516,8 +516,11 @@
     packed = round_ring(packed)
     coil_rows = coil_maps.reshape(2, slabs, rows, zdepth, lines).transpose(2, 0, 1, 3, 4)
     coil_rows = coil_rows.reshape(rows, 2, slices, lines)
-    slab_one, spread = slab_gradient(packed, coil_rows, column_inv, encodings, nhi)
-    one = round_ring(spread)
+    first = nlo + nlo // 2
+    slab_one, spread = slab_gradient(packed, coil_rows, column_inv, encodings, nhi, first)
+    order = [(i + first) % slabs for i in range(slabs)]
+    one = lax.all_to_all(spread, ("hi", "lo"), 0, 0, tiled=True, axis_index_groups=[order])
+    one = jnp.roll(one, first, axis=0).reshape(slices, -1)
     own = lax.all_gather(packed[:, encodings * rows * WIDE :], "phase")
     other = lax.ppermute(own, "enc", [(i, (i + 1) % ncore) for i in range(ncore)])
 

time: 195 us -> 197 us (1.010)
  starting transfers between devices: 88.9 us -> 92.8 us
  waiting for transfers between devices: 71.1 us -> 67.9 us
    all_to_all x0 -> x1, starting transfers between devices: none -> 10.5 us  [reconstruct(): lax.all_to_all(spread, ('hi', 'lo'), 0, 0, tiled=True, axis_index_groups=...]
    all_to_all x2 -> x1, waiting for transfers between devices: 62.8 us -> 55.3 us  [round_ring(): lax.all_to_all(value, ('hi', 'lo'), 0, 0, tiled=True).reshape(slices, -1)]
    all_to_all x2 -> x1, starting transfers between devices: 51.1 us -> 46.3 us  [round_ring(): lax.all_to_all(value, ('hi', 'lo'), 0, 0, tiled=True).reshape(slices, -1)]
    all_to_all x0 -> x1, waiting for transfers between devices: none -> 4.29 us  [reconstruct(): lax.all_to_all(spread, ('hi', 'lo'), 0, 0, tiled=True, axis_index_groups=...]
where the time goes in v5:
time: 197 us; the launch traced here: 196 us
  starting transfers between devices  92.8 us (47%)
  waiting for transfers between devices  67.9 us (34%)
  Pallas kernels  19.8 us (10%)
  blocking collectives  12.6 us (6%)
    all_to_all x1, waiting for transfers between devices, round_ring(): lax.all_to_all(value, ('hi', 'lo'), 0, 0, tiled=True).reshape(slices, -1)  55.3 us
    all_to_all x1, starting transfers between devices, round_ring(): lax.all_to_all(value, ('hi', 'lo'), 0, 0, tiled=True).reshape(slices, -1)  46.3 us
    all_to_all x2, starting transfers between devices, total(): return lax.all_to_all(norms, ('lo', 'phase', 'enc'), 0, 0, tiled=True)  16 us
    all_gather x1, blocking collectives, reconstruct(): own = lax.all_gather(packed[:, encodings * rows * WIDE:], 'phase')  12.6 us
    all_to_all x1, starting transfers between devices, reconstruct(): lax.all_to_all(spread, ('hi', 'lo'), 0, 0, tiled=True, axis_index_groups=...  10.5 us
    ppermute x3, starting transfers between devices, swap(): return lax.ppermute(value, 'lo', [(i, i ^ j) for i in range(nlo)])  9.4 us
    ppermute x3, waiting for transfers between devices, swap(): return lax.ppermute(value, 'lo', [(i, i ^ j) for i in range(nlo)])  8.37 us
    pallas_call x1, Pallas kernels, adjoint_step(): call(kernel, 2 * 10 ** 9, grid=(steps,), in_specs=[spectrum_spec, coil_sp...  5.27 us
  transfers between devices with their start and end apart: 10, of which 4 were waited for; matrix products, arithmetic and copies ran while one was open for 1% of the time, Pallas kernels for 3%

profile of v5, /device:TPU:33, one launch (start us, length us, event | category | flops | bytes accessed | tf_op | source)
XLA Modules:
  0.0 195.6 jit_solution(13867603266706489338)
XLA Ops:
  0.6 0.0 copy-start.2
  0.7 0.0 copy-start.3
  0.7 0.0 copy-start.4
  0.7 0.0 copy-start.5
  0.7 2.4 %shard_map.86 = bf16[32,2,3456]{2,1,0:T(2,128)(2,1)} custom-call(bf16[2,2,3,64,192]{4,3,2,1,0:T(8,128)(2,1)} %bitcast.13, s32[2,64,192]{2,1,0:T(8,128)} %bitcast.19, bf16[2,24,4,2,192]{4,3,2,1,0:T(2,128)(2,1)} %coil_ref.1, bf16[128,128]{1,0:T(8,128)(2,1)} %constant.11.clone.table.refs_6_.zi.refs_13_), custom_call_target="tpu_custom_call" | custom-call | flops 100000000 | bytes 1048576 | tf_op jit(solution)/shard_map/pallas_call | solution.py:137
  3.0 46.3 %all-to-all-start = ((bf16[32,2,3456]{2,1,0:T(2,128)(2,1)}), bf16[32,2,3456]{2,1,0:T(2,128)(2,1)S(1)}, u32[]{:S(2)}, u32[]{:S(2)}) async-start(bf16[32,2,3456]{2,1,0:T(2,128)(2,1)} %shard_map.86), calls=%async_computation | async-start | bytes 884736 | tf_op jit(solution)/shard_map/all_to_all | solution.py:513
  49.4 1.1 copy.13
  50.4 0.2 reshape.18.coil_ref
  50.6 55.3 %all-to-all-done = bf16[32,2,3456]{2,1,0:T(2,128)(2,1)S(1)} async-done(((bf16[32,2,3456]{2,1,0:T(2,128)(2,1)}), bf16[32,2,3456]{2,1,0:T(2,128)(2,1)S(1)}, u32[]{:S(2)}, u32[]{:S(2)}) %all-to-all-start) | async-done | bytes 442400 | tf_op jit(solution)/shard_map/all_to_all | solution.py:513
  105.9 0.2 reshape.16.in_ref
  106.1 1.1 shard_map.87
  107.1 10.5 %all-to-all-start.1 = ((bf16[32,2,768]{2,1,0:T(2,128)(2,1)}), bf16[32,2,768]{2,1,0:T(2,128)(2,1)S(1)}, u32[]{:S(2)}, u32[]{:S(2)}) async-start(bf16[32,2,768]{2,1,0:T(2,128)(2,1)} %get-tuple-element.16), calls=%async_computation.1 | async-start | bytes 196608 | tf_op jit(solution)/shard_map/all_to_all | solution.py:522
  117.6 12.6 %all-gather = bf16[256,1152]{1,0:T(8,128)(2,1)S(1)} all-gather(bf16[64,1152]{1,0:T(8,128)(2,1)S(1)} %slice.16), channel_id=2, replica_groups=mesh['pat'=2,'hi'=8,'lo'=4,'phase'=4,'enc'=2] {'phase'}, dimensions={0}, use_global_device_ids=true | all-gather | bytes 737280 | tf_op jit(solution)/shard_map/all_gather | solution.py:524
  130.2 4.0 %collective-permute-start = (bf16[4,64,1152]{2,1,0:T(8,128)(2,1)S(1)}, bf16[4,64,1152]{2,1,0:T(8,128)(2,1)S(1)}, u32[]{:S(2)}, u32[]{:S(2)}) collective-permute-start(bf16[4,64,1152]{2,1,0:T(8,128)(2,1)S(1)} %bitcast.15), channel_id=1, source_target_pairs={{0,1},{1,0},{2,3},{3,2},{4,5},{5,4},{6,7},{7,6},{8,9},{9,8},{10,11... | collective-permute-start | bytes 1769480 | tf_op jit(solution)/shard_map/ppermute | solution.py:525
  134.2 4.3 %all-to-all-done.1 = bf16[32,2,768]{2,1,0:T(2,128)(2,1)S(1)} async-done(((bf16[32,2,768]{2,1,0:T(2,128)(2,1)}), bf16[32,2,768]{2,1,0:T(2,128)(2,1)S(1)}, u32[]{:S(2)}, u32[]{:S(2)}) %all-to-all-start.1) | async-done | bytes 98336 | tf_op jit(solution)/shard_map/all_to_all | solution.py:522
  138.5 0.1 slice.15
  138.6 0.1 pad_maximum_fusion
  138.8 4.9 %shard_map.88 = (bf16[64,768]{1,0:T(8,128)(2,1)}, bf16[64,768]{1,0:T(8,128)(2,1)}, bf16[64,768]{1,0:T(8,128)(2,1)}, f32[32,2,128]{2,1,0:T(2,128)}, bf16[24,64,1024]{2,1,0:T(8,128)(2,1)}) custom-call(bf16[64,768]{1,0:T(8,128)(2,1)S(1)} %reshape.19.refs_0_.refs_1_, s32[2,64,192]{2,1,0:T(8,128)S(1)} %bitcast.20, bf16[4,64,1152]{2,1,0:T(8,128)(2,1)S(1)} %bitcast.16, ...), custom_call_target="tpu_custom_call" | custom-call | flops 2000000000 | bytes 1048576 | tf_op jit(solution)/shard_map/pallas_call | solution.py:377
  143.7 8.6 %all-to-all-start.2 = ((f32[32,2,128]{2,1,0:T(2,128)}), f32[32,2,128]{2,1,0:T(2,128)S(1)}, u32[]{:S(2)}, u32[]{:S(2)}) async-start(f32[32,2,128]{2,1,0:T(2,128)} %get-tuple-element.17), calls=%async_computation.2 | async-start | bytes 65536 | tf_op jit(solution)/shard_map/all_to_all | solution.py:532
  152.3 3.3 %collective-permute-start.1 = (bf16[64,768]{1,0:T(8,128)(2,1)S(1)}, bf16[64,768]{1,0:T(8,128)(2,1)S(1)}, u32[]{:S(2)}, u32[]{:S(2)}) collective-permute-start(bf16[64,768]{1,0:T(8,128)(2,1)S(1)} %reshape.19.refs_0_.refs_1_), channel_id=1, source_target_pairs={{0,2},{2,4},{4,6},{6,0},{1,3},{3,5},{5,7},{7,1},{8,10},{10,12},{12... | collective-permute-start | bytes 294920 | tf_op jit(solution)/shard_map/ppermute | solution.py:528
  155.5 3.3 %collective-permute-start.2 = (bf16[64,768]{1,0:T(8,128)(2,1)S(1)}, bf16[64,768]{1,0:T(8,128)(2,1)S(1)}, u32[]{:S(2)}, u32[]{:S(2)}) collective-permute-start(bf16[64,768]{1,0:T(8,128)(2,1)S(1)} %reshape.19.refs_0_.refs_1_), channel_id=1, source_target_pairs={{2,0},{4,2},{6,4},{0,6},{3,1},{5,3},{7,5},{1,7},{10,8},{12,10},{14... | collective-permute-start | bytes 294920 | tf_op jit(solution)/shard_map/ppermute | solution.py:529
  158.8 5.3 %shard_map.89.refs_4_ = f32[64,768]{1,0:T(8,128)} custom-call(bf16[24,64,1024]{2,1,0:T(8,128)(2,1)} %get-tuple-element.18.spectrum_ref, bf16[4,64,1152]{2,1,0:T(8,128)(2,1)S(1)} %bitcast.17, bf16[4,64,1152]{2,1,0:T(8,128)(2,1)S(1)} %collective-permute-done.refs_3_.other_ref.refs_10_, bf16[384,512]{1,0:T(8,128)(2,1)S(1)} %copy-done.2, ...), custom_call_target="tpu_custom_call" | custom-call | flops 2000000000 | bytes 1048576 | tf_op jit(solution)/shard_map/pallas_call | solution.py:435
  164.1 0.0 collective-permute-done.1.refs_2_
  164.1 0.0 copy-start
  164.1 5.1 %shard_map.90 = (bf16[144,768]{1,0:T(8,128)(2,1)S(1)}, bf16[144,768]{1,0:T(8,128)(2,1)S(1)}, bf16[144,768]{1,0:T(8,128)(2,1)S(1)}, f32[32,2,128]{2,1,0:T(2,128)}, bf16[16,768]{1,0:T(8,128)(2,1)S(1)}) custom-call(f32[32,2,128]{2,1,0:T(2,128)S(1)} %all-to-all-done.2.refs_0_.norm_one, bf16[64,768]{1,0:T(8,128)(2,1)S(1)} %reshape.19.refs_0_.refs_1_, ...), custom_call_target="tpu_custom_call" | custom-call | flops 2000000000 | bytes 1048576 | tf_op jit(solution)/shard_map/pallas_call | solution.py:366
  169.2 7.5 %all-to-all-start.3 = ((f32[32,2,128]{2,1,0:T(2,128)}), f32[32,2,128]{2,1,0:T(2,128)S(1)}, u32[]{:S(2)}, u32[]{:S(2)}) async-start(f32[32,2,128]{2,1,0:T(2,128)} %get-tuple-element.22), calls=%async_computation.3 | async-start | bytes 65536 | tf_op jit(solution)/shard_map/all_to_all | solution.py:532
  176.7 3.3 %collective-permute-start.3 = (bf16[144,768]{1,0:T(8,128)(2,1)S(1)}, bf16[144,768]{1,0:T(8,128)(2,1)S(1)}, u32[]{:S(2)}, u32[]{:S(2)}) collective-permute-start(bf16[144,768]{1,0:T(8,128)(2,1)S(1)} %get-tuple-element.25), channel_id=1, source_target_pairs={{0,8},{8,0},{16,24},{24,16},{1,9},{9,1},{17,25},{25,17},{2,10},{10... | collective-permute-start | bytes 663560 | tf_op jit(solution)/shard_map/ppermute | solution.py:537
  180.0 4.2 %collective-permute-start.4 = (bf16[144,768]{1,0:T(8,128)(2,1)S(1)}, bf16[144,768]{1,0:T(8,128)(2,1)S(1)}, u32[]{:S(2)}, u32[]{:S(2)}) collective-permute-start(bf16[144,768]{1,0:T(8,128)(2,1)S(1)} %get-tuple-element.26), channel_id=1, source_target_pairs={{0,16},{8,24},{16,0},{24,8},{1,17},{9,25},{17,1},{25,9},{2,18},{10... | collective-permute-start | bytes 663560 | tf_op jit(solution)/shard_map/ppermute | solution.py:537
  184.1 2.0 collective-permute-start.5
  186.1 6.1 %collective-permute-done.5.last_ref = bf16[16,768]{1,0:T(8,128)(2,1)S(1)} collective-permute-done((bf16[16,768]{1,0:T(8,128)(2,1)S(1)}, bf16[16,768]{1,0:T(8,128)(2,1)S(1)}, u32[]{:S(2)}, u32[]{:S(2)}) %collective-permute-start.5) | collective-permute-done | bytes 24608 | tf_op jit(solution)/shard_map/ppermute | solution.py:537
  192.2 2.2 %collective-permute-done.4.two = bf16[144,768]{1,0:T(8,128)(2,1)S(1)} collective-permute-done((bf16[144,768]{1,0:T(8,128)(2,1)S(1)}, bf16[144,768]{1,0:T(8,128)(2,1)S(1)}, u32[]{:S(2)}, u32[]{:S(2)}) %collective-permute-start.4) | collective-permute-done | bytes 221216 | tf_op jit(solution)/shard_map/ppermute | solution.py:537
  194.5 1.2 shard_map.91
  (15 shorter events, 0.1 us)
Async XLA Ops:
  0.6 105.4 %copy-start.2 = (bf16[384,512]{1,0:T(8,128)(2,1)S(1)}, bf16[384,512]{1,0:T(8,128)(2,1)}, u32[]{:S(2)}) copy-start(bf16[384,512]{1,0:T(8,128)(2,1)} %constant.9.clone.table.wi) | copy-start | bytes 1179652
  0.6 138.1 %copy-start.1 = (s32[1,2,64,192]{3,2,1,0:T(8,128)S(1)}, s32[1,2,64,192]{3,2,1,0:T(8,128)}, u32[]{:S(2)}) copy-start(s32[1,2,64,192]{3,2,1,0:T(8,128)} %param.9) | copy-start | bytes 294916
  0.7 138.1 %copy-start.3 = (bf16[128,128]{1,0:T(8,128)(2,1)S(1)}, bf16[128,128]{1,0:T(8,128)(2,1)}, u32[]{:S(2)}) copy-start(bf16[128,128]{1,0:T(8,128)(2,1)} %constant.11.clone.table.refs_6_.zi.refs_13_) | copy-start | bytes 98308
  0.7 138.1 %copy-start.4 = (bf16[384,512]{1,0:T(8,128)(2,1)S(1)}, bf16[384,512]{1,0:T(8,128)(2,1)}, u32[]{:S(2)}) copy-start(bf16[384,512]{1,0:T(8,128)(2,1)} %constant.8.clone.refs_4_.refs_11_) | copy-start | bytes 1179652
  0.7 138.1 %copy-start.5 = (bf16[128,128]{1,0:T(8,128)(2,1)S(1)}, bf16[128,128]{1,0:T(8,128)(2,1)}, u32[]{:S(2)}) copy-start(bf16[128,128]{1,0:T(8,128)(2,1)} %constant.10.clone.refs_5_.zf.refs_12_) | copy-start | bytes 98308
  3.0 102.8 %all-to-all-start = ((bf16[32,2,3456]{2,1,0:T(2,128)(2,1)}), bf16[32,2,3456]{2,1,0:T(2,128)(2,1)S(1)}, u32[]{:S(2)}, u32[]{:S(2)}) async-start(bf16[32,2,3456]{2,1,0:T(2,128)(2,1)} %shard_map.86), calls=%async_computation | async-start | bytes 884736 | tf_op jit(solution)/shard_map/all_to_all | solution.py:513
  107.1 31.4 %all-to-all-start.1 = ((bf16[32,2,768]{2,1,0:T(2,128)(2,1)}), bf16[32,2,768]{2,1,0:T(2,128)(2,1)S(1)}, u32[]{:S(2)}, u32[]{:S(2)}) async-start(bf16[32,2,768]{2,1,0:T(2,128)(2,1)} %get-tuple-element.16), calls=%async_computation.1 | async-start | bytes 196608 | tf_op jit(solution)/shard_map/all_to_all | solution.py:522
  130.2 8.6 %collective-permute-start = (bf16[4,64,1152]{2,1,0:T(8,128)(2,1)S(1)}, bf16[4,64,1152]{2,1,0:T(8,128)(2,1)S(1)}, u32[]{:S(2)}, u32[]{:S(2)}) collective-permute-start(bf16[4,64,1152]{2,1,0:T(8,128)(2,1)S(1)} %bitcast.15), channel_id=1, source_target_pairs={{0,1},{1,0},{2,3},{3,2},{4,5},{5,4},{6,7},{7,6},{8,9},{9,8},{10,11... | collective-permute-start | bytes 1769480 | tf_op jit(solution)/shard_map/ppermute | solution.py:525
  143.7 20.4 %all-to-all-start.2 = ((f32[32,2,128]{2,1,0:T(2,128)}), f32[32,2,128]{2,1,0:T(2,128)S(1)}, u32[]{:S(2)}, u32[]{:S(2)}) async-start(f32[32,2,128]{2,1,0:T(2,128)} %get-tuple-element.17), calls=%async_computation.2 | async-start | bytes 65536 | tf_op jit(solution)/shard_map/all_to_all | solution.py:532
  152.3 11.8 %collective-permute-start.1 = (bf16[64,768]{1,0:T(8,128)(2,1)S(1)}, bf16[64,768]{1,0:T(8,128)(2,1)S(1)}, u32[]{:S(2)}, u32[]{:S(2)}) collective-permute-start(bf16[64,768]{1,0:T(8,128)(2,1)S(1)} %reshape.19.refs_0_.refs_1_), channel_id=1, source_target_pairs={{0,2},{2,4},{4,6},{6,0},{1,3},{3,5},{5,7},{7,1},{8,10},{10,12},{12... | collective-permute-start | bytes 294920 | tf_op jit(solution)/shard_map/ppermute | solution.py:528
  155.5 8.5 %collective-permute-start.2 = (bf16[64,768]{1,0:T(8,128)(2,1)S(1)}, bf16[64,768]{1,0:T(8,128)(2,1)S(1)}, u32[]{:S(2)}, u32[]{:S(2)}) collective-permute-start(bf16[64,768]{1,0:T(8,128)(2,1)S(1)} %reshape.19.refs_0_.refs_1_), channel_id=1, source_target_pairs={{2,0},{4,2},{6,4},{0,6},{3,1},{5,3},{7,5},{1,7},{10,8},{12,10},{14... | collective-permute-start | bytes 294920 | tf_op jit(solution)/shard_map/ppermute | solution.py:529
  164.1 30.4 %copy-start = (bf16[2,1,2,3,64,192]{5,4,3,2,1,0:T(8,128)(2,1)S(1)}, bf16[2,1,2,3,64,192]{5,4,3,2,1,0:T(8,128)(2,1)}, u32[]{:S(2)}) copy-start(bf16[2,1,2,3,64,192]{5,4,3,2,1,0:T(8,128)(2,1)} %param.7) | copy-start | bytes 884740
  169.2 25.3 %all-to-all-start.3 = ((f32[32,2,128]{2,1,0:T(2,128)}), f32[32,2,128]{2,1,0:T(2,128)S(1)}, u32[]{:S(2)}, u32[]{:S(2)}) async-start(f32[32,2,128]{2,1,0:T(2,128)} %get-tuple-element.22), calls=%async_computation.3 | async-start | bytes 65536 | tf_op jit(solution)/shard_map/all_to_all | solution.py:532
  176.7 15.6 %collective-permute-start.3 = (bf16[144,768]{1,0:T(8,128)(2,1)S(1)}, bf16[144,768]{1,0:T(8,128)(2,1)S(1)}, u32[]{:S(2)}, u32[]{:S(2)}) collective-permute-start(bf16[144,768]{1,0:T(8,128)(2,1)S(1)} %get-tuple-element.25), channel_id=1, source_target_pairs={{0,8},{8,0},{16,24},{24,16},{1,9},{9,1},{17,25},{25,17},{2,10},{10... | collective-permute-start | bytes 663560 | tf_op jit(solution)/shard_map/ppermute | solution.py:537
  180.0 14.5 %collective-permute-start.4 = (bf16[144,768]{1,0:T(8,128)(2,1)S(1)}, bf16[144,768]{1,0:T(8,128)(2,1)S(1)}, u32[]{:S(2)}, u32[]{:S(2)}) collective-permute-start(bf16[144,768]{1,0:T(8,128)(2,1)S(1)} %get-tuple-element.26), channel_id=1, source_target_pairs={{0,16},{8,24},{16,0},{24,8},{1,17},{9,25},{17,1},{25,9},{2,18},{10... | collective-permute-start | bytes 663560 | tf_op jit(solution)/shard_map/ppermute | solution.py:537
  184.1 8.1 %collective-permute-start.5 = (bf16[16,768]{1,0:T(8,128)(2,1)S(1)}, bf16[16,768]{1,0:T(8,128)(2,1)S(1)}, u32[]{:S(2)}, u32[]{:S(2)}) collective-permute-start(bf16[16,768]{1,0:T(8,128)(2,1)S(1)} %get-tuple-element.27), channel_id=1, source_target_pairs={{0,24},{8,16},{16,8},{24,0},{1,25},{9,17},{17,9},{25,1},{2,26},{10... | collective-permute-start | bytes 73736 | tf_op jit(solution)/shard_map/ppermute | solution.py:537

commit v6 on v4

--- a/solution.py
+++ b/solution.py
@@ -114,31 +114,43 @@
 
     def kernel(data_ref, mask_ref, coil_ref, table, out):
         share_index = lax.axis_index("phase") * lax.axis_size("enc") + lax.axis_index("enc")
-        for e in range(encodings):
-            weight = -mask_ref[e].astype(f32)
+        step = pl.program_id(0)
+
+        @pl.when(step < encodings)
+        def _():
+            weight = -mask_ref[0].astype(f32)
             for r in range(rows):
-                both = stack(*((data_ref[c, e, r].astype(f32) * weight).astype(bf16) for c in range(2)))
+                both = stack(*((data_ref[c, 0, r].astype(f32) * weight).astype(bf16) for c in range(2)))
                 both = dot(table[...], both)
                 real, imag = both[:slices], both[slices:]
-                at = (e * rows + r) * WIDE
+                at = r * WIDE
                 for j, x in enumerate((real[:, :LANE], imag[:, :LANE], lanes(real[:, LANE:], imag[:, LANE:]))):
                     x = x.astype(bf16).reshape(slabs, 2, LANE)
                     out[:, :, at + j * LANE : at + (j + 1) * LANE] = x
-        first = share_index * group
-        for k in range(group):
-            real, imag = (coil_ref[c, first + k].astype(f32) for c in range(2))
-            tail = jnp.concatenate([real[:, :, LANE:], imag[:, :, LANE:]], axis=2)
-            at = (images + k) * WIDE
-            for j, x in enumerate((real[:, :, :LANE], imag[:, :, :LANE], tail)):
-                x = x.astype(bf16)
-                for h in range(nhi):
-                    out[4 * h : 4 * h + 4, :, at + j * LANE : at + (j + 1) * LANE] = x
+
+        @pl.when(step == encodings)
+        def _():
+            first = share_index * group
+            for k in range(group):
+                real, imag = (coil_ref[c, first + k].astype(f32) for c in range(2))
+                tail = jnp.concatenate([real[:, :, LANE:], imag[:, :, LANE:]], axis=2)
+                at = k * WIDE
+                for j, x in enumerate((real[:, :, :LANE], imag[:, :, :LANE], tail)):
+                    x = x.astype(bf16)
+                    for h in range(nhi):
+                        out[4 * h : 4 * h + 4, :, at + j * LANE : at + (j + 1) * LANE] = x
 
     return call(
         kernel,
         10**8,
-        in_specs=[VMEM, VMEM, VMEM, VMEM],
-        out_specs=VMEM,
+        grid=(encodings + 1,),
+        in_specs=[
+            pl.BlockSpec((2, 1, *data.shape[2:]), lambda g: (0, jnp.minimum(g, encodings - 1), 0, 0, 0)),
+            pl.BlockSpec((1, *sampling.shape[1:]), lambda g: (jnp.minimum(g, encodings - 1), 0, 0)),
+            whole(coils),
+            whole(depth_inv),
+        ],
+        out_specs=pl.BlockSpec((slabs, 2, rows * WIDE), lambda g: (0, 0, g)),
         out_shape=jax.ShapeDtypeStruct((slabs, 2, (images + group) * WIDE), bf16),
     )(*(distant(a) for a in (data, sampling, coils, depth_inv)))
 
@@ -501,7 +513,7 @@
     slabs = nhi * nlo
     group = coils // (nphase * ncore)
     assert (nlo, readout, rows, zdepth, lines, slices) == (4, 4, 3, 2, LANE + HALF, 2 * slabs)
-    assert group * nhi == coils and nphase * ncore == nhi and ncore == 2
+    assert group == rows and group * nhi == coils and nphase * ncore == nhi and ncore == 2
     column_fwd, column_inv = column_table(lines, -1.0), column_table(lines, 1.0)
     depth_fwd, depth_inv = depth_table(slices, -1.0), depth_table(slices, 1.0)
     tables = (column_fwd, column_inv, depth_fwd, depth_inv)

time: 195 us -> 196 us (level)
  no operation moved by 1% of the time
where the time goes in v6:
time: 196 us; the launch traced here: 195 us
  starting transfers between devices  88.9 us (45%)
  waiting for transfers between devices  71.1 us (36%)
  Pallas kernels  20.3 us (10%)
  blocking collectives  12 us (6%)
    all_to_all x2, waiting for transfers between devices, round_ring(): lax.all_to_all(value, ('hi', 'lo'), 0, 0, tiled=True).reshape(slices, -1)  62.8 us
    all_to_all x2, starting transfers between devices, round_ring(): lax.all_to_all(value, ('hi', 'lo'), 0, 0, tiled=True).reshape(slices, -1)  51.1 us
    all_to_all x2, starting transfers between devices, total(): return lax.all_to_all(norms, ('lo', 'phase', 'enc'), 0, 0, tiled=True)  16.3 us
    all_gather x1, blocking collectives, reconstruct(): own = lax.all_gather(packed[:, encodings * rows * WIDE:], 'phase')  12 us
    ppermute x3, starting transfers between devices, swap(): return lax.ppermute(value, 'lo', [(i, i ^ j) for i in range(nlo)])  9.4 us
    ppermute x3, waiting for transfers between devices, swap(): return lax.ppermute(value, 'lo', [(i, i ^ j) for i in range(nlo)])  8.37 us
    ppermute x1, starting transfers between devices, reconstruct(): lax.ppermute(own, 'enc', [(i, (i + 1) % ncore) for i in range(ncore)])  5.55 us
    pallas_call x1, Pallas kernels, adjoint_step(): call(kernel, 2 * 10 ** 9, grid=(steps,), in_specs=[spectrum_spec, coil_sp...  5.26 us
  transfers between devices with their start and end apart: 10, of which 4 were waited for; matrix products, arithmetic and copies ran while one was open for 1% of the time, Pallas kernels for 3%

profile of v6, /device:TPU:33, one launch (start us, length us, event | category | flops | bytes accessed | tf_op | source)
XLA Modules:
  0.0 194.6 jit_solution(5445080714037990306)
XLA Ops:
  0.6 0.0 copy-start.3
  0.6 0.0 copy-start.2
  0.7 0.0 copy-start.5
  0.7 0.0 copy-start.4
  0.7 2.9 %shard_map.86 = bf16[32,2,3456]{2,1,0:T(2,128)(2,1)} custom-call(bf16[2,2,3,64,192]{4,3,2,1,0:T(8,128)(2,1)} %bitcast.13, s32[2,64,192]{2,1,0:T(8,128)} %bitcast.19, bf16[2,24,4,2,192]{4,3,2,1,0:T(2,128)(2,1)} %coil_ref.1, bf16[128,128]{1,0:T(8,128)(2,1)} %constant.11.clone.table.refs_6_.zi.refs_13_), custom_call_target="tpu_custom_call" | custom-call | flops 100000000 | bytes 1048576 | tf_op jit(solution)/shard_map/pallas_call | solution.py:143
  3.6 46.3 %all-to-all-start = ((bf16[32,2,3456]{2,1,0:T(2,128)(2,1)}), bf16[32,2,3456]{2,1,0:T(2,128)(2,1)S(1)}, u32[]{:S(2)}, u32[]{:S(2)}) async-start(bf16[32,2,3456]{2,1,0:T(2,128)(2,1)} %shard_map.86), calls=%async_computation | async-start | bytes 884736 | tf_op jit(solution)/shard_map/all_to_all | solution.py:525
  49.9 1.1 copy.13
  50.9 0.2 reshape.18.coil_ref
  51.1 55.3 %all-to-all-done = bf16[32,2,3456]{2,1,0:T(2,128)(2,1)S(1)} async-done(((bf16[32,2,3456]{2,1,0:T(2,128)(2,1)}), bf16[32,2,3456]{2,1,0:T(2,128)(2,1)S(1)}, u32[]{:S(2)}, u32[]{:S(2)}) %all-to-all-start) | async-done | bytes 442400 | tf_op jit(solution)/shard_map/all_to_all | solution.py:525
  106.4 0.2 reshape.16.in_ref
  106.6 1.0 shard_map.87
  107.6 4.8 %all-to-all-start.1 = ((bf16[32,2,768]{2,1,0:T(2,128)(2,1)}), bf16[32,2,768]{2,1,0:T(2,128)(2,1)S(1)}, u32[]{:S(2)}, u32[]{:S(2)}) async-start(bf16[32,2,768]{2,1,0:T(2,128)(2,1)} %get-tuple-element.16), calls=%async_computation.1 | async-start | bytes 196608 | tf_op jit(solution)/shard_map/all_to_all | solution.py:525
  112.4 12.0 %all-gather = bf16[256,1152]{1,0:T(8,128)(2,1)S(1)} all-gather(bf16[64,1152]{1,0:T(8,128)(2,1)S(1)} %slice.4), channel_id=2, replica_groups=mesh['pat'=2,'hi'=8,'lo'=4,'phase'=4,'enc'=2] {'phase'}, dimensions={0}, use_global_device_ids=true | all-gather | bytes 737280 | tf_op jit(solution)/shard_map/all_gather | solution.py:533
  124.4 5.5 %collective-permute-start = (bf16[4,64,1152]{2,1,0:T(8,128)(2,1)S(1)}, bf16[4,64,1152]{2,1,0:T(8,128)(2,1)S(1)}, u32[]{:S(2)}, u32[]{:S(2)}) collective-permute-start(bf16[4,64,1152]{2,1,0:T(8,128)(2,1)S(1)} %bitcast.15), channel_id=1, source_target_pairs={{0,1},{1,0},{2,3},{3,2},{4,5},{5,4},{6,7},{7,6},{8,9},{9,8},{10,11... | collective-permute-start | bytes 1769480 | tf_op jit(solution)/shard_map/ppermute | solution.py:534
  129.9 7.5 %all-to-all-done.1 = bf16[32,2,768]{2,1,0:T(2,128)(2,1)S(1)} async-done(((bf16[32,2,768]{2,1,0:T(2,128)(2,1)}), bf16[32,2,768]{2,1,0:T(2,128)(2,1)S(1)}, u32[]{:S(2)}, u32[]{:S(2)}) %all-to-all-start.1) | async-done | bytes 98336 | tf_op jit(solution)/shard_map/all_to_all | solution.py:525
  137.5 0.0 collective-permute-done.refs_3_.other_ref.refs_10_
  137.5 4.9 %shard_map.88 = (bf16[64,768]{1,0:T(8,128)(2,1)}, bf16[64,768]{1,0:T(8,128)(2,1)}, bf16[64,768]{1,0:T(8,128)(2,1)}, f32[32,2,128]{2,1,0:T(2,128)}, bf16[24,64,1024]{2,1,0:T(8,128)(2,1)}) custom-call(bf16[64,768]{1,0:T(8,128)(2,1)S(1)} %reshape.19.refs_0_.refs_1_, s32[2,64,192]{2,1,0:T(8,128)S(1)} %bitcast.20, bf16[4,64,1152]{2,1,0:T(8,128)(2,1)S(1)} %bitcast.16, ...), custom_call_target="tpu_custom_call" | custom-call | flops 2000000000 | bytes 1048576 | tf_op jit(solution)/shard_map/pallas_call | solution.py:389
  142.4 8.9 %all-to-all-start.2 = ((f32[32,2,128]{2,1,0:T(2,128)}), f32[32,2,128]{2,1,0:T(2,128)S(1)}, u32[]{:S(2)}, u32[]{:S(2)}) async-start(f32[32,2,128]{2,1,0:T(2,128)} %get-tuple-element.17), calls=%async_computation.2 | async-start | bytes 65536 | tf_op jit(solution)/shard_map/all_to_all | solution.py:541
  151.2 3.3 %collective-permute-start.1 = (bf16[64,768]{1,0:T(8,128)(2,1)S(1)}, bf16[64,768]{1,0:T(8,128)(2,1)S(1)}, u32[]{:S(2)}, u32[]{:S(2)}) collective-permute-start(bf16[64,768]{1,0:T(8,128)(2,1)S(1)} %reshape.19.refs_0_.refs_1_), channel_id=1, source_target_pairs={{0,2},{2,4},{4,6},{6,0},{1,3},{3,5},{5,7},{7,1},{8,10},{10,12},{12... | collective-permute-start | bytes 294920 | tf_op jit(solution)/shard_map/ppermute | solution.py:537
  154.5 3.3 %collective-permute-start.2 = (bf16[64,768]{1,0:T(8,128)(2,1)S(1)}, bf16[64,768]{1,0:T(8,128)(2,1)S(1)}, u32[]{:S(2)}, u32[]{:S(2)}) collective-permute-start(bf16[64,768]{1,0:T(8,128)(2,1)S(1)} %reshape.19.refs_0_.refs_1_), channel_id=1, source_target_pairs={{2,0},{4,2},{6,4},{0,6},{3,1},{5,3},{7,5},{1,7},{10,8},{12,10},{14... | collective-permute-start | bytes 294920 | tf_op jit(solution)/shard_map/ppermute | solution.py:538
  157.8 5.3 %shard_map.89.refs_4_ = f32[64,768]{1,0:T(8,128)} custom-call(bf16[24,64,1024]{2,1,0:T(8,128)(2,1)} %get-tuple-element.18.spectrum_ref, bf16[4,64,1152]{2,1,0:T(8,128)(2,1)S(1)} %bitcast.17, bf16[4,64,1152]{2,1,0:T(8,128)(2,1)S(1)} %collective-permute-done.refs_3_.other_ref.refs_10_, bf16[384,512]{1,0:T(8,128)(2,1)S(1)} %copy-done.2, ...), custom_call_target="tpu_custom_call" | custom-call | flops 2000000000 | bytes 1048576 | tf_op jit(solution)/shard_map/pallas_call | solution.py:447
  163.1 0.0 copy-start
  163.1 5.1 %shard_map.90 = (bf16[144,768]{1,0:T(8,128)(2,1)S(1)}, bf16[144,768]{1,0:T(8,128)(2,1)S(1)}, bf16[144,768]{1,0:T(8,128)(2,1)S(1)}, f32[32,2,128]{2,1,0:T(2,128)}, bf16[16,768]{1,0:T(8,128)(2,1)S(1)}) custom-call(f32[32,2,128]{2,1,0:T(2,128)S(1)} %all-to-all-done.2.refs_0_.norm_one, bf16[64,768]{1,0:T(8,128)(2,1)S(1)} %reshape.19.refs_0_.refs_1_, ...), custom_call_target="tpu_custom_call" | custom-call | flops 2000000000 | bytes 1048576 | tf_op jit(solution)/shard_map/pallas_call | solution.py:378
  168.2 7.5 %all-to-all-start.3 = ((f32[32,2,128]{2,1,0:T(2,128)}), f32[32,2,128]{2,1,0:T(2,128)S(1)}, u32[]{:S(2)}, u32[]{:S(2)}) async-start(f32[32,2,128]{2,1,0:T(2,128)} %get-tuple-element.22), calls=%async_computation.3 | async-start | bytes 65536 | tf_op jit(solution)/shard_map/all_to_all | solution.py:541
  175.7 3.3 %collective-permute-start.3 = (bf16[144,768]{1,0:T(8,128)(2,1)S(1)}, bf16[144,768]{1,0:T(8,128)(2,1)S(1)}, u32[]{:S(2)}, u32[]{:S(2)}) collective-permute-start(bf16[144,768]{1,0:T(8,128)(2,1)S(1)} %get-tuple-element.25), channel_id=1, source_target_pairs={{0,8},{8,0},{16,24},{24,16},{1,9},{9,1},{17,25},{25,17},{2,10},{10... | collective-permute-start | bytes 663560 | tf_op jit(solution)/shard_map/ppermute | solution.py:546
  179.0 4.2 %collective-permute-start.4 = (bf16[144,768]{1,0:T(8,128)(2,1)S(1)}, bf16[144,768]{1,0:T(8,128)(2,1)S(1)}, u32[]{:S(2)}, u32[]{:S(2)}) collective-permute-start(bf16[144,768]{1,0:T(8,128)(2,1)S(1)} %get-tuple-element.26), channel_id=1, source_target_pairs={{0,16},{8,24},{16,0},{24,8},{1,17},{9,25},{17,1},{25,9},{2,18},{10... | collective-permute-start | bytes 663560 | tf_op jit(solution)/shard_map/ppermute | solution.py:546
  183.1 2.0 %collective-permute-start.5 = (bf16[16,768]{1,0:T(8,128)(2,1)S(1)}, bf16[16,768]{1,0:T(8,128)(2,1)S(1)}, u32[]{:S(2)}, u32[]{:S(2)}) collective-permute-start(bf16[16,768]{1,0:T(8,128)(2,1)S(1)} %get-tuple-element.27), channel_id=1, source_target_pairs={{0,24},{8,16},{16,8},{24,0},{1,25},{9,17},{17,9},{25,1},{2,26},{10... | collective-permute-start | bytes 73736 | tf_op jit(solution)/shard_map/ppermute | solution.py:546
  185.1 6.1 %collective-permute-done.5.last_ref = bf16[16,768]{1,0:T(8,128)(2,1)S(1)} collective-permute-done((bf16[16,768]{1,0:T(8,128)(2,1)S(1)}, bf16[16,768]{1,0:T(8,128)(2,1)S(1)}, u32[]{:S(2)}, u32[]{:S(2)}) %collective-permute-start.5) | collective-permute-done | bytes 24608 | tf_op jit(solution)/shard_map/ppermute | solution.py:546
  191.2 0.0 collective-permute-done.3.one
  191.2 2.2 %collective-permute-done.4.two = bf16[144,768]{1,0:T(8,128)(2,1)S(1)} collective-permute-done((bf16[144,768]{1,0:T(8,128)(2,1)S(1)}, bf16[144,768]{1,0:T(8,128)(2,1)S(1)}, u32[]{:S(2)}, u32[]{:S(2)}) %collective-permute-start.4) | collective-permute-done | bytes 221216 | tf_op jit(solution)/shard_map/ppermute | solution.py:546
  193.5 0.0 all-to-all-done.3.norm_two
  193.5 1.2 shard_map.91
  (12 shorter events, 0.1 us)
Async XLA Ops:
  0.6 136.8 %copy-start.3 = (bf16[128,128]{1,0:T(8,128)(2,1)S(1)}, bf16[128,128]{1,0:T(8,128)(2,1)}, u32[]{:S(2)}) copy-start(bf16[128,128]{1,0:T(8,128)(2,1)} %constant.11.clone.table.refs_6_.zi.refs_13_) | copy-start | bytes 98308
  0.6 105.9 %copy-start.2 = (bf16[384,512]{1,0:T(8,128)(2,1)S(1)}, bf16[384,512]{1,0:T(8,128)(2,1)}, u32[]{:S(2)}) copy-start(bf16[384,512]{1,0:T(8,128)(2,1)} %constant.9.clone.table.wi) | copy-start | bytes 1179652
  0.7 136.8 %copy-start.5 = (bf16[128,128]{1,0:T(8,128)(2,1)S(1)}, bf16[128,128]{1,0:T(8,128)(2,1)}, u32[]{:S(2)}) copy-start(bf16[128,128]{1,0:T(8,128)(2,1)} %constant.10.clone.refs_5_.zf.refs_12_) | copy-start | bytes 98308
  0.7 136.8 %copy-start.4 = (bf16[384,512]{1,0:T(8,128)(2,1)S(1)}, bf16[384,512]{1,0:T(8,128)(2,1)}, u32[]{:S(2)}) copy-start(bf16[384,512]{1,0:T(8,128)(2,1)} %constant.8.clone.refs_4_.refs_11_) | copy-start | bytes 1179652
  0.7 136.8 %copy-start.1 = (s32[1,2,64,192]{3,2,1,0:T(8,128)S(1)}, s32[1,2,64,192]{3,2,1,0:T(8,128)}, u32[]{:S(2)}) copy-start(s32[1,2,64,192]{3,2,1,0:T(8,128)} %param.9) | copy-start | bytes 294916
  3.6 102.8 %all-to-all-start = ((bf16[32,2,3456]{2,1,0:T(2,128)(2,1)}), bf16[32,2,3456]{2,1,0:T(2,128)(2,1)S(1)}, u32[]{:S(2)}, u32[]{:S(2)}) async-start(bf16[32,2,3456]{2,1,0:T(2,128)(2,1)} %shard_map.86), calls=%async_computation | async-start | bytes 884736 | tf_op jit(solution)/shard_map/all_to_all | solution.py:525
  107.6 29.8 %all-to-all-start.1 = ((bf16[32,2,768]{2,1,0:T(2,128)(2,1)}), bf16[32,2,768]{2,1,0:T(2,128)(2,1)S(1)}, u32[]{:S(2)}, u32[]{:S(2)}) async-start(bf16[32,2,768]{2,1,0:T(2,128)(2,1)} %get-tuple-element.16), calls=%async_computation.1 | async-start | bytes 196608 | tf_op jit(solution)/shard_map/all_to_all | solution.py:525
  124.4 13.1 %collective-permute-start = (bf16[4,64,1152]{2,1,0:T(8,128)(2,1)S(1)}, bf16[4,64,1152]{2,1,0:T(8,128)(2,1)S(1)}, u32[]{:S(2)}, u32[]{:S(2)}) collective-permute-start(bf16[4,64,1152]{2,1,0:T(8,128)(2,1)S(1)} %bitcast.15), channel_id=1, source_target_pairs={{0,1},{1,0},{2,3},{3,2},{4,5},{5,4},{6,7},{7,6},{8,9},{9,8},{10,11... | collective-permute-start | bytes 1769480 | tf_op jit(solution)/shard_map/ppermute | solution.py:534
  142.4 20.7 %all-to-all-start.2 = ((f32[32,2,128]{2,1,0:T(2,128)}), f32[32,2,128]{2,1,0:T(2,128)S(1)}, u32[]{:S(2)}, u32[]{:S(2)}) async-start(f32[32,2,128]{2,1,0:T(2,128)} %get-tuple-element.17), calls=%async_computation.2 | async-start | bytes 65536 | tf_op jit(solution)/shard_map/all_to_all | solution.py:541
  151.2 11.8 %collective-permute-start.1 = (bf16[64,768]{1,0:T(8,128)(2,1)S(1)}, bf16[64,768]{1,0:T(8,128)(2,1)S(1)}, u32[]{:S(2)}, u32[]{:S(2)}) collective-permute-start(bf16[64,768]{1,0:T(8,128)(2,1)S(1)} %reshape.19.refs_0_.refs_1_), channel_id=1, source_target_pairs={{0,2},{2,4},{4,6},{6,0},{1,3},{3,5},{5,7},{7,1},{8,10},{10,12},{12... | collective-permute-start | bytes 294920 | tf_op jit(solution)/shard_map/ppermute | solution.py:537
  154.5 8.5 %collective-permute-start.2 = (bf16[64,768]{1,0:T(8,128)(2,1)S(1)}, bf16[64,768]{1,0:T(8,128)(2,1)S(1)}, u32[]{:S(2)}, u32[]{:S(2)}) collective-permute-start(bf16[64,768]{1,0:T(8,128)(2,1)S(1)} %reshape.19.refs_0_.refs_1_), channel_id=1, source_target_pairs={{2,0},{4,2},{6,4},{0,6},{3,1},{5,3},{7,5},{1,7},{10,8},{12,10},{14... | collective-permute-start | bytes 294920 | tf_op jit(solution)/shard_map/ppermute | solution.py:538
  163.1 30.4 %copy-start = (bf16[2,1,2,3,64,192]{5,4,3,2,1,0:T(8,128)(2,1)S(1)}, bf16[2,1,2,3,64,192]{5,4,3,2,1,0:T(8,128)(2,1)}, u32[]{:S(2)}) copy-start(bf16[2,1,2,3,64,192]{5,4,3,2,1,0:T(8,128)(2,1)} %param.7) | copy-start | bytes 884740
  168.2 25.3 %all-to-all-start.3 = ((f32[32,2,128]{2,1,0:T(2,128)}), f32[32,2,128]{2,1,0:T(2,128)S(1)}, u32[]{:S(2)}, u32[]{:S(2)}) async-start(f32[32,2,128]{2,1,0:T(2,128)} %get-tuple-element.22), calls=%async_computation.3 | async-start | bytes 65536 | tf_op jit(solution)/shard_map/all_to_all | solution.py:541
  175.7 15.6 %collective-permute-start.3 = (bf16[144,768]{1,0:T(8,128)(2,1)S(1)}, bf16[144,768]{1,0:T(8,128)(2,1)S(1)}, u32[]{:S(2)}, u32[]{:S(2)}) collective-permute-start(bf16[144,768]{1,0:T(8,128)(2,1)S(1)} %get-tuple-element.25), channel_id=1, source_target_pairs={{0,8},{8,0},{16,24},{24,16},{1,9},{9,1},{17,25},{25,17},{2,10},{10... | collective-permute-start | bytes 663560 | tf_op jit(solution)/shard_map/ppermute | solution.py:546
  179.0 14.5 %collective-permute-start.4 = (bf16[144,768]{1,0:T(8,128)(2,1)S(1)}, bf16[144,768]{1,0:T(8,128)(2,1)S(1)}, u32[]{:S(2)}, u32[]{:S(2)}) collective-permute-start(bf16[144,768]{1,0:T(8,128)(2,1)S(1)} %get-tuple-element.26), channel_id=1, source_target_pairs={{0,16},{8,24},{16,0},{24,8},{1,17},{9,25},{17,1},{25,9},{2,18},{10... | collective-permute-start | bytes 663560 | tf_op jit(solution)/shard_map/ppermute | solution.py:546
  183.1 8.1 %collective-permute-start.5 = (bf16[16,768]{1,0:T(8,128)(2,1)S(1)}, bf16[16,768]{1,0:T(8,128)(2,1)S(1)}, u32[]{:S(2)}, u32[]{:S(2)}) collective-permute-start(bf16[16,768]{1,0:T(8,128)(2,1)S(1)} %get-tuple-element.27), channel_id=1, source_target_pairs={{0,24},{8,16},{16,8},{24,0},{1,25},{9,17},{17,9},{25,1},{2,26},{10... | collective-permute-start | bytes 73736 | tf_op jit(solution)/shard_map/ppermute | solution.py:546
